TPU v7x, 32 devices: a whole 2x2x4 slice. The times are simulated.
32 devices in a mesh: grp: 4 (over y, core), dom: 8 (over z, x).
Axes of the slice: x: 2, y: 2, z: 4, core: 2. Of those that a mesh axis runs over, the one named last changes fastest.
Arguments:
- fine_nodes: bfloat16 [4, 6144, 128], P('grp', 'dom'), may hold values from -6 to 6
- fine_edges: bfloat16 [4, 73728, 128], P('grp', 'dom'), may hold values from -6 to 6
- fine_senders: int32 [4, 73728], P('grp', 'dom'), may hold values from 0 to 959
- fine_receivers: int32 [4, 73728], P('grp', 'dom'), may hold values from 0 to 767, as said below
- edge_count: int32 [4, 8], P('grp', 'dom'), may hold values from 4608 to 9216, as said below
- ghost_send: int32 [4, 64, 24], P('grp', 'dom'), may hold values from 0 to 767
- fine_parent: int32 [4, 6144], P('grp', 'dom'), may hold values from 0 to 4095, as said below
- coarse_nodes: bfloat16 [4096, 128], P('dom'), may hold values from -6 to 6
- coarse_edges: bfloat16 [32768, 128], P('dom'), may hold values from -6 to 6
- coarse_senders: int32 [32768], P('dom'), may hold values from 0 to 4095
- coarse_receivers: int32 [32768], P('dom'), may hold values from 0 to 511, as said below
- edge_in: bfloat16 [2, 384, 128], replicated, may hold values from -0.3125 to 0.3125
- node_in: bfloat16 [3, 256, 128], replicated, may hold values from -0.375 to 0.375
- mlp_out: bfloat16 [5, 128, 128], replicated, may hold values from -0.5 to 0.5
Outputs:
- fine_out: bfloat16 [4, 6144, 128], P('grp', 'dom')
- coarse_out: bfloat16 [4096, 128], P('dom')
Inputs may be any that keep to these rules, and one draw needn't show every extreme that they name: `edge_count`: each device's live edge slot count; slots from that count on are padding; 9216 on at least one device. `fine_receivers`: nondecreasing along each device's 9216 slots; padding slots hold 767. `fine_senders`: below 768: a local node; 768 + s * 24 + k: ghost slot k received from dom index s of the same slab. `ghost_send`: local node indices; row p of a device's block lists the nodes sent to dom index p. `fine_parent`: global coarse index; owner o holds coarse nodes o * 512 to (o + 1) * 512 - 1. Most parents of a fine node of dom index d are owned by d itself; the others may be owned by any owner. `coarse_senders`: global coarse index of the sender. `coarse_receivers`: nondecreasing within each owner's 4096 edges.
All inputs are finite; a program needn't handle non-finite values.
Results may differ from a plain program's by a relative error of at most 0.015.
Values may be sent and summed in bfloat16 or wider, within the bound.
No kernel may reach another device: no remote copies, remote signals or barrier semaphores. Data moves between devices by JAX's collectives and lax.ppermute only.
A program may use at most 64 MiB of HBM per device.

v0:
```python
import jax
import jax.numpy as jnp
from jax import lax
from jax.sharding import PartitionSpec as P


def layer_norm(values):
    centre = values - jnp.mean(values, -1, keepdims=True)
    spread = jnp.mean(centre * centre, -1, keepdims=True)
    return centre * lax.rsqrt(spread + 1e-05)


def perceptron(inputs, w_first, w_second):
    hidden = jax.nn.silu(jnp.dot(inputs, w_first, preferred_element_type=jnp.float32)).astype(
        jnp.bfloat16
    )
    return layer_norm(jnp.dot(hidden, w_second, preferred_element_type=jnp.float32))


def per_device(
    fine_nodes,
    fine_edges,
    fine_senders,
    fine_receivers,
    edge_count,
    ghost_send,
    fine_parent,
    coarse_nodes,
    coarse_edges,
    coarse_senders,
    coarse_receivers,
    edge_in,
    node_in,
    mlp_out,
):
    domains = lax.axis_size("dom")
    groups = lax.axis_size("grp")
    local = fine_nodes[0]
    node_rows, width = local.shape
    owner_rows = coarse_nodes.shape[0]
    coarse_total = owner_rows * domains
    outgoing = local[ghost_send[0]]
    incoming = lax.all_to_all(outgoing, "dom", split_axis=0, concat_axis=0, tiled=True)
    table = jnp.concatenate([local, incoming.reshape(-1, width)], 0)
    edges = fine_edges[0]
    receivers = fine_receivers[0]
    inputs = jnp.concatenate([edges, local[receivers], table[fine_senders[0]]], -1)
    edge_new = edges.astype(jnp.float32) + perceptron(inputs, edge_in[0], mlp_out[0])
    live = (jnp.arange(edges.shape[0]) < edge_count[0, 0]).astype(jnp.float32)
    summed = jax.ops.segment_sum(
        edge_new * live[:, None], receivers, num_segments=node_rows
    ).astype(jnp.bfloat16)
    fine_mid = (
        local.astype(jnp.float32)
        + perceptron(jnp.concatenate([local, summed], -1), node_in[0], mlp_out[1])
    ).astype(jnp.bfloat16)
    parents = fine_parent[0]
    ones_rows = jnp.ones(parents.shape, jnp.float32)
    mid_wide = fine_mid.astype(jnp.float32)
    piece = owner_rows // groups
    owner = parents // owner_rows
    within = parents % owner_rows
    mapped = within // piece * (domains * piece) + owner * piece + within % piece
    pooled = jax.ops.segment_sum(mid_wide, mapped, num_segments=coarse_total).reshape(
        groups, domains, piece, width
    )
    children = jax.ops.segment_sum(ones_rows, mapped, num_segments=coarse_total).reshape(
        groups, domains, piece
    )
    pooled, children = (
        lax.psum_scatter(
            pooled.astype(jnp.bfloat16), "grp", scatter_dimension=0, tiled=True
        ).astype(jnp.float32),
        lax.psum_scatter(
            children.astype(jnp.bfloat16), "grp", scatter_dimension=0, tiled=True
        ).astype(jnp.float32),
    )
    pooled, children = (
        lax.psum_scatter(
            pooled.astype(jnp.bfloat16), "dom", scatter_dimension=1, tiled=True
        ).astype(jnp.float32),
        lax.psum_scatter(
            children.astype(jnp.bfloat16), "dom", scatter_dimension=1, tiled=True
        ).astype(jnp.float32),
    )
    pooled, children = (
        lax.all_gather(pooled, "grp", axis=0, tiled=True),
        lax.all_gather(children, "grp", axis=0, tiled=True),
    )
    pooled = pooled.reshape(owner_rows, width)
    children = children.reshape(owner_rows)
    coarse_mid = ((coarse_nodes.astype(jnp.float32) + pooled) / (1.0 + children)[:, None]).astype(
        jnp.bfloat16
    )
    coarse_table = lax.all_gather(coarse_mid, "dom", axis=0, tiled=True)
    cinputs = jnp.concatenate(
        [coarse_edges, coarse_mid[coarse_receivers], coarse_table[coarse_senders]], -1
    )
    cedge_new = coarse_edges.astype(jnp.float32) + perceptron(cinputs, edge_in[1], mlp_out[2])
    csummed = jax.ops.segment_sum(cedge_new, coarse_receivers, num_segments=owner_rows).astype(
        jnp.bfloat16
    )
    coarse_out = (
        coarse_mid.astype(jnp.float32)
        + perceptron(jnp.concatenate([coarse_mid, csummed], -1), node_in[1], mlp_out[3])
    ).astype(jnp.bfloat16)
    updated_table = lax.all_gather(coarse_out, "dom", axis=0, tiled=True)
    above = updated_table[parents]
    fine_out = (
        mid_wide + perceptron(jnp.concatenate([fine_mid, above], -1), node_in[2], mlp_out[4])
    ).astype(jnp.bfloat16)
    return (fine_out[None], coarse_out)


def solution(mesh):
    placed = (
        P("grp", "dom", None),
        P("grp", "dom", None),
        P("grp", "dom"),
        P("grp", "dom"),
        P("grp", "dom"),
        P("grp", "dom", None),
        P("grp", "dom"),
        P("dom", None),
        P("dom", None),
        P("dom"),
        P("dom"),
        P(),
        P(),
        P(),
    )
    return jax.shard_map(
        per_device,
        mesh=mesh,
        in_specs=placed,
        out_specs=(P("grp", "dom", None), P("dom", None)),
        check_vma=False,
    )
```

profile of v0, /device:TPU:0, one launch (start us, length us, event | category | flops | bytes accessed | tf_op | source)
XLA Modules:
  0.0 416.5 jit_solution(2890163426016908127)
XLA Ops:
  7.2 0.7 compare_select_fusion.4
  8.0 2.3 gather_fusion.1
  10.3 7.3 %all-to-all-start = ((bf16[8,24,128]{2,1,0:T(8,128)(2,1)}), bf16[8,24,128]{2,1,0:T(8,128)(2,1)S(1)}, u32[]{:S(2)}, u32[]{:S(2)}) async-start(bf16[8,24,128]{2,1,0:T(8,128)(2,1)} %bitcast.8), calls=%async_computation | async-start | bytes 98304 | tf_op jit(solution)/shard_map/all_to_all | solution.py:43
  17.6 1.1 copy.54
  18.6 0.8 compare_select_fusion
  19.5 0.8 compare_select_fusion.1
  20.3 27.0 %gather_fusion = bf16[9216,128]{1,0:T(8,128)(2,1)S(1)} fusion(bf16[768,128]{1,0:T(8,128)(2,1)S(1)} %bitcast.104, s32[9216]{0:T(1024)S(1)} %broadcast_clamp_fusion.1), kind=kCustom, calls=%fused_computation | custom fusion | bytes 4755456 | tf_op jit(solution)/shard_map/gather | solution.py:47
  47.3 2.5 copy.60
  49.9 4.3 %copy.55 = bf16[1,9216,128]{1,2,0:T(8,128)(2,1)} copy(bf16[1,9216,128]{2,1,0:T(8,128)(2,1)} %param.15) | data formatting | bytes 4718592 | tf_op args[1]
  55.2 27.0 %gather_fusion.2 = bf16[9216,128]{1,0:T(8,128)(2,1)S(1)} fusion(bf16[960,128]{1,0:T(8,128)(2,1)S(1)} %copy.59, s32[9216]{0:T(1024)S(1)} %broadcast_clamp_fusion), kind=kCustom, calls=%fused_computation.2 | custom fusion | bytes 4755456 | tf_op jit(solution)/shard_map/gather | solution.py:47
  82.3 2.5 copy.61
  84.8 6.8 %fusion.114 = (f32[9216]{0:T(1024)S(1)}, f32[9216,128]{0,1:T(8,128)}) fusion(bf16[5,128,128]{2,1,0:T(8,128)(2,1)} %param.27, bf16[9216,128]{0,1:T(8,128)(2,1)} %copy.61, bf16[9216,128]{0,1:T(8,128)(2,1)} %copy.60, bf16[9216,128]{0,1:T(8,128)(2,1)} %bitcast.105, bf16[2,384,128]{2,1,0:T(8,128)(2,1)S(1)} %copy-done.9), kind=kOutput, calls=%fused_computation.142 | convolution fusion | flops 1236261888 | bytes 11964416 | tf_op jit(solution)/shard_map/dot_general | solution.py:17
  91.6 3.0 multiply_reduce_fusion
  94.6 0.7 copy-done.1
  95.3 3.0 add_multiply_fusion
  98.3 6.1 %copy.62 = f32[9216,128]{1,0:T(8,128)} copy(f32[9216,128]{0,1:T(8,128)} %add_multiply_fusion) | data formatting | bytes 9437184 | tf_op jit(solution)/shard_map/mul | solution.py:51
  104.4 60.8 %scatter_custom_fusion = f32[768,128]{1,0:T(8,128)S(1)} fusion(s32[9216]{0:T(1024)} %bitcast.113, f32[9216,128]{1,0:T(8,128)} %copy.62, f32[]{:T(128)} %constant.85.clone.1), kind=kCustom, calls=%fused_computation.64 | custom fusion | flops 1179648 | bytes 393728 | tf_op jit(solution)/shard_map/scatter-add | solution.py:50
  165.4 1.4 fusion.119
  167.0 6.5 %scatter_custom_fusion.1 = f32[4096,128]{1,0:T(8,128)S(1)} fusion(s32[768]{0:T(1024)S(1)} %get-tuple-element.9, f32[768,128]{1,0:T(8,128)S(1)} %copy.65, f32[]{:T(128)} %constant.85.clone.1), kind=kCustom, calls=%fused_computation.31 | custom fusion | flops 98304 | bytes 2097156 | tf_op jit(solution)/shard_map/scatter-add | solution.py:64
  173.6 1.1 convert_element_type.89
  175.0 4.6 %scatter_custom_fusion.2 = f32[4096]{0:T(1024)S(1)} fusion(s32[768]{0:T(1024)S(1)} %get-tuple-element.9, f32[768]{0:T(1024)S(1)} %broadcast.349, f32[]{:T(128)} %constant.85.clone.1), kind=kCustom, calls=%fused_computation.107 | custom fusion | flops 768 | bytes 16388 | tf_op jit(solution)/shard_map/scatter-add | solution.py:67
  179.6 21.5 %reduce-scatter.4.cloned.1.call-done = bf16[1,8,128,128]{3,2,1,0:T(8,128)(2,1)} async-done(((bf16[4,8,128,128]{3,2,1,0:T(8,128)(2,1)}), bf16[1,8,128,128]{3,2,1,0:T(8,128)(2,1)}) %reduce-scatter.4.cloned.1.call-update) | async-done | bytes 262160 | tf_op jit(solution)/shard_map/reduce_scatter | solution.py:71
  201.2 0.6 dynamic-slice
  202.5 5.9 %all-reduce = bf16[4,8,128]{2,1,0:T(8,128)(2,1)S(1)} all-reduce(bf16[4,8,128]{2,1,0:T(8,128)(2,1)S(1)} %convert_bitcast_fusion), channel_id=4, replica_groups=mesh['grp'=4,'dom'=8] {'grp'}, use_global_device_ids=true, to_apply=%region_9.10.clone | all-reduce | flops 4096 | bytes 16384
  208.3 0.7 constant_dynamic-slice_fusion.1
  209.0 21.6 %all-reduce.1 = bf16[1,8,128]{2,1,0:T(8,128)(2,1)S(1)} all-reduce(bf16[1,8,128]{2,1,0:T(8,128)(2,1)S(1)} %constant_dynamic-slice_fusion.1), channel_id=5, replica_groups=mesh['grp'=4,'dom'=8] {'dom'}, use_global_device_ids=true, to_apply=%region_10.11.clone | all-reduce | flops 1024 | bytes 4096
  230.6 0.7 fusion.98
  231.3 5.1 %all_gather.13 = f32[4,1,128]{2,1,0:T(1,128)S(1)} all-gather(f32[1,1,128]{2,1,0:T(1,128)S(1)} %fusion.98), channel_id=1, replica_groups=mesh['grp'=4,'dom'=8] {'grp'}, dimensions={0}, use_global_device_ids=true | all-gather | bytes 2560 | tf_op jit(solution)/shard_map/all_gather | solution.py:88
  236.3 30.8 %reduce-scatter.6.cloned.1.call-done = bf16[1,1,128,128]{3,2,1,0:T(8,128)(2,1)} async-done(((bf16[1,8,128,128]{3,2,1,0:T(8,128)(2,1)}), bf16[1,1,128,128]{3,2,1,0:T(8,128)(2,1)}) %reduce-scatter.6.cloned.1.call-update) | async-done | bytes 32784 | tf_op jit(solution)/shard_map/reduce_scatter | solution.py:79
  267.1 0.8 convert_element_type.91
  267.9 5.8 %all_gather.12 = f32[4,1,128,128]{3,2,1,0:T(8,128)S(1)} all-gather(f32[1,1,128,128]{3,2,1,0:T(8,128)S(1)} %convert_element_type.91), channel_id=1, replica_groups=mesh['grp'=4,'dom'=8] {'grp'}, dimensions={0}, use_global_device_ids=true | all-gather | bytes 327680 | tf_op jit(solution)/shard_map/all_gather | solution.py:87
  273.8 0.7 divide_convert_fusion
  275.5 14.9 %gather_fusion.3 = bf16[4096,128]{1,0:T(8,128)(2,1)} fusion(bf16[512,128]{1,0:T(8,128)(2,1)S(1)} %copy.68, s32[4096]{0:T(1024)S(1)} %fusion.91), kind=kCustom, calls=%fused_computation.3 | custom fusion | bytes 2113536 | tf_op jit(solution)/shard_map/gather | solution.py:97
  290.4 22.7 %all-gather.3.cloned.1.call-done = bf16[4096,128]{0,1:T(8,128)(2,1)} async-done(((bf16[512,128]{0,1:T(8,128)(2,1)}), bf16[4096,128]{0,1:T(8,128)(2,1)}) %all-gather.3.cloned.1.call-update) | async-done | bytes 1048592 | tf_op jit(solution)/shard_map/all_gather | solution.py:95
  313.1 1.6 copy.69
  314.7 14.9 %gather_fusion.4 = bf16[4096,128]{1,0:T(8,128)(2,1)} fusion(bf16[4096,128]{1,0:T(8,128)(2,1)S(1)} %copy.69, s32[4096]{0:T(1024)S(1)} %fusion.92), kind=kCustom, calls=%fused_computation.4 | custom fusion | bytes 2113536 | tf_op jit(solution)/shard_map/gather | solution.py:97
  329.6 3.3 fusion.124
  333.2 1.7 multiply_add_fusion
  334.9 1.9 copy.70
  336.9 26.5 %scatter_custom_fusion.3 = f32[512,128]{1,0:T(8,128)S(1)} fusion(s32[4096]{0:T(1024)S(1)} %copy-done.7, f32[4096,128]{1,0:T(8,128)S(1)} %copy.70, f32[]{:T(128)} %constant.85.clone.1), kind=kCustom, calls=%fused_computation.67 | custom fusion | flops 524288 | bytes 262148 | tf_op jit(solution)/shard_map/scatter-add | solution.py:100
  363.5 1.2 fusion.129
  364.8 0.7 add_convert_fusion.2
  365.5 1.7 copy.75
  367.2 36.9 %all-gather.5.cloned.1.call-done = bf16[4096,128]{0,1:T(8,128)(2,1)} async-done(((bf16[512,128]{0,1:T(8,128)(2,1)}), bf16[4096,128]{0,1:T(8,128)(2,1)}) %all-gather.5.cloned.1.call-update) | async-done | bytes 1048592 | tf_op jit(solution)/shard_map/all_gather | solution.py:107
  404.0 1.6 copy.72
  405.7 1.9 gather_fusion.5
  407.7 1.3 fusion.134
  409.1 0.8 copy.74
  (74 shorter events, 3.8 us)
Async XLA Ops:
  7.2 13.1 %copy-start = (bf16[1,768,128]{2,1,0:T(8,128)(2,1)S(1)}, bf16[1,768,128]{2,1,0:T(8,128)(2,1)}, u32[]{:S(2)}) copy-start(bf16[1,768,128]{2,1,0:T(8,128)(2,1)} %param.14) | copy-start | bytes 589828
  10.3 44.6 %all-to-all-start = ((bf16[8,24,128]{2,1,0:T(8,128)(2,1)}), bf16[8,24,128]{2,1,0:T(8,128)(2,1)S(1)}, u32[]{:S(2)}, u32[]{:S(2)}) async-start(bf16[8,24,128]{2,1,0:T(8,128)(2,1)} %bitcast.8), calls=%async_computation | async-start | bytes 98304 | tf_op jit(solution)/shard_map/all_to_all | solution.py:43
  17.5 183.5 %reduce-scatter.4.cloned.1.call-start = ((), (), s32[]{:S(2)}) async-start(), calls=%async_computation.3 | async-start | bytes 1310720 | tf_op jit(solution)/shard_map/reduce_scatter | solution.py:71
  49.9 5.0 %copy-start.8 = (s32[1,768]{1,0:T(1,128)S(1)}, s32[1,768]{1,0:T(1,128)}, u32[]{:S(2)}) copy-start(s32[1,768]{1,0:T(1,128)} %param.20) | copy-start | bytes 9220
  82.3 2.5 copy-start.9
  84.8 9.9 %copy-start.2 = (bf16[1,9216,128]{1,2,0:T(8,128)(2,1)S(1)}, bf16[1,9216,128]{1,2,0:T(8,128)(2,1)}, u32[]{:S(2)}) copy-start(bf16[1,9216,128]{1,2,0:T(8,128)(2,1)} %copy.55) | copy-start | bytes 7077892
  91.6 3.8 copy-start.1
  173.6 27.6 %copy-start.12 = (u32[32]{0:T(128)S(1)}, u32[32]{0:T(128)}, u32[]{:S(2)}) copy-start(u32[32]{0:T(128)} %constant.111) | copy-start | bytes 388
  173.6 28.2 %copy-start.11 = (u32[32]{0:T(128)S(1)}, u32[32]{0:T(128)}, u32[]{:S(2)}) copy-start(u32[32]{0:T(128)} %constant.115) | copy-start | bytes 388
  173.6 28.8 %copy-start.5 = (bf16[512,128]{1,0:T(8,128)(2,1)S(1)}, bf16[512,128]{1,0:T(8,128)(2,1)}, u32[]{:S(2)}) copy-start(bf16[512,128]{1,0:T(8,128)(2,1)} %param.21) | copy-start | bytes 393220
  174.7 99.9 %copy-start.4 = (bf16[4096,128]{1,0:T(8,128)(2,1)S(1)}, bf16[4096,128]{1,0:T(8,128)(2,1)}, u32[]{:S(2)}) copy-start(bf16[4096,128]{1,0:T(8,128)(2,1)} %param.22) | copy-start | bytes 3145732
  174.7 100.4 %copy-start.6 = (s32[4096]{0:T(1024)S(1)}, s32[4096]{0:T(1024)}, u32[]{:S(2)}) copy-start(s32[4096]{0:T(1024)} %param.23) | copy-start | bytes 49156
  174.7 100.4 %copy-start.7 = (s32[4096]{0:T(1024)S(1)}, s32[4096]{0:T(1024)}, u32[]{:S(2)}) copy-start(s32[4096]{0:T(1024)} %param.24) | copy-start | bytes 49156
  174.7 92.4 %reduce-scatter.6.cloned.1.call-start = ((), (), s32[]{:S(2)}) async-start(), calls=%async_computation.4 | async-start | bytes 294912 | tf_op jit(solution)/shard_map/reduce_scatter | solution.py:79
  201.1 112.0 %all-gather.3.cloned.1.call-start = ((), (), s32[]{:S(2)}) async-start(), calls=%async_computation.5 | async-start | bytes 1179648 | tf_op jit(solution)/shard_map/all_gather | solution.py:95
  274.5 0.9 copy-start.3
  274.5 129.5 %all-gather.5.cloned.1.call-start = ((), (), s32[]{:S(2)}) async-start(), calls=%async_computation.6 | async-start | bytes 1179648 | tf_op jit(solution)/shard_map/all_gather | solution.py:107
  334.9 28.6 %copy-start.10 = (bf16[3,256,128]{2,1,0:T(8,128)(2,1)S(1)}, bf16[3,256,128]{2,1,0:T(8,128)(2,1)}, u32[]{:S(2)}) copy-start(bf16[3,256,128]{2,1,0:T(8,128)(2,1)} %param.26) | copy-start | bytes 589828
Sparse Core Ops, SparseCore 0:
  174.8 26.1 reduce-scatter.3
  204.4 62.6 reduce-scatter.5
  274.6 38.4 all-gather.2
  365.6 38.3 all-gather.4
where the time goes:
time: 417 us; the launch traced here: 416 us
  local copies, waits for them, and re-layouts  117 us (28%)
  other arithmetic  113 us (27%)
  waiting for transfers between devices  112 us (27%)
  blocking collectives  38.3 us (9%)
  between operations  14.9 us (4%)
  matrix products  14 us (3%)
  starting transfers between devices  7.62 us (2%)
    scatter-add x1, other arithmetic, per_device(): jax.ops.segment_sum(edge_new * live[:, None], receivers, num_segments=nod...  60.8 us
    all_gather x1, waiting for transfers between devices, per_device(): updated_table = lax.all_gather(coarse_out, 'dom', axis=0, tiled=True)  36.9 us
    reduce_scatter x1, waiting for transfers between devices, per_device(): lax.psum_scatter(pooled.astype(jnp.bfloat16), 'dom', scatter_dimension=1,...  30.8 us
    gather x2, local copies, waits for them, and re-layouts, per_device(): local[receivers]  29.5 us
    gather x2, local copies, waits for them, and re-layouts, per_device(): table[fine_senders[0]]  29.5 us
    unnamed x2, blocking collectives  27.5 us
    scatter-add x1, other arithmetic, per_device(): jax.ops.segment_sum(cedge_new, coarse_receivers, num_segments=owner_rows)  26.5 us
    all_gather x1, waiting for transfers between devices, per_device(): coarse_table = lax.all_gather(coarse_mid, 'dom', axis=0, tiled=True)  22.7 us
  transfers between devices with their start and end apart: 5, of which 4 were waited for; matrix products, arithmetic and copies ran while one was open for 15% of the time, Pallas kernels for 0%

commit v1 on v0

v1 whole, which is shorter than its diff:
```python
import functools

import jax
import jax.numpy as jnp
from jax import lax
from jax.experimental import pallas as pl
from jax.experimental.pallas import tpu as pltpu
from jax.sharding import PartitionSpec as P

F32 = jnp.float32
BF16 = jnp.bfloat16
NT = (((1,), (1,)), ((), ()))
CHUNK = 256
LANES = 128
VMEM = pl.BlockSpec(memory_space=pltpu.VMEM)
SMEM = pl.BlockSpec(memory_space=pltpu.SMEM)


def log2(n):
    bits = n.bit_length() - 1
    assert 1 << bits == n
    return bits


def mm(a, b):
    return jnp.dot(a, b, preferred_element_type=F32)


def mm_nt(a, b):
    return lax.dot_general(a, b, NT, preferred_element_type=F32)


def turn(w):
    return w.astype(F32).T.astype(BF16)


def silu(v):
    u = 0.5 * v
    return (u + u * jnp.tanh(u)).astype(BF16)


def norm(y, axis):
    centre = y - jnp.mean(y, axis, keepdims=True)
    spread = jnp.mean(centre * centre, axis, keepdims=True)
    return centre * lax.rsqrt(spread + 1e-05)


def mlp_rows(first, w_second):
    return norm(mm(silu(first), w_second), 1)


def steps(rows):
    base = lax.broadcasted_iota(jnp.int32, (16, LANES), 0)
    return [(base + 16 * j).astype(F32).astype(BF16) for j in range(rows // 16)]


def hot(row, base, blocks):
    rows = 16 * len(blocks)
    n = row.shape[1]
    near = jnp.clip(jnp.broadcast_to(row, (16, n)) - base, -1, rows).astype(F32).astype(BF16)
    one = jnp.ones((16, n), BF16)
    zero = jnp.zeros((16, n), BF16)
    return jnp.concatenate(
        [jnp.where(jnp.concatenate([b] * (n // LANES), 1) == near, one, zero) for b in blocks], 0
    )


def ghosts_kernel(send, local, out, wide, picked):
    wide[...] = local[...].astype(F32)
    peers, slots = send.shape

    def one(p, _):
        for k in range(slots):
            picked[pl.ds(p * slots + k, 1), :] = wide[pl.ds(send[p, k], 1), :]
        return 0

    lax.fori_loop(0, peers, one, 0)
    out[...] = picked[...].astype(BF16)


def fine_kernel(
    count, bounds, edges, senders, receivers, local, ghosts, parents, w_edge, w_node, w_out,
    out, tab, rec, pre, agg, mix, second,
):
    step = pl.program_id(0)
    tile, width = edges.shape
    nodes = local.shape[0]
    table_rows = nodes + ghosts.shape[0]
    chunks = tab.shape[0]
    windows = rec.shape[0]
    blocks = steps(CHUNK)

    @pl.when(step == 0)
    def _():
        w = w_edge[...]
        w_self = turn(w[:width])
        w_recv = turn(w[width : 2 * width])
        w_send = turn(w[2 * width :])
        eye = (
            lax.broadcasted_iota(jnp.int32, (width, width), 0)
            == lax.broadcasted_iota(jnp.int32, (width, width), 1)
        ).astype(F32).astype(BF16)
        mix[...] = jnp.concatenate([w_self, eye], 0)
        second[...] = turn(w_out[0])
        mine = local[...]
        for c in range(windows):
            rec[c] = mm_nt(w_recv, mine[c * CHUNK : (c + 1) * CHUNK]).astype(BF16)
        whole = jnp.concatenate([mine, ghosts[...]], 0)
        extra = chunks * CHUNK - table_rows
        if extra:
            whole = jnp.concatenate([whole, jnp.zeros((extra, width), BF16)], 0)
        for c in range(chunks):
            tab[c] = mm_nt(w_send, whole[c * CHUNK : (c + 1) * CHUNK]).astype(BF16)
        agg[...] = jnp.zeros_like(agg)

    live = count[0, 0]

    @pl.when(step * tile < live)
    def _():
        row = senders[...]
        both = mm_nt(mix[...], edges[...])
        first = both[:width]
        for c in range(chunks):
            first += mm(tab[c], hot(row, c * CHUNK, blocks))
        pre[...] = first
        slots = step * tile + lax.broadcasted_iota(jnp.int32, (1, tile), 1)
        to = jnp.where(slots < live, receivers[...], -1)
        low = bounds[0, 0]
        high = bounds[0, tile - 1]

        def inside(c):
            return (low < (c + 1) * CHUNK) & (high >= c * CHUNK)

        for c in range(windows):

            @pl.when(inside(c))
            def _():
                pre[...] += mm(rec[c], hot(to, c * CHUNK, blocks))

        y = mm(second[...], silu(pre[...]))
        new = (both[width:] + norm(y, 0)).astype(BF16)
        for c in range(windows):

            @pl.when(inside(c))
            def _():
                agg[pl.ds(c * CHUNK, CHUNK), :] += mm_nt(hot(to, c * CHUNK, blocks), new)

    @pl.when(step == pl.num_programs(0) - 1)
    def _():
        mine = local[...]
        w = w_node[0]
        first = mm(mine, w[:width]) + mm(agg[...].astype(BF16), w[width:])
        out[pl.ds(0, nodes), :] = (mine.astype(F32) + mlp_rows(first, w_out[1])).astype(BF16)
        ids = parents[...]
        lines = nodes // LANES
        pads = out.shape[0] - nodes - 2 * lines
        parts = [ids[:, j * LANES : (j + 1) * LANES] for j in range(lines)]
        digits = [p >> 6 for p in parts] + [p & 63 for p in parts]
        digits = digits + [jnp.zeros((1, LANES), jnp.int32)] * pads
        out[pl.ds(nodes, 2 * lines + pads), :] = jnp.concatenate(digits, 0).astype(F32).astype(BF16)


def place(ids, owner_rows, piece, domains, group):
    owner = ids >> log2(owner_rows)
    within = ids & (owner_rows - 1)
    return (within >> log2(piece)) ^ group, owner * piece + (within & (piece - 1))


def pool_kernel(*refs, owner_rows, piece, domains, nodes):
    packs, out = refs[:-1], refs[-1]
    group = lax.axis_index("grp")
    lines = nodes // LANES
    blocks = steps(CHUNK)
    width = out.shape[1]
    chunk_rows = piece + 16
    spots = []
    fulls = []
    for pack in packs:
        tail = pack[pl.ds(nodes, pack.shape[0] - nodes), :].astype(F32).astype(jnp.int32)
        ids = jnp.concatenate(
            [(tail[j : j + 1] << 6) + tail[lines + j : lines + j + 1] for j in range(lines)], 1
        )
        side, spot = place(ids, owner_rows, piece, domains, group)
        spots.append(jnp.where(side == 0, spot, -1))
        fulls.append(
            jnp.concatenate([pack[pl.ds(0, nodes), :], jnp.ones((nodes, LANES), BF16)], 1)
        )
    eye = lax.broadcasted_iota(jnp.int32, (piece, LANES), 0) == lax.broadcasted_iota(
        jnp.int32, (piece, LANES), 1
    )
    lane_row = lax.broadcasted_iota(jnp.int32, (16, LANES), 0)
    for c in range(domains * piece // CHUNK):
        total = mm(hot(spots[0], c * CHUNK, blocks), fulls[0])
        for spot, full in zip(spots[1:], fulls[1:]):
            total += mm(hot(spot, c * CHUNK, blocks), full)
        for q in range(CHUNK // piece):
            base = (c * CHUNK // piece + q) * chunk_rows
            part = total[q * piece : (q + 1) * piece]
            out[pl.ds(base, piece), :] = part[:, :width].astype(BF16)
            many = jnp.sum(jnp.where(eye, part[:, width:], 0.0), 0, keepdims=True)
            high = jnp.floor(many * (1.0 / 256.0))
            low = many - 256.0 * high
            both = jnp.where(lane_row == 0, high, jnp.where(lane_row == 1, low, 0.0))
            out[pl.ds(base + piece, 16), :] = both.astype(BF16)


def coarse_mid_kernel(got, nodes, out, *, piece, domains):
    group = lax.axis_index("grp")
    chunk_rows = piece + 16
    parts = [got[pl.ds(s * chunk_rows, chunk_rows), :].astype(F32) for s in range(domains)]
    total = functools.reduce(jnp.add, parts)
    row = 256.0 * total[piece : piece + 1] + total[piece + 1 : piece + 2]
    eye = lax.broadcasted_iota(jnp.int32, (piece, LANES), 0) == lax.broadcasted_iota(
        jnp.int32, (piece, LANES), 1
    )
    many = jnp.sum(jnp.where(eye, jnp.broadcast_to(row, (piece, LANES)), 0.0), 1, keepdims=True)
    start = pl.multiple_of(group * piece, piece)
    mine = nodes[pl.ds(start, piece), :].astype(F32)
    mid = ((mine + total[:piece]) / (1.0 + many)).astype(BF16)
    for s in range(domains):
        out[pl.ds(s * piece, piece), :] = mid


def fill_table(parts, w, tab):
    per = parts[0].shape[0] // CHUNK
    for k, part in enumerate(parts):
        for c in range(per):
            tab[k * per + c] = mm_nt(w, part[pl.ds(c * CHUNK, CHUNK), :]).astype(BF16)


def coarse_kernel(
    *refs, groups, owner_rows, piece, domains, tile
):
    parts = refs[:groups]
    edges, senders, receivers, w_edge, w_node, w_out = refs[groups : groups + 6]
    out, tab, agg = refs[groups + 6 :]
    group = lax.axis_index("grp")
    domain = lax.axis_index("dom")
    width = edges.shape[1]
    blocks = steps(CHUNK)
    small = steps(piece)
    w = w_edge[1]
    eye = (
        lax.broadcasted_iota(jnp.int32, (width, width), 0)
        == lax.broadcasted_iota(jnp.int32, (width, width), 1)
    ).astype(F32).astype(BF16)
    mix = jnp.concatenate([turn(w[:width]), eye], 0)
    fill_table(parts, turn(w[2 * width :]), tab)
    start = pl.multiple_of(domain * piece, piece)
    mine = parts[0][pl.ds(start, piece), :]
    rec = mm_nt(turn(w[width : 2 * width]), mine).astype(BF16)
    second = turn(w_out[2])
    agg[...] = jnp.zeros_like(agg)
    every = receivers[...]
    low = group * piece
    first_edge = jnp.sum((every < low).astype(jnp.int32))
    last_edge = jnp.sum((every < low + piece).astype(jnp.int32))

    def one(t, _):
        at = pl.multiple_of(t * tile, tile)
        block = edges[pl.ds(at, tile), :]
        side, spot = place(senders[:, pl.ds(at, tile)], owner_rows, piece, domains, group)
        row = side * (domains * piece) + spot
        both = mm_nt(mix, block)
        to = receivers[:, pl.ds(at, tile)] - low
        hot_to = hot(to, 0, small)
        first = both[:width] + mm(rec, hot_to)
        for c in range(tab.shape[0]):
            first += mm(tab[c], hot(row, c * CHUNK, blocks))
        y = mm(second, silu(first))
        new = (both[width:] + norm(y, 0)).astype(BF16)
        agg[...] += mm_nt(hot_to, new)
        return 0

    lax.fori_loop(first_edge // tile, (last_edge + tile - 1) // tile, one, 0)
    wn = w_node[1]
    first = mm(mine, wn[:width]) + mm(agg[...].astype(BF16), wn[width:])
    new = (mine.astype(F32) + mlp_rows(first, w_out[3])).astype(BF16)
    for s in range(domains):
        out[pl.ds(s * piece, piece), :] = new


def return_kernel(*refs, groups, owner_rows, piece, domains, nodes):
    parts = refs[:groups]
    packed, parents, w_node, w_out = refs[groups : groups + 4]
    out, coarse, tab = refs[groups + 4 :]
    group = lax.axis_index("grp")
    domain = lax.axis_index("dom")
    width = out.shape[1]
    blocks = steps(CHUNK)
    w = w_node[2]
    start = pl.multiple_of(domain * piece, piece)
    for side in range(groups):
        to = pl.multiple_of((group ^ side) * piece, piece)
        coarse[pl.ds(to, piece), :] = parts[side][pl.ds(start, piece), :]
    fill_table(parts, turn(w[width:]), tab)
    mine = packed[pl.ds(0, nodes), :]
    side, spot = place(parents[...], owner_rows, piece, domains, group)
    row = side * (domains * piece) + spot
    first = mm_nt(turn(w[:width]), mine)
    for c in range(tab.shape[0]):
        first += mm(tab[c], hot(row, c * CHUNK, blocks))
    y = norm(mm(turn(w_out[4]), silu(first)), 0)
    out[...] = (mine.astype(F32) + y.T).astype(BF16)


def spread(x, groups):
    held = {0: x}
    bit = groups >> 1
    while bit:
        for k in sorted(held):
            held[k | bit] = lax.ppermute(
                held[k], "grp", [(i, i ^ bit) for i in range(groups)]
            )
        bit >>= 1
    return [held[k] for k in range(groups)]


def swap(x):
    return lax.all_to_all(x, "dom", split_axis=0, concat_axis=0, tiled=True)


def per_device(
    fine_nodes,
    fine_edges,
    fine_senders,
    fine_receivers,
    edge_count,
    ghost_send,
    fine_parent,
    coarse_nodes,
    coarse_edges,
    coarse_senders,
    coarse_receivers,
    edge_in,
    node_in,
    mlp_out,
):
    domains = lax.axis_size("dom")
    groups = lax.axis_size("grp")
    local = fine_nodes[0]
    edges = fine_edges[0]
    nodes, width = local.shape
    slots = edges.shape[0]
    owner_rows = coarse_nodes.shape[0]
    coarse_slots = coarse_edges.shape[0]
    piece = owner_rows // groups
    ghosts = ghost_send.shape[1] * ghost_send.shape[2]
    sizes = dict(owner_rows=owner_rows, piece=piece, domains=domains)
    assert nodes % CHUNK == 0 and CHUNK % piece == 0 and piece <= LANES
    assert owner_rows * domains <= 1 << 14
    tile = max(t for t in (128, 256, 512, 1024) if slots % t == 0)
    ctile = max(t for t in (128, 256) if coarse_slots % t == 0)

    outgoing = pl.pallas_call(
        ghosts_kernel,
        out_shape=jax.ShapeDtypeStruct((ghosts, width), BF16),
        in_specs=[SMEM, VMEM],
        out_specs=VMEM,
        scratch_shapes=[pltpu.VMEM((nodes, width), F32), pltpu.VMEM((ghosts, width), F32)],
        name="ghosts",
    )(ghost_send[0], local)
    incoming = swap(outgoing)

    chunks = -(-(nodes + ghosts) // CHUNK)
    windows = nodes // CHUNK
    pack_rows = nodes + -(-2 * (nodes // LANES) // 16) * 16

    def whole(shape):
        return pl.BlockSpec(shape, lambda i: (0,) * len(shape))

    packed = pl.pallas_call(
        fine_kernel,
        out_shape=jax.ShapeDtypeStruct((pack_rows, width), BF16),
        grid=(slots // tile,),
        in_specs=[
            SMEM,
            pl.BlockSpec((1, tile), lambda i: (0, i), memory_space=pltpu.SMEM),
            pl.BlockSpec((tile, width), lambda i: (i, 0)),
            pl.BlockSpec((1, tile), lambda i: (0, i)),
            pl.BlockSpec((1, tile), lambda i: (0, i)),
            whole((nodes, width)),
            whole((ghosts, width)),
            whole((1, nodes)),
            pl.BlockSpec((None, 3 * width, width), lambda i: (0, 0, 0)),
            whole(node_in.shape),
            whole(mlp_out.shape),
        ],
        out_specs=whole((pack_rows, width)),
        scratch_shapes=[
            pltpu.VMEM((chunks, width, CHUNK), BF16),
            pltpu.VMEM((windows, width, CHUNK), BF16),
            pltpu.VMEM((width, tile), F32),
            pltpu.VMEM((nodes, width), F32),
            pltpu.VMEM((2 * width, width), BF16),
            pltpu.VMEM((width, width), BF16),
        ],
        name="fine",
    )(
        edge_count, fine_receivers, edges, fine_senders, fine_receivers, local, incoming,
        fine_parent, edge_in, node_in, mlp_out,
    )

    packs = spread(packed, groups)
    pooled = pl.pallas_call(
        functools.partial(pool_kernel, nodes=nodes, **sizes),
        out_shape=jax.ShapeDtypeStruct((domains * (piece + 16), width), BF16),
        in_specs=[VMEM] * groups,
        out_specs=VMEM,
        name="pool",
    )(*packs)
    got = swap(pooled)
    copies = jax.ShapeDtypeStruct((domains * piece, width), BF16)
    mid = pl.pallas_call(
        functools.partial(coarse_mid_kernel, piece=piece, domains=domains),
        out_shape=copies,
        in_specs=[VMEM] * 2,
        out_specs=VMEM,
        name="coarse_mid",
    )(got, coarse_nodes)
    table = pltpu.VMEM((owner_rows * domains // CHUNK, width, CHUNK), BF16)
    coarse = pl.pallas_call(
        functools.partial(coarse_kernel, groups=groups, tile=ctile, **sizes),
        out_shape=copies,
        in_specs=[VMEM] * (groups + 6),
        out_specs=VMEM,
        scratch_shapes=[table, pltpu.VMEM((piece, width), F32)],
        name="coarse",
    )(
        *spread(swap(mid), groups), coarse_edges, coarse_senders[None], coarse_receivers[None],
        edge_in, node_in, mlp_out,
    )
    fine_out, coarse_out = pl.pallas_call(
        functools.partial(return_kernel, groups=groups, nodes=nodes, **sizes),
        out_shape=(
            jax.ShapeDtypeStruct((nodes, width), BF16),
            jax.ShapeDtypeStruct((owner_rows, width), BF16),
        ),
        in_specs=[VMEM] * (groups + 4),
        out_specs=(VMEM, VMEM),
        scratch_shapes=[table],
        name="back",
    )(*spread(swap(coarse), groups), packed, fine_parent, node_in, mlp_out)
    return (fine_out[None], coarse_out)


def solution(mesh):
    placed = (
        P("grp", "dom", None),
        P("grp", "dom", None),
        P("grp", "dom"),
        P("grp", "dom"),
        P("grp", "dom"),
        P("grp", "dom", None),
        P("grp", "dom"),
        P("dom", None),
        P("dom", None),
        P("dom"),
        P("dom"),
        P(),
        P(),
        P(),
    )
    return jax.shard_map(
        per_device,
        mesh=mesh,
        in_specs=placed,
        out_specs=(P("grp", "dom", None), P("dom", None)),
        check_vma=False,
    )
```

time: 417 us -> 120 us (0.29)
  local copies, waits for them, and re-layouts: 117 us -> 2.71 us
  other arithmetic: 113 us -> 0 us
  waiting for transfers between devices: 112 us -> 26 us
  Pallas kernels: 0 us -> 32.1 us
  matrix products: 14 us -> 0 us
  between operations: 14.9 us -> 1.35 us
  starting transfers between devices: 7.62 us -> 16 us
    scatter-add x4 -> x0, other arithmetic: 98.4 us -> none  [the longest x1 60.8 us: per_device(): jax.ops.segment_sum(edge_new * live[:, None], receivers, num_segments=nod...]
    gather x9 -> x0, local copies, waits for them, and re-layouts: 93.1 us -> none  [the longest x2 29.5 us: per_device(): local[receivers]]
    all_gather x2 -> x0, waiting for transfers between devices: 59.6 us -> none  [the longest x1 36.9 us: per_device(): updated_table = lax.all_gather(coarse_out, 'dom', axis=0, tiled=True)]
    reduce_scatter x2 -> x0, waiting for transfers between devices: 52.3 us -> none  [the longest x1 30.8 us: per_device(): lax.psum_scatter(pooled.astype(jnp.bfloat16), 'dom', scatter_dimension=1,...]
    all_to_all x0 -> x3, blocking collectives: none -> 42 us  [swap(): return lax.all_to_all(x, 'dom', split_axis=0, concat_axis=0, tiled=True)]
    pallas_call x0 -> x6, Pallas kernels: none -> 32.1 us  [the longest x1 13.8 us: per_device(): pl.pallas_call(fine_kernel, out_shape=jax.ShapeDtypeStruct((pack_rows, wi...]
    unnamed x2 -> x0, blocking collectives: 27.5 us -> none
    ppermute x0 -> x9, waiting for transfers between devices: none -> 19.8 us  [spread(): lax.ppermute(held[k], 'grp', [(i, i ^ bit) for i in range(groups)])]
  transfers between devices with their start and end apart: 5 -> 10, of which waited for: 4 -> 7; matrix products, arithmetic and copies ran while one was open for 15% -> 0% of each run, Pallas kernels for 0% -> 0%
where the time goes in v1:
time: 120 us
  blocking collectives  42 us (35%)
  Pallas kernels  32.1 us (27%)
  waiting for transfers between devices  26 us (22%)
  starting transfers between devices  16 us (13%)
  local copies, waits for them, and re-layouts  2.71 us (2%)
  between operations  1.35 us (1%)
    all_to_all x3, blocking collectives, swap(): return lax.all_to_all(x, 'dom', split_axis=0, concat_axis=0, tiled=True)  42 us
    ppermute x9, waiting for transfers between devices, spread(): lax.ppermute(held[k], 'grp', [(i, i ^ bit) for i in range(groups)])  19.8 us
    pallas_call x1, Pallas kernels, per_device(): pl.pallas_call(fine_kernel, out_shape=jax.ShapeDtypeStruct((pack_rows, wi...  13.8 us
    ppermute x9, starting transfers between devices, spread(): lax.ppermute(held[k], 'grp', [(i, i ^ bit) for i in range(groups)])  8.74 us
    all_to_all x1, starting transfers between devices, swap(): return lax.all_to_all(x, 'dom', split_axis=0, concat_axis=0, tiled=True)  7.28 us
    pallas_call x1, Pallas kernels, per_device(): pl.pallas_call(functools.partial(coarse_kernel, groups=groups, tile=ctile...  7.04 us
    all_to_all x1, waiting for transfers between devices, swap(): return lax.all_to_all(x, 'dom', split_axis=0, concat_axis=0, tiled=True)  6.14 us
    pallas_call x1, Pallas kernels, per_device(): pl.pallas_call(functools.partial(return_kernel, groups=groups, nodes=node...  3.88 us
  transfers between devices with their start and end apart: 10, of which 7 were waited for; matrix products, arithmetic and copies ran while one was open for 0% of the time, Pallas kernels for 0%

profile of v1, /device:TPU:0, one launch (start us, length us, event | category | flops | bytes accessed | tf_op | source)
XLA Modules:
  0.0 120.2 jit_solution(7639433740040614677)
XLA Ops:
  0.6 1.8 %ghosts.1 = bf16[192,128]{1,0:T(8,128)(2,1)} custom-call(s32[8,24]{1,0:T(8,128)} %bitcast.31, bf16[768,128]{1,0:T(8,128)(2,1)} %bitcast.25), custom_call_target="tpu_custom_call" | custom-call | tf_op jit(solution)/shard_map/ghosts/pallas_call | solution.py:355
  2.4 7.3 %all-to-all-start = ((bf16[8,24,128]{2,1,0:T(8,128)(2,1)}), bf16[8,24,128]{2,1,0:T(8,128)(2,1)S(1)}, u32[]{:S(2)}, u32[]{:S(2)}) async-start(bf16[8,24,128]{2,1,0:T(8,128)(2,1)} %bitcast.27), calls=%async_computation | async-start | bytes 98304 | tf_op jit(solution)/shard_map/all_to_all | solution.py:320
  10.3 6.1 %all-to-all-done = bf16[8,24,128]{2,1,0:T(8,128)(2,1)S(1)} async-done(((bf16[8,24,128]{2,1,0:T(8,128)(2,1)}), bf16[8,24,128]{2,1,0:T(8,128)(2,1)S(1)}, u32[]{:S(2)}, u32[]{:S(2)}) %all-to-all-start) | async-done | bytes 49184 | tf_op jit(solution)/shard_map/all_to_all | solution.py:320
  16.5 0.0 copy-start.11
  16.5 0.6 copy-done.11
  17.1 13.8 %fine.1.refs_0_.refs_4_ = bf16[784,128]{1,0:T(8,128)(2,1)} custom-call(s32[1,1]{1,0:T(1,128)S(6)} %copy.16.count, s32[1,9216]{1,0:T(1,128)} %receivers.1, bf16[9216,128]{1,0:T(8,128)(2,1)} %bitcast.14, s32[1,9216]{1,0:T(1,128)} %senders.1, s32[1,9216]{1,0:T(1,128)} %receivers.1, bf16[768,128]{1,0:T(8,128)(2,1)} %bitcast.26, bf16[192,128]{1,0:T(8,128)(2,1)} %bitcast.28, ...), custom_call_target="tpu_custom_call" | custom-call | tf_op jit(solution)/shard_map/fine/pallas_call | solution.py:372
  30.9 5.7 %collective-permute-start.1 = (bf16[784,128]{1,0:T(8,128)(2,1)}, bf16[784,128]{1,0:T(8,128)(2,1)S(1)}, u32[]{:S(2)}, u32[]{:S(2)}) collective-permute-start(bf16[784,128]{1,0:T(8,128)(2,1)} %fine.1.refs_0_.refs_4_), channel_id=1, source_target_pairs={{0,16},{8,24},{16,0},{24,8},{1,17},{9,25},{17,1},{25,9},{2,18},{10... | collective-permute-start | bytes 602120 | tf_op jit(solution)/shard_map/ppermute | solution.py:312
  36.6 0.0 collective-permute-start
  36.6 3.9 %collective-permute-done.1.refs_2_ = bf16[784,128]{1,0:T(8,128)(2,1)S(1)} collective-permute-done((bf16[784,128]{1,0:T(8,128)(2,1)}, bf16[784,128]{1,0:T(8,128)(2,1)S(1)}, u32[]{:S(2)}, u32[]{:S(2)}) %collective-permute-start.1) | collective-permute-done | bytes 200736 | tf_op jit(solution)/shard_map/ppermute | solution.py:312
  40.5 0.0 copy-start.8
  40.5 0.0 collective-permute-start.2
  40.5 0.0 collective-permute-done.refs_1_
  40.5 0.0 copy-start.9
  40.6 1.4 %collective-permute-done.2.refs_3_ = bf16[784,128]{1,0:T(8,128)(2,1)S(1)} collective-permute-done((bf16[784,128]{1,0:T(8,128)(2,1)S(1)}, bf16[784,128]{1,0:T(8,128)(2,1)S(1)}, u32[]{:S(2)}, u32[]{:S(2)}) %collective-permute-start.2) | collective-permute-done | bytes 200736 | tf_op jit(solution)/shard_map/ppermute | solution.py:312
  42.0 0.0 copy-done.8
  42.0 0.0 copy-done.9
  42.0 0.0 copy-start.10
  42.0 0.7 copy-done.10
  42.7 3.8 %pool.1 = bf16[1152,128]{1,0:T(8,128)(2,1)} custom-call(bf16[784,128]{1,0:T(8,128)(2,1)} %fine.1.refs_0_.refs_4_, bf16[784,128]{1,0:T(8,128)(2,1)} %copy-done.9, bf16[784,128]{1,0:T(8,128)(2,1)} %copy-done.8, bf16[784,128]{1,0:T(8,128)(2,1)} %copy-done.10), custom_call_target="tpu_custom_call" | custom-call | tf_op jit(solution)/shard_map/pool/pallas_call | solution.py:405
  46.4 15.0 %all_to_all.44 = bf16[8,144,128]{2,1,0:T(8,128)(2,1)} all-to-all(bf16[8,144,128]{2,1,0:T(8,128)(2,1)} %bitcast.15), channel_id=1, replica_groups=mesh['grp'=4,'dom'=8] {'dom'}, dimensions={0} | all-to-all | bytes 589824 | tf_op jit(solution)/shard_map/all_to_all | solution.py:320
  61.4 1.8 %coarse_mid.1 = bf16[1024,128]{1,0:T(8,128)(2,1)} custom-call(bf16[1152,128]{1,0:T(8,128)(2,1)} %bitcast.16, bf16[512,128]{1,0:T(8,128)(2,1)} %nodes.1), custom_call_target="tpu_custom_call" | custom-call | tf_op jit(solution)/shard_map/coarse_mid/pallas_call | solution.py:414
  63.2 11.8 %all_to_all.45 = bf16[8,128,128]{2,1,0:T(8,128)(2,1)S(1)} all-to-all(bf16[8,128,128]{2,1,0:T(8,128)(2,1)} %bitcast.21), channel_id=1, replica_groups=mesh['grp'=4,'dom'=8] {'dom'}, dimensions={0} | all-to-all | bytes 524288 | tf_op jit(solution)/shard_map/all_to_all | solution.py:320
  75.0 2.0 %collective-permute-start.4 = (bf16[1024,128]{1,0:T(8,128)(2,1)S(1)}, bf16[1024,128]{1,0:T(8,128)(2,1)S(1)}, u32[]{:S(2)}, u32[]{:S(2)}) collective-permute-start(bf16[1024,128]{1,0:T(8,128)(2,1)S(1)} %bitcast.17), channel_id=1, source_target_pairs={{0,16},{8,24},{16,0},{24,8},{1,17},{9,25},{17,1},{25,9},{2,18},{10... | collective-permute-start | bytes 786440 | tf_op jit(solution)/shard_map/ppermute | solution.py:312
  77.1 0.0 collective-permute-start.3
  77.1 4.3 %collective-permute-done.4.refs_2_ = bf16[1024,128]{1,0:T(8,128)(2,1)S(1)} collective-permute-done((bf16[1024,128]{1,0:T(8,128)(2,1)S(1)}, bf16[1024,128]{1,0:T(8,128)(2,1)S(1)}, u32[]{:S(2)}, u32[]{:S(2)}) %collective-permute-start.4) | collective-permute-done | bytes 262176 | tf_op jit(solution)/shard_map/ppermute | solution.py:312
  81.4 0.0 collective-permute-start.5
  81.4 0.0 collective-permute-done.3.refs_1_
  81.4 0.0 copy-start.3
  81.4 1.5 %collective-permute-done.5.refs_3_ = bf16[1024,128]{1,0:T(8,128)(2,1)S(1)} collective-permute-done((bf16[1024,128]{1,0:T(8,128)(2,1)S(1)}, bf16[1024,128]{1,0:T(8,128)(2,1)S(1)}, u32[]{:S(2)}, u32[]{:S(2)}) %collective-permute-start.5) | collective-permute-done | bytes 262176 | tf_op jit(solution)/shard_map/ppermute | solution.py:312
  83.0 0.0 copy-done
  83.0 0.0 copy-done.2
  83.0 0.0 copy-done.3
  83.0 0.7 copy-done.4
  83.7 7.0 %coarse.1 = bf16[1024,128]{1,0:T(8,128)(2,1)} custom-call(bf16[1024,128]{1,0:T(8,128)(2,1)} %bitcast.19, bf16[1024,128]{1,0:T(8,128)(2,1)} %copy-done.3, bf16[1024,128]{1,0:T(8,128)(2,1)} %copy-done.2, bf16[1024,128]{1,0:T(8,128)(2,1)} %copy-done.4, bf16[4096,128]{1,0:T(8,128)(2,1)} %refs_4_.1, s32[1,4096]{1,0:T(1,128)} %bitcast.29, s32[1,4096]{1,0:T(1,128)} %bitcast.30, ...), custom_call_target="tpu_custom_call" | custom-call | tf_op jit(solution)/shard_map/coarse/pallas_call | solution.py:422
  90.7 15.2 %all_to_all.46 = bf16[8,128,128]{2,1,0:T(8,128)(2,1)S(1)} all-to-all(bf16[8,128,128]{2,1,0:T(8,128)(2,1)} %bitcast.20), channel_id=1, replica_groups=mesh['grp'=4,'dom'=8] {'dom'}, dimensions={0} | all-to-all | bytes 524288 | tf_op jit(solution)/shard_map/all_to_all | solution.py:320
  105.9 1.0 collective-permute-start.7
  106.9 0.0 collective-permute-start.6
  106.9 7.1 %collective-permute-done.7.refs_2_ = bf16[1024,128]{1,0:T(8,128)(2,1)S(1)} collective-permute-done((bf16[1024,128]{1,0:T(8,128)(2,1)S(1)}, bf16[1024,128]{1,0:T(8,128)(2,1)S(1)}, u32[]{:S(2)}, u32[]{:S(2)}) %collective-permute-start.7) | collective-permute-done | bytes 262176 | tf_op jit(solution)/shard_map/ppermute | solution.py:312
  114.0 0.0 collective-permute-start.8
  114.0 0.0 collective-permute-done.6.refs_1_
  114.0 0.0 copy-start.6
  114.0 1.5 %collective-permute-done.8.refs_3_ = bf16[1024,128]{1,0:T(8,128)(2,1)S(1)} collective-permute-done((bf16[1024,128]{1,0:T(8,128)(2,1)S(1)}, bf16[1024,128]{1,0:T(8,128)(2,1)S(1)}, u32[]{:S(2)}, u32[]{:S(2)}) %collective-permute-start.8) | collective-permute-done | bytes 262176 | tf_op jit(solution)/shard_map/ppermute | solution.py:312
  115.6 0.0 copy-done.1
  115.6 0.0 copy-done.5
  115.6 0.0 copy-done.6
  115.6 0.0 copy-start.7
  115.6 0.7 copy-done.7
  116.3 3.9 %back.1 = (bf16[768,128]{1,0:T(8,128)(2,1)}, bf16[512,128]{1,0:T(8,128)(2,1)}) custom-call(bf16[1024,128]{1,0:T(8,128)(2,1)} %bitcast.24, bf16[1024,128]{1,0:T(8,128)(2,1)} %copy-done.6, bf16[1024,128]{1,0:T(8,128)(2,1)} %copy-done.5, bf16[1024,128]{1,0:T(8,128)(2,1)} %copy-done.7, bf16[784,128]{1,0:T(8,128)(2,1)} %fine.1.refs_0_.refs_4_, s32[1,768]{1,0:T(1,128)} %refs_5_.1, ...), custom_call_target="tpu_custom_call" | custom-call | tf_op jit(solution)/shard_map/back/pallas_call | solution.py:433
  (5 shorter events, 0.0 us)
Async XLA Ops:
  2.4 14.1 %all-to-all-start = ((bf16[8,24,128]{2,1,0:T(8,128)(2,1)}), bf16[8,24,128]{2,1,0:T(8,128)(2,1)S(1)}, u32[]{:S(2)}, u32[]{:S(2)}) async-start(bf16[8,24,128]{2,1,0:T(8,128)(2,1)} %bitcast.27), calls=%async_computation | async-start | bytes 98304 | tf_op jit(solution)/shard_map/all_to_all | solution.py:320
  16.5 0.6 copy-start.11
  30.9 9.6 %collective-permute-start.1 = (bf16[784,128]{1,0:T(8,128)(2,1)}, bf16[784,128]{1,0:T(8,128)(2,1)S(1)}, u32[]{:S(2)}, u32[]{:S(2)}) collective-permute-start(bf16[784,128]{1,0:T(8,128)(2,1)} %fine.1.refs_0_.refs_4_), channel_id=1, source_target_pairs={{0,16},{8,24},{16,0},{24,8},{1,17},{9,25},{17,1},{25,9},{2,18},{10... | collective-permute-start | bytes 602120 | tf_op jit(solution)/shard_map/ppermute | solution.py:312
  36.6 3.9 %collective-permute-start = (bf16[784,128]{1,0:T(8,128)(2,1)}, bf16[784,128]{1,0:T(8,128)(2,1)S(1)}, u32[]{:S(2)}, u32[]{:S(2)}) collective-permute-start(bf16[784,128]{1,0:T(8,128)(2,1)} %fine.1.refs_0_.refs_4_), channel_id=1, source_target_pairs={{0,8},{8,0},{16,24},{24,16},{1,9},{9,1},{17,25},{25,17},{2,10},{10... | collective-permute-start | bytes 602120 | tf_op jit(solution)/shard_map/ppermute | solution.py:312
  40.5 1.5 %copy-start.8 = (bf16[784,128]{1,0:T(8,128)(2,1)}, bf16[784,128]{1,0:T(8,128)(2,1)S(1)}, u32[]{:S(2)}) copy-start(bf16[784,128]{1,0:T(8,128)(2,1)S(1)} %collective-permute-done.1.refs_2_) | copy-start | bytes 602116
  40.5 1.4 %collective-permute-start.2 = (bf16[784,128]{1,0:T(8,128)(2,1)S(1)}, bf16[784,128]{1,0:T(8,128)(2,1)S(1)}, u32[]{:S(2)}, u32[]{:S(2)}) collective-permute-start(bf16[784,128]{1,0:T(8,128)(2,1)S(1)} %collective-permute-done.1.refs_2_), channel_id=1, source_target_pairs={{0,8},{8,0},{16,24},{24,16},{1,9},{9,1},{17,25},{25,17},{2,10},{10... | collective-permute-start | bytes 602120 | tf_op jit(solution)/shard_map/ppermute | solution.py:312
  40.5 1.4 %copy-start.9 = (bf16[784,128]{1,0:T(8,128)(2,1)}, bf16[784,128]{1,0:T(8,128)(2,1)S(1)}, u32[]{:S(2)}) copy-start(bf16[784,128]{1,0:T(8,128)(2,1)S(1)} %collective-permute-done.refs_1_) | copy-start | bytes 602116
  42.0 0.7 copy-start.10
  75.0 7.9 %copy-start = (bf16[8,128,128]{2,1,0:T(8,128)(2,1)}, bf16[8,128,128]{2,1,0:T(8,128)(2,1)S(1)}, u32[]{:S(2)}) copy-start(bf16[8,128,128]{2,1,0:T(8,128)(2,1)S(1)} %all_to_all.45) | copy-start | bytes 786436
  75.0 6.4 %collective-permute-start.4 = (bf16[1024,128]{1,0:T(8,128)(2,1)S(1)}, bf16[1024,128]{1,0:T(8,128)(2,1)S(1)}, u32[]{:S(2)}, u32[]{:S(2)}) collective-permute-start(bf16[1024,128]{1,0:T(8,128)(2,1)S(1)} %bitcast.17), channel_id=1, source_target_pairs={{0,16},{8,24},{16,0},{24,8},{1,17},{9,25},{17,1},{25,9},{2,18},{10... | collective-permute-start | bytes 786440 | tf_op jit(solution)/shard_map/ppermute | solution.py:312
  77.1 4.4 %collective-permute-start.3 = (bf16[1024,128]{1,0:T(8,128)(2,1)S(1)}, bf16[1024,128]{1,0:T(8,128)(2,1)S(1)}, u32[]{:S(2)}, u32[]{:S(2)}) collective-permute-start(bf16[1024,128]{1,0:T(8,128)(2,1)S(1)} %bitcast.18), channel_id=1, source_target_pairs={{0,8},{8,0},{16,24},{24,16},{1,9},{9,1},{17,25},{25,17},{2,10},{10... | collective-permute-start | bytes 786440 | tf_op jit(solution)/shard_map/ppermute | solution.py:312
  81.4 1.5 %copy-start.2 = (bf16[1024,128]{1,0:T(8,128)(2,1)}, bf16[1024,128]{1,0:T(8,128)(2,1)S(1)}, u32[]{:S(2)}) copy-start(bf16[1024,128]{1,0:T(8,128)(2,1)S(1)} %collective-permute-done.4.refs_2_) | copy-start | bytes 786436
  81.4 1.5 %collective-permute-start.5 = (bf16[1024,128]{1,0:T(8,128)(2,1)S(1)}, bf16[1024,128]{1,0:T(8,128)(2,1)S(1)}, u32[]{:S(2)}, u32[]{:S(2)}) collective-permute-start(bf16[1024,128]{1,0:T(8,128)(2,1)S(1)} %collective-permute-done.4.refs_2_), channel_id=1, source_target_pairs={{0,8},{8,0},{16,24},{24,16},{1,9},{9,1},{17,25},{25,17},{2,10},{10... | collective-permute-start | bytes 786440 | tf_op jit(solution)/shard_map/ppermute | solution.py:312
  81.4 1.5 %copy-start.3 = (bf16[1024,128]{1,0:T(8,128)(2,1)}, bf16[1024,128]{1,0:T(8,128)(2,1)S(1)}, u32[]{:S(2)}) copy-start(bf16[1024,128]{1,0:T(8,128)(2,1)S(1)} %collective-permute-done.3.refs_1_) | copy-start | bytes 786436
  83.0 0.7 copy-start.4
  105.9 9.7 %copy-start.1 = (bf16[8,128,128]{2,1,0:T(8,128)(2,1)}, bf16[8,128,128]{2,1,0:T(8,128)(2,1)S(1)}, u32[]{:S(2)}) copy-start(bf16[8,128,128]{2,1,0:T(8,128)(2,1)S(1)} %all_to_all.46) | copy-start | bytes 786436
  105.9 8.1 %collective-permute-start.7 = (bf16[1024,128]{1,0:T(8,128)(2,1)S(1)}, bf16[1024,128]{1,0:T(8,128)(2,1)S(1)}, u32[]{:S(2)}, u32[]{:S(2)}) collective-permute-start(bf16[1024,128]{1,0:T(8,128)(2,1)S(1)} %bitcast.22), channel_id=1, source_target_pairs={{0,16},{8,24},{16,0},{24,8},{1,17},{9,25},{17,1},{25,9},{2,18},{10... | collective-permute-start | bytes 786440 | tf_op jit(solution)/shard_map/ppermute | solution.py:312
  106.9 7.1 %collective-permute-start.6 = (bf16[1024,128]{1,0:T(8,128)(2,1)S(1)}, bf16[1024,128]{1,0:T(8,128)(2,1)S(1)}, u32[]{:S(2)}, u32[]{:S(2)}) collective-permute-start(bf16[1024,128]{1,0:T(8,128)(2,1)S(1)} %bitcast.23), channel_id=1, source_target_pairs={{0,8},{8,0},{16,24},{24,16},{1,9},{9,1},{17,25},{25,17},{2,10},{10... | collective-permute-start | bytes 786440 | tf_op jit(solution)/shard_map/ppermute | solution.py:312
  114.0 1.5 %copy-start.5 = (bf16[1024,128]{1,0:T(8,128)(2,1)}, bf16[1024,128]{1,0:T(8,128)(2,1)S(1)}, u32[]{:S(2)}) copy-start(bf16[1024,128]{1,0:T(8,128)(2,1)S(1)} %collective-permute-done.7.refs_2_) | copy-start | bytes 786436
  114.0 1.5 %collective-permute-start.8 = (bf16[1024,128]{1,0:T(8,128)(2,1)S(1)}, bf16[1024,128]{1,0:T(8,128)(2,1)S(1)}, u32[]{:S(2)}, u32[]{:S(2)}) collective-permute-start(bf16[1024,128]{1,0:T(8,128)(2,1)S(1)} %collective-permute-done.7.refs_2_), channel_id=1, source_target_pairs={{0,8},{8,0},{16,24},{24,16},{1,9},{9,1},{17,25},{25,17},{2,10},{10... | collective-permute-start | bytes 786440 | tf_op jit(solution)/shard_map/ppermute | solution.py:312
  114.0 1.5 %copy-start.6 = (bf16[1024,128]{1,0:T(8,128)(2,1)}, bf16[1024,128]{1,0:T(8,128)(2,1)S(1)}, u32[]{:S(2)}) copy-start(bf16[1024,128]{1,0:T(8,128)(2,1)S(1)} %collective-permute-done.6.refs_1_) | copy-start | bytes 786436
  115.6 0.7 copy-start.7

commit v2 on v1

--- a/solution.py
+++ b/solution.py
@@ -78,72 +78,110 @@
     out[...] = picked[...].astype(BF16)
 
 
-def fine_kernel(
-    count, bounds, edges, senders, receivers, local, ghosts, parents, w_edge, w_node, w_out,
-    out, tab, rec, pre, agg, mix, second,
+def windows_after(step, base, high):
+    def run(k, _):
+        step(base + LANES * k)
+        return 0
+
+    lax.fori_loop(1, (high - base) // LANES + 1, run, 0)
+
+
+def chunk_list(rows):
+    return [(c, min(CHUNK, rows - c)) for c in range(0, rows, CHUNK)]
+
+
+def fine_first_kernel(
+    count, bounds, edges, senders, receivers, local, w_edge, pre, turned, marks, rec, tab, w_self
 ):
     step = pl.program_id(0)
-    tile, width = edges.shape
-    nodes = local.shape[0]
-    table_rows = nodes + ghosts.shape[0]
-    chunks = tab.shape[0]
-    windows = rec.shape[0]
+    tile = edges.shape[0]
+    nodes, width = local.shape
     blocks = steps(CHUNK)
+    small = steps(LANES)
 
     @pl.when(step == 0)
     def _():
         w = w_edge[...]
-        w_self = turn(w[:width])
-        w_recv = turn(w[width : 2 * width])
         w_send = turn(w[2 * width :])
-        eye = (
-            lax.broadcasted_iota(jnp.int32, (width, width), 0)
-            == lax.broadcasted_iota(jnp.int32, (width, width), 1)
-        ).astype(F32).astype(BF16)
-        mix[...] = jnp.concatenate([w_self, eye], 0)
-        second[...] = turn(w_out[0])
+        w_self[...] = turn(w[:width])
         mine = local[...]
-        for c in range(windows):
-            rec[c] = mm_nt(w_recv, mine[c * CHUNK : (c + 1) * CHUNK]).astype(BF16)
-        whole = jnp.concatenate([mine, ghosts[...]], 0)
-        extra = chunks * CHUNK - table_rows
-        if extra:
-            whole = jnp.concatenate([whole, jnp.zeros((extra, width), BF16)], 0)
-        for c in range(chunks):
-            tab[c] = mm_nt(w_send, whole[c * CHUNK : (c + 1) * CHUNK]).astype(BF16)
-        agg[...] = jnp.zeros_like(agg)
+        rec[...] = mm(mine, w[width : 2 * width]).astype(BF16)
+        for c in range(tab.shape[0]):
+            tab[c] = mm_nt(w_send, mine[c * CHUNK : (c + 1) * CHUNK]).astype(BF16)
 
     live = count[0, 0]
-
-    @pl.when(step * tile < live)
+    at = step * tile
+
+    @pl.when(at < live)
     def _():
+        low = bounds[0, 0]
+        high = bounds[0, jnp.minimum(tile, live - at) - 1]
+        base = pl.multiple_of(jnp.minimum((low >> 4) << 4, nodes - LANES), 16)
+        marks[0, step] = base
+        marks[1, step] = high
+        flat = edges[...].T
+        turned[...] = flat
+        slots = at + lax.broadcasted_iota(jnp.int32, (1, tile), 1)
+        to = jnp.where(slots < live, receivers[...], -1)
         row = senders[...]
-        both = mm_nt(mix[...], edges[...])
-        first = both[:width]
-        for c in range(chunks):
+        first = mm(
+            jnp.concatenate([w_self[...], rec[pl.ds(base, LANES), :].T], 1),
+            jnp.concatenate([flat, hot(to, base, small)], 0),
+        )
+        for c in range(tab.shape[0]):
             first += mm(tab[c], hot(row, c * CHUNK, blocks))
         pre[...] = first
-        slots = step * tile + lax.broadcasted_iota(jnp.int32, (1, tile), 1)
+
+        def more(start):
+            begin = pl.multiple_of(jnp.minimum(start, nodes - LANES), 16)
+            far_to = jnp.where(to >= start, to, -1)
+            pre[...] += mm(rec[pl.ds(begin, LANES), :].T, hot(far_to, begin, small))
+
+        windows_after(more, base, high)
+
+
+def fine_second_kernel(
+    count, marks, pre, turned, senders, receivers, local, ghosts, parents, w_edge, w_node, w_out,
+    out, agg, tabs, second,
+):
+    step = pl.program_id(0)
+    width, tile = pre.shape
+    nodes = local.shape[0]
+    small = steps(LANES)
+    blocks = steps(CHUNK)
+    pieces = chunk_list(ghosts.shape[0])
+
+    @pl.when(step == 0)
+    def _():
+        w_send = turn(w_edge[0][2 * width :])
+        for j, (c, n) in enumerate(pieces):
+            tabs[j, :, :n] = mm_nt(w_send, ghosts[pl.ds(c, n), :]).astype(BF16)
+        second[...] = turn(w_out[0])
+        agg[...] = jnp.zeros_like(agg)
+
+    live = count[0, 0]
+    at = step * tile
+
+    @pl.when(at < live)
+    def _():
+        base = pl.multiple_of(marks[0, step], 16)
+        high = marks[1, step]
+        slots = at + lax.broadcasted_iota(jnp.int32, (1, tile), 1)
         to = jnp.where(slots < live, receivers[...], -1)
-        low = bounds[0, 0]
-        high = bounds[0, tile - 1]
-
-        def inside(c):
-            return (low < (c + 1) * CHUNK) & (high >= c * CHUNK)
-
-        for c in range(windows):
-
-            @pl.when(inside(c))
-            def _():
-                pre[...] += mm(rec[c], hot(to, c * CHUNK, blocks))
-
-        y = mm(second[...], silu(pre[...]))
-        new = (both[width:] + norm(y, 0)).astype(BF16)
-        for c in range(windows):
-
-            @pl.when(inside(c))
-            def _():
-                agg[pl.ds(c * CHUNK, CHUNK), :] += mm_nt(hot(to, c * CHUNK, blocks), new)
+        row = senders[...]
+        first = pre[...]
+        for j, (c, n) in enumerate(pieces):
+            first += mm(tabs[j, :, :n], hot(row, nodes + c, blocks[: n // 16]))
+        y = mm(second[...], silu(first))
+        new = (turned[...].astype(F32) + norm(y, 0)).astype(BF16)
+        agg[pl.ds(base, LANES), :] += mm_nt(hot(to, base, small), new)
+
+        def more(start):
+            begin = pl.multiple_of(jnp.minimum(start, nodes - LANES), 16)
+            far_to = jnp.where(to >= start, to, -1)
+            agg[pl.ds(begin, LANES), :] += mm_nt(hot(far_to, begin, small), new)
+
+        windows_after(more, base, high)
 
     @pl.when(step == pl.num_programs(0) - 1)
     def _():
@@ -157,7 +195,9 @@
         parts = [ids[:, j * LANES : (j + 1) * LANES] for j in range(lines)]
         digits = [p >> 6 for p in parts] + [p & 63 for p in parts]
         digits = digits + [jnp.zeros((1, LANES), jnp.int32)] * pads
-        out[pl.ds(nodes, 2 * lines + pads), :] = jnp.concatenate(digits, 0).astype(F32).astype(BF16)
+        out[pl.ds(nodes, 2 * lines + pads), :] = (
+            jnp.concatenate(digits, 0).astype(F32).astype(BF16)
+        )
 
 
 def place(ids, owner_rows, piece, domains, group):
@@ -240,15 +280,11 @@
     blocks = steps(CHUNK)
     small = steps(piece)
     w = w_edge[1]
-    eye = (
-        lax.broadcasted_iota(jnp.int32, (width, width), 0)
-        == lax.broadcasted_iota(jnp.int32, (width, width), 1)
-    ).astype(F32).astype(BF16)
-    mix = jnp.concatenate([turn(w[:width]), eye], 0)
     fill_table(parts, turn(w[2 * width :]), tab)
     start = pl.multiple_of(domain * piece, piece)
     mine = parts[0][pl.ds(start, piece), :]
     rec = mm_nt(turn(w[width : 2 * width]), mine).astype(BF16)
+    mix = jnp.concatenate([turn(w[:width]), rec], 1)
     second = turn(w_out[2])
     agg[...] = jnp.zeros_like(agg)
     every = receivers[...]
@@ -256,23 +292,27 @@
     first_edge = jnp.sum((every < low).astype(jnp.int32))
     last_edge = jnp.sum((every < low + piece).astype(jnp.int32))
 
+    begin = (first_edge >> log2(LANES)) << log2(LANES)
+
     def one(t, _):
-        at = pl.multiple_of(t * tile, tile)
-        block = edges[pl.ds(at, tile), :]
-        side, spot = place(senders[:, pl.ds(at, tile)], owner_rows, piece, domains, group)
+        wanted = begin + t * tile
+        at = pl.multiple_of(jnp.minimum(wanted, edges.shape[0] - tile), LANES)
+        here = pl.ds(at, tile)
+        side, spot = place(senders[:, here], owner_rows, piece, domains, group)
         row = side * (domains * piece) + spot
-        both = mm_nt(mix, block)
-        to = receivers[:, pl.ds(at, tile)] - low
+        flat = edges[here, :].T
+        slots = at + lax.broadcasted_iota(jnp.int32, (1, tile), 1)
+        to = jnp.where(slots >= wanted, receivers[:, here] - low, -1)
         hot_to = hot(to, 0, small)
-        first = both[:width] + mm(rec, hot_to)
+        first = mm(mix, jnp.concatenate([flat, hot_to], 0))
         for c in range(tab.shape[0]):
             first += mm(tab[c], hot(row, c * CHUNK, blocks))
         y = mm(second, silu(first))
-        new = (both[width:] + norm(y, 0)).astype(BF16)
+        new = (flat.astype(F32) + norm(y, 0)).astype(BF16)
         agg[...] += mm_nt(hot_to, new)
         return 0
 
-    lax.fori_loop(first_edge // tile, (last_edge + tile - 1) // tile, one, 0)
+    lax.fori_loop(0, (last_edge - begin + tile - 1) // tile, one, 0)
     wn = w_node[1]
     first = mm(mine, wn[:width]) + mm(agg[...].astype(BF16), wn[width:])
     new = (mine.astype(F32) + mlp_rows(first, w_out[3])).astype(BF16)
@@ -314,6 +354,14 @@
             )
         bit >>= 1
     return [held[k] for k in range(groups)]
+
+
+def near(x):
+    return pltpu.with_memory_space_constraint(x, pltpu.VMEM)
+
+
+def far(x):
+    return pltpu.with_memory_space_constraint(x, pltpu.HBM)
 
 
 def swap(x):
@@ -349,75 +397,105 @@
     sizes = dict(owner_rows=owner_rows, piece=piece, domains=domains)
     assert nodes % CHUNK == 0 and CHUNK % piece == 0 and piece <= LANES
     assert owner_rows * domains <= 1 << 14
-    tile = max(t for t in (128, 256, 512, 1024) if slots % t == 0)
+    tile = max(t for t in (128, 256, 512, 768, 1536) if slots % t == 0)
     ctile = max(t for t in (128, 256) if coarse_slots % t == 0)
+
+    params = pltpu.CompilerParams(vmem_limit_bytes=24 << 20)
+    w_edge = near(edge_in)
+    w_node = near(node_in)
+    w_out = near(mlp_out)
+    parents = near(fine_parent)
 
     outgoing = pl.pallas_call(
         ghosts_kernel,
-        out_shape=jax.ShapeDtypeStruct((ghosts, width), BF16),
+        out_shape=pltpu.VMEM((ghosts, width), BF16),
         in_specs=[SMEM, VMEM],
         out_specs=VMEM,
         scratch_shapes=[pltpu.VMEM((nodes, width), F32), pltpu.VMEM((ghosts, width), F32)],
+        compiler_params=params,
         name="ghosts",
-    )(ghost_send[0], local)
-    incoming = swap(outgoing)
-
-    chunks = -(-(nodes + ghosts) // CHUNK)
-    windows = nodes // CHUNK
-    pack_rows = nodes + -(-2 * (nodes // LANES) // 16) * 16
+    )(far(ghost_send[0]), far(local))
+    incoming = near(swap(outgoing))
+
+    tiles = slots // tile
+    row_tile = pl.BlockSpec((1, tile), lambda i: (0, i))
+    square = pl.BlockSpec((None, width, tile), lambda i: (i, 0, 0))
 
     def whole(shape):
         return pl.BlockSpec(shape, lambda i: (0,) * len(shape))
 
-    packed = pl.pallas_call(
-        fine_kernel,
-        out_shape=jax.ShapeDtypeStruct((pack_rows, width), BF16),
-        grid=(slots // tile,),
+    pre, turned, marks = pl.pallas_call(
+        fine_first_kernel,
+        grid=(tiles,),
+        out_shape=(
+            pltpu.HBM((tiles, width, tile), F32),
+            pltpu.HBM((tiles, width, tile), BF16),
+            jax.ShapeDtypeStruct((2, tiles), jnp.int32),
+        ),
         in_specs=[
             SMEM,
             pl.BlockSpec((1, tile), lambda i: (0, i), memory_space=pltpu.SMEM),
             pl.BlockSpec((tile, width), lambda i: (i, 0)),
-            pl.BlockSpec((1, tile), lambda i: (0, i)),
-            pl.BlockSpec((1, tile), lambda i: (0, i)),
+            row_tile,
+            row_tile,
             whole((nodes, width)),
-            whole((ghosts, width)),
-            whole((1, nodes)),
             pl.BlockSpec((None, 3 * width, width), lambda i: (0, 0, 0)),
-            whole(node_in.shape),
-            whole(mlp_out.shape),
         ],
-        out_specs=whole((pack_rows, width)),
+        out_specs=(square, square, SMEM),
         scratch_shapes=[
-            pltpu.VMEM((chunks, width, CHUNK), BF16),
-            pltpu.VMEM((windows, width, CHUNK), BF16),
-            pltpu.VMEM((width, tile), F32),
-            pltpu.VMEM((nodes, width), F32),
-            pltpu.VMEM((2 * width, width), BF16),
+            pltpu.VMEM((nodes, width), BF16),
+            pltpu.VMEM((nodes // CHUNK, width, CHUNK), BF16),
             pltpu.VMEM((width, width), BF16),
         ],
-        name="fine",
+        compiler_params=params,
+        cost_estimate=pl.CostEstimate(
+            flops=2 * slots * width * (nodes + 2 * width), transcendentals=0, bytes_accessed=0
+        ),
+        name="fine_first",
     )(
-        edge_count, fine_receivers, edges, fine_senders, fine_receivers, local, incoming,
-        fine_parent, edge_in, node_in, mlp_out,
-    )
-
-    packs = spread(packed, groups)
+        edge_count, far(fine_receivers), far(edges), far(fine_senders), far(fine_receivers),
+        far(local), far(edge_in),
+    )
+
+    pack_rows = nodes + -(-2 * (nodes // LANES) // 16) * 16
+    packed = pl.pallas_call(
+        fine_second_kernel,
+        grid=(tiles,),
+        out_shape=pltpu.VMEM((pack_rows, width), BF16),
+        in_specs=[SMEM, SMEM, square, square, row_tile, row_tile] + [VMEM] * 6,
+        out_specs=VMEM,
+        scratch_shapes=[
+            pltpu.VMEM((nodes, width), F32),
+            pltpu.VMEM((len(chunk_list(ghosts)), width, CHUNK), BF16),
+            pltpu.VMEM((width, width), BF16),
+        ],
+        compiler_params=params,
+        name="fine_second",
+    )(
+        edge_count, marks, far(pre), far(turned), far(fine_senders), far(fine_receivers),
+        near(local), incoming, parents, w_edge, w_node, w_out,
+    )
+    packed = near(packed)
+
+    packs = [near(p) for p in spread(packed, groups)]
     pooled = pl.pallas_call(
         functools.partial(pool_kernel, nodes=nodes, **sizes),
-        out_shape=jax.ShapeDtypeStruct((domains * (piece + 16), width), BF16),
+        out_shape=pltpu.VMEM((domains * (piece + 16), width), BF16),
         in_specs=[VMEM] * groups,
         out_specs=VMEM,
+        compiler_params=params,
         name="pool",
     )(*packs)
-    got = swap(pooled)
-    copies = jax.ShapeDtypeStruct((domains * piece, width), BF16)
+    got = near(swap(pooled))
+    copies = pltpu.VMEM((domains * piece, width), BF16)
     mid = pl.pallas_call(
         functools.partial(coarse_mid_kernel, piece=piece, domains=domains),
         out_shape=copies,
         in_specs=[VMEM] * 2,
         out_specs=VMEM,
+        compiler_params=params,
         name="coarse_mid",
-    )(got, coarse_nodes)
+    )(got, near(coarse_nodes))
     table = pltpu.VMEM((owner_rows * domains // CHUNK, width, CHUNK), BF16)
     coarse = pl.pallas_call(
         functools.partial(coarse_kernel, groups=groups, tile=ctile, **sizes),
@@ -425,10 +503,11 @@
         in_specs=[VMEM] * (groups + 6),
         out_specs=VMEM,
         scratch_shapes=[table, pltpu.VMEM((piece, width), F32)],
+        compiler_params=params,
         name="coarse",
     )(
-        *spread(swap(mid), groups), coarse_edges, coarse_senders[None], coarse_receivers[None],
-        edge_in, node_in, mlp_out,
+        *[near(p) for p in spread(swap(mid), groups)], near(coarse_edges),
+        near(coarse_senders[None]), near(coarse_receivers[None]), w_edge, w_node, w_out,
     )
     fine_out, coarse_out = pl.pallas_call(
         functools.partial(return_kernel, groups=groups, nodes=nodes, **sizes),
@@ -439,8 +518,9 @@
         in_specs=[VMEM] * (groups + 4),
         out_specs=(VMEM, VMEM),
         scratch_shapes=[table],
+        compiler_params=params,
         name="back",
-    )(*spread(swap(coarse), groups), packed, fine_parent, node_in, mlp_out)
+    )(*[near(p) for p in spread(swap(coarse), groups)], packed, parents, w_node, w_out)
     return (fine_out[None], coarse_out)
 
 

time: 120 us -> 105 us (0.88)
  starting transfers between devices: 16 us -> 7.97 us
  waiting for transfers between devices: 26 us -> 22.6 us
  local copies, waits for them, and re-layouts: 2.71 us -> 0.06 us
  Pallas kernels: 32.1 us -> 29.8 us
    ppermute x9, starting transfers between devices: 8.74 us -> 0.68 us  [spread(): lax.ppermute(held[k], 'grp', [(i, i ^ bit) for i in range(groups)])]
    all_to_all x1, waiting for transfers between devices: 6.14 us -> 0.01 us  [swap(): return lax.all_to_all(x, 'dom', split_axis=0, concat_axis=0, tiled=True)]
    pallas_call x2 -> x3, Pallas kernels: 15.6 us -> 19.8 us  [the longest x1 9.13 us: per_device(): pl.pallas_call(fine_second_kernel, grid=(tiles,), out_shape=pltpu.VMEM((p...]
    ppermute x9, waiting for transfers between devices: 19.8 us -> 22.6 us  [spread(): lax.ppermute(held[k], 'grp', [(i, i ^ bit) for i in range(groups)])]
    unnamed x24 -> x18, local copies, waits for them, and re-layouts: 2.71 us -> 0.06 us
    pallas_call x1, Pallas kernels: 3.75 us -> 1.8 us  [per_device(): pl.pallas_call(functools.partial(pool_kernel, nodes=nodes, **sizes), out_...]
    pallas_call x1, Pallas kernels: 1.81 us -> 0.11 us  [per_device(): pl.pallas_call(functools.partial(coarse_mid_kernel, piece=piece, domains=...]
    pallas_call x1, Pallas kernels: 7.04 us -> 5.62 us  [per_device(): pl.pallas_call(functools.partial(coarse_kernel, groups=groups, tile=ctile...]
  transfers between devices with their start and end apart: 10 -> 10, of which waited for: 7 -> 6; matrix products, arithmetic and copies ran while one was open for 0% -> 0% of each run, Pallas kernels for 0% -> 9%
where the time goes in v2:
time: 105 us; the launch traced here: 104 us
  blocking collectives  42.3 us (40%)
  Pallas kernels  29.8 us (28%)
  waiting for transfers between devices  22.6 us (22%)
  starting transfers between devices  7.97 us (8%)
  between operations  1.45 us (1%)
    all_to_all x3, blocking collectives, swap(): return lax.all_to_all(x, 'dom', split_axis=0, concat_axis=0, tiled=True)  42.3 us
    ppermute x9, waiting for transfers between devices, spread(): lax.ppermute(held[k], 'grp', [(i, i ^ bit) for i in range(groups)])  22.6 us
    pallas_call x1, Pallas kernels, per_device(): pl.pallas_call(fine_second_kernel, grid=(tiles,), out_shape=pltpu.VMEM((p...  9.13 us
    pallas_call x1, Pallas kernels, per_device(): pl.pallas_call(fine_first_kernel, grid=(tiles,), out_shape=(pltpu.HBM((ti...  8.87 us
    all_to_all x1, starting transfers between devices, swap(): return lax.all_to_all(x, 'dom', split_axis=0, concat_axis=0, tiled=True)  7.28 us
    pallas_call x1, Pallas kernels, per_device(): pl.pallas_call(functools.partial(coarse_kernel, groups=groups, tile=ctile...  5.62 us
    pallas_call x1, Pallas kernels, per_device(): pl.pallas_call(functools.partial(return_kernel, groups=groups, nodes=node...  2.52 us
  transfers between devices with their start and end apart: 10, of which 6 were waited for; matrix products, arithmetic and copies ran while one was open for 0% of the time, Pallas kernels for 9%

profile of v2, /device:TPU:0, one launch (start us, length us, event | category | flops | bytes accessed | tf_op | source)
XLA Modules:
  0.0 104.3 jit_solution(11984333053251697296)
XLA Ops:
  0.6 1.8 %ghosts.1 = bf16[192,128]{1,0:T(8,128)(2,1)} custom-call(s32[8,24]{1,0:T(8,128)} %bitcast.30, bf16[768,128]{1,0:T(8,128)(2,1)} %bitcast.24), custom_call_target="tpu_custom_call" | custom-call | tf_op jit(solution)/shard_map/ghosts/pallas_call | solution.py:409
  2.4 7.3 %all-to-all-start = ((bf16[8,24,128]{2,1,0:T(8,128)(2,1)}), bf16[8,24,128]{2,1,0:T(8,128)(2,1)S(1)}, u32[]{:S(2)}, u32[]{:S(2)}) async-start(bf16[8,24,128]{2,1,0:T(8,128)(2,1)} %bitcast.3), calls=%async_computation | async-start | bytes 98304 | tf_op jit(solution)/shard_map/all_to_all | solution.py:368
  10.3 0.0 copy-start
  10.4 0.0 copy-start.1
  10.4 0.0 copy-start.3
  10.4 0.0 copy-start.4
  10.4 0.0 copy-start.8
  10.4 8.9 %fine_first.1 = (f32[6,128,1536]{2,1,0:T(8,128)}, bf16[6,128,1536]{2,1,0:T(8,128)(2,1)}, s32[2,6]{1,0:T(2,128)S(1)}) custom-call(s32[1,1]{1,0:T(1,128)S(6)} %copy.16.count, s32[1,9216]{1,0:T(1,128)} %receivers.3, bf16[9216,128]{1,0:T(8,128)(2,1)} %bitcast.31, s32[1,9216]{1,0:T(1,128)} %senders.3, s32[1,9216]{1,0:T(1,128)} %receivers.3, ...), custom_call_target="tpu_custom_call" | custom-call | flops 2415919104 | tf_op jit(solution)/shard_map/fine_first/pallas_call | solution.py:427
  19.3 0.0 all-to-all-done
  19.3 0.0 copy-done
  19.3 0.0 copy-done.1
  19.3 0.0 copy-done.3
  19.3 0.0 copy-done.4
  19.3 0.0 copy-done.8
  19.3 0.0 copy-start.5
  19.3 9.1 %fine_second.1.refs_0_.refs_4_ = bf16[784,128]{1,0:T(8,128)(2,1)S(1)} custom-call(s32[1,1]{1,0:T(1,128)S(6)} %copy.16.count, s32[2,6]{1,0:T(2,128)S(1)} %get-tuple-element.7.marks, f32[6,128,1536]{2,1,0:T(8,128)} %get-tuple-element.8.pre, bf16[6,128,1536]{2,1,0:T(8,128)(2,1)} %get-tuple-element.9.turned, s32[1,9216]{1,0:T(1,128)} %senders.3, ...), custom_call_target="tpu_custom_call" | custom-call | tf_op jit(solution)/shard_map/fine_second/pallas_call | solution.py:461
  28.5 0.0 copy-start.2
  28.5 0.0 copy-start.6
  28.5 0.0 copy-start.7
  28.5 0.1 collective-permute-start.1
  28.6 0.1 collective-permute-start
  28.7 5.6 %collective-permute-done.1.refs_2_ = bf16[784,128]{1,0:T(8,128)(2,1)S(1)} collective-permute-done((bf16[784,128]{1,0:T(8,128)(2,1)S(1)}, bf16[784,128]{1,0:T(8,128)(2,1)S(1)}, u32[]{:S(2)}, u32[]{:S(2)}) %collective-permute-start.1) | collective-permute-done | bytes 200736 | tf_op jit(solution)/shard_map/ppermute | solution.py:352
  34.3 0.0 collective-permute-start.2
  34.3 0.0 collective-permute-done.refs_1_
  34.3 1.4 %collective-permute-done.2.refs_3_ = bf16[784,128]{1,0:T(8,128)(2,1)S(1)} collective-permute-done((bf16[784,128]{1,0:T(8,128)(2,1)S(1)}, bf16[784,128]{1,0:T(8,128)(2,1)S(1)}, u32[]{:S(2)}, u32[]{:S(2)}) %collective-permute-start.2) | collective-permute-done | bytes 200736 | tf_op jit(solution)/shard_map/ppermute | solution.py:352
  35.7 1.8 %pool.1 = bf16[1152,128]{1,0:T(8,128)(2,1)S(1)} custom-call(bf16[784,128]{1,0:T(8,128)(2,1)S(1)} %fine_second.1.refs_0_.refs_4_, bf16[784,128]{1,0:T(8,128)(2,1)S(1)} %collective-permute-done.refs_1_, bf16[784,128]{1,0:T(8,128)(2,1)S(1)} %collective-permute-done.1.refs_2_, bf16[784,128]{1,0:T(8,128)(2,1)S(1)} %collective-permute-done.2.refs_3_), custom_call_target="tpu_custom_call" | custom-call | tf_op jit(solution)/shard_map/pool/pallas_call | solution.py:481
  37.5 16.9 %all_to_all.44 = bf16[8,144,128]{2,1,0:T(8,128)(2,1)S(1)} all-to-all(bf16[8,144,128]{2,1,0:T(8,128)(2,1)S(1)} %bitcast.14), channel_id=1, replica_groups=mesh['grp'=4,'dom'=8] {'dom'}, dimensions={0} | all-to-all | bytes 589824 | tf_op jit(solution)/shard_map/all_to_all | solution.py:368
  54.4 0.0 copy-done.5
  54.4 0.1 coarse_mid.1
  54.6 11.5 %all_to_all.45 = bf16[8,128,128]{2,1,0:T(8,128)(2,1)S(1)} all-to-all(bf16[8,128,128]{2,1,0:T(8,128)(2,1)S(1)} %bitcast.20), channel_id=1, replica_groups=mesh['grp'=4,'dom'=8] {'dom'}, dimensions={0} | all-to-all | bytes 524288 | tf_op jit(solution)/shard_map/all_to_all | solution.py:368
  66.1 0.3 collective-permute-start.4
  66.4 0.0 collective-permute-start.3
  66.4 6.1 %collective-permute-done.4.refs_2_ = bf16[1024,128]{1,0:T(8,128)(2,1)S(1)} collective-permute-done((bf16[1024,128]{1,0:T(8,128)(2,1)S(1)}, bf16[1024,128]{1,0:T(8,128)(2,1)S(1)}, u32[]{:S(2)}, u32[]{:S(2)}) %collective-permute-start.4) | collective-permute-done | bytes 262176 | tf_op jit(solution)/shard_map/ppermute | solution.py:352
  72.5 0.0 collective-permute-start.5
  72.5 0.0 collective-permute-done.3.refs_1_
  72.5 1.5 %collective-permute-done.5.refs_3_ = bf16[1024,128]{1,0:T(8,128)(2,1)S(1)} collective-permute-done((bf16[1024,128]{1,0:T(8,128)(2,1)S(1)}, bf16[1024,128]{1,0:T(8,128)(2,1)S(1)}, u32[]{:S(2)}, u32[]{:S(2)}) %collective-permute-start.5) | collective-permute-done | bytes 262176 | tf_op jit(solution)/shard_map/ppermute | solution.py:352
  74.0 0.0 copy-done.2
  74.0 0.0 copy-done.6
  74.0 0.0 copy-done.7
  74.0 5.6 %coarse.1 = bf16[1024,128]{1,0:T(8,128)(2,1)S(1)} custom-call(bf16[1024,128]{1,0:T(8,128)(2,1)S(1)} %bitcast.18, bf16[1024,128]{1,0:T(8,128)(2,1)S(1)} %collective-permute-done.3.refs_1_, bf16[1024,128]{1,0:T(8,128)(2,1)S(1)} %collective-permute-done.4.refs_2_, bf16[1024,128]{1,0:T(8,128)(2,1)S(1)} %collective-permute-done.5.refs_3_, ...), custom_call_target="tpu_custom_call" | custom-call | tf_op jit(solution)/shard_map/coarse/pallas_call | solution.py:500
  79.6 13.9 %all_to_all.46 = bf16[8,128,128]{2,1,0:T(8,128)(2,1)S(1)} all-to-all(bf16[8,128,128]{2,1,0:T(8,128)(2,1)S(1)} %bitcast.19), channel_id=1, replica_groups=mesh['grp'=4,'dom'=8] {'dom'}, dimensions={0} | all-to-all | bytes 524288 | tf_op jit(solution)/shard_map/all_to_all | solution.py:368
  93.5 0.2 collective-permute-start.7
  93.8 0.0 collective-permute-start.6
  93.8 6.4 %collective-permute-done.7.refs_2_ = bf16[1024,128]{1,0:T(8,128)(2,1)S(1)} collective-permute-done((bf16[1024,128]{1,0:T(8,128)(2,1)S(1)}, bf16[1024,128]{1,0:T(8,128)(2,1)S(1)}, u32[]{:S(2)}, u32[]{:S(2)}) %collective-permute-start.7) | collective-permute-done | bytes 262176 | tf_op jit(solution)/shard_map/ppermute | solution.py:352
  100.2 0.0 collective-permute-start.8
  100.2 0.0 collective-permute-done.6.refs_1_
  100.2 1.5 %collective-permute-done.8.refs_3_ = bf16[1024,128]{1,0:T(8,128)(2,1)S(1)} collective-permute-done((bf16[1024,128]{1,0:T(8,128)(2,1)S(1)}, bf16[1024,128]{1,0:T(8,128)(2,1)S(1)}, u32[]{:S(2)}, u32[]{:S(2)}) %collective-permute-start.8) | collective-permute-done | bytes 262176 | tf_op jit(solution)/shard_map/ppermute | solution.py:352
  101.7 2.5 %back.1 = (bf16[768,128]{1,0:T(8,128)(2,1)}, bf16[512,128]{1,0:T(8,128)(2,1)}) custom-call(bf16[1024,128]{1,0:T(8,128)(2,1)S(1)} %bitcast.23, bf16[1024,128]{1,0:T(8,128)(2,1)S(1)} %collective-permute-done.6.refs_1_, bf16[1024,128]{1,0:T(8,128)(2,1)S(1)} %collective-permute-done.7.refs_2_, bf16[1024,128]{1,0:T(8,128)(2,1)S(1)} %collective-permute-done.8.refs_3_, ...), custom_call_target="tpu_custom_call" | custom-call | tf_op jit(solution)/shard_map/back/pallas_call | solution.py:512
Async XLA Ops:
  2.4 16.9 %all-to-all-start = ((bf16[8,24,128]{2,1,0:T(8,128)(2,1)}), bf16[8,24,128]{2,1,0:T(8,128)(2,1)S(1)}, u32[]{:S(2)}, u32[]{:S(2)}) async-start(bf16[8,24,128]{2,1,0:T(8,128)(2,1)} %bitcast.3), calls=%async_computation | async-start | bytes 98304 | tf_op jit(solution)/shard_map/all_to_all | solution.py:368
  10.3 8.9 %copy-start = (bf16[3,256,128]{2,1,0:T(8,128)(2,1)S(1)}, bf16[3,256,128]{2,1,0:T(8,128)(2,1)}, u32[]{:S(2)}) copy-start(bf16[3,256,128]{2,1,0:T(8,128)(2,1)} %refs_6_.1) | copy-start | bytes 589828
  10.4 8.9 %copy-start.1 = (bf16[5,128,128]{2,1,0:T(8,128)(2,1)S(1)}, bf16[5,128,128]{2,1,0:T(8,128)(2,1)}, u32[]{:S(2)}) copy-start(bf16[5,128,128]{2,1,0:T(8,128)(2,1)} %refs_7_.3) | copy-start | bytes 491524
  10.4 8.9 %copy-start.3 = (bf16[2,384,128]{2,1,0:T(8,128)(2,1)S(1)}, bf16[2,384,128]{2,1,0:T(8,128)(2,1)}, u32[]{:S(2)}) copy-start(bf16[2,384,128]{2,1,0:T(8,128)(2,1)} %refs_7_.2) | copy-start | bytes 589828
  10.4 8.9 %copy-start.4 = (bf16[1,768,128]{2,1,0:T(8,128)(2,1)S(1)}, bf16[1,768,128]{2,1,0:T(8,128)(2,1)}, u32[]{:S(2)}) copy-start(bf16[1,768,128]{2,1,0:T(8,128)(2,1)} %param.14) | copy-start | bytes 589828
  10.4 8.9 %copy-start.8 = (s32[1,768]{1,0:T(1,128)S(1)}, s32[1,768]{1,0:T(1,128)}, u32[]{:S(2)}) copy-start(s32[1,768]{1,0:T(1,128)} %refs_5_.1) | copy-start | bytes 9220
  19.3 35.1 %copy-start.5 = (bf16[512,128]{1,0:T(8,128)(2,1)S(1)}, bf16[512,128]{1,0:T(8,128)(2,1)}, u32[]{:S(2)}) copy-start(bf16[512,128]{1,0:T(8,128)(2,1)} %nodes.1) | copy-start | bytes 393220
  28.5 45.5 %copy-start.2 = (bf16[4096,128]{1,0:T(8,128)(2,1)S(1)}, bf16[4096,128]{1,0:T(8,128)(2,1)}, u32[]{:S(2)}) copy-start(bf16[4096,128]{1,0:T(8,128)(2,1)} %refs_4_.1) | copy-start | bytes 3145732
  28.5 45.5 %copy-start.6 = (s32[4096]{0:T(1024)S(1)}, s32[4096]{0:T(1024)}, u32[]{:S(2)}) copy-start(s32[4096]{0:T(1024)} %param.23) | copy-start | bytes 49156
  28.5 45.5 %copy-start.7 = (s32[4096]{0:T(1024)S(1)}, s32[4096]{0:T(1024)}, u32[]{:S(2)}) copy-start(s32[4096]{0:T(1024)} %param.24) | copy-start | bytes 49156
  28.5 5.8 %collective-permute-start.1 = (bf16[784,128]{1,0:T(8,128)(2,1)S(1)}, bf16[784,128]{1,0:T(8,128)(2,1)S(1)}, u32[]{:S(2)}, u32[]{:S(2)}) collective-permute-start(bf16[784,128]{1,0:T(8,128)(2,1)S(1)} %fine_second.1.refs_0_.refs_4_), channel_id=1, source_target_pairs={{0,16},{8,24},{16,0},{24,8},{1,17},{9,25},{17,1},{25,9},{2,18},{10... | collective-permute-start | bytes 602120 | tf_op jit(solution)/shard_map/ppermute | solution.py:352
  28.6 5.7 %collective-permute-start = (bf16[784,128]{1,0:T(8,128)(2,1)S(1)}, bf16[784,128]{1,0:T(8,128)(2,1)S(1)}, u32[]{:S(2)}, u32[]{:S(2)}) collective-permute-start(bf16[784,128]{1,0:T(8,128)(2,1)S(1)} %fine_second.1.refs_0_.refs_4_), channel_id=1, source_target_pairs={{0,8},{8,0},{16,24},{24,16},{1,9},{9,1},{17,25},{25,17},{2,10},{10... | collective-permute-start | bytes 602120 | tf_op jit(solution)/shard_map/ppermute | solution.py:352
  34.3 1.4 %collective-permute-start.2 = (bf16[784,128]{1,0:T(8,128)(2,1)S(1)}, bf16[784,128]{1,0:T(8,128)(2,1)S(1)}, u32[]{:S(2)}, u32[]{:S(2)}) collective-permute-start(bf16[784,128]{1,0:T(8,128)(2,1)S(1)} %collective-permute-done.1.refs_2_), channel_id=1, source_target_pairs={{0,8},{8,0},{16,24},{24,16},{1,9},{9,1},{17,25},{25,17},{2,10},{10... | collective-permute-start | bytes 602120 | tf_op jit(solution)/shard_map/ppermute | solution.py:352
  66.1 6.4 %collective-permute-start.4 = (bf16[1024,128]{1,0:T(8,128)(2,1)S(1)}, bf16[1024,128]{1,0:T(8,128)(2,1)S(1)}, u32[]{:S(2)}, u32[]{:S(2)}) collective-permute-start(bf16[1024,128]{1,0:T(8,128)(2,1)S(1)} %bitcast.16), channel_id=1, source_target_pairs={{0,16},{8,24},{16,0},{24,8},{1,17},{9,25},{17,1},{25,9},{2,18},{10... | collective-permute-start | bytes 786440 | tf_op jit(solution)/shard_map/ppermute | solution.py:352
  66.4 6.1 %collective-permute-start.3 = (bf16[1024,128]{1,0:T(8,128)(2,1)S(1)}, bf16[1024,128]{1,0:T(8,128)(2,1)S(1)}, u32[]{:S(2)}, u32[]{:S(2)}) collective-permute-start(bf16[1024,128]{1,0:T(8,128)(2,1)S(1)} %bitcast.17), channel_id=1, source_target_pairs={{0,8},{8,0},{16,24},{24,16},{1,9},{9,1},{17,25},{25,17},{2,10},{10... | collective-permute-start | bytes 786440 | tf_op jit(solution)/shard_map/ppermute | solution.py:352
  72.5 1.5 %collective-permute-start.5 = (bf16[1024,128]{1,0:T(8,128)(2,1)S(1)}, bf16[1024,128]{1,0:T(8,128)(2,1)S(1)}, u32[]{:S(2)}, u32[]{:S(2)}) collective-permute-start(bf16[1024,128]{1,0:T(8,128)(2,1)S(1)} %collective-permute-done.4.refs_2_), channel_id=1, source_target_pairs={{0,8},{8,0},{16,24},{24,16},{1,9},{9,1},{17,25},{25,17},{2,10},{10... | collective-permute-start | bytes 786440 | tf_op jit(solution)/shard_map/ppermute | solution.py:352
  93.5 6.7 %collective-permute-start.7 = (bf16[1024,128]{1,0:T(8,128)(2,1)S(1)}, bf16[1024,128]{1,0:T(8,128)(2,1)S(1)}, u32[]{:S(2)}, u32[]{:S(2)}) collective-permute-start(bf16[1024,128]{1,0:T(8,128)(2,1)S(1)} %bitcast.21), channel_id=1, source_target_pairs={{0,16},{8,24},{16,0},{24,8},{1,17},{9,25},{17,1},{25,9},{2,18},{10... | collective-permute-start | bytes 786440 | tf_op jit(solution)/shard_map/ppermute | solution.py:352
  93.8 6.4 %collective-permute-start.6 = (bf16[1024,128]{1,0:T(8,128)(2,1)S(1)}, bf16[1024,128]{1,0:T(8,128)(2,1)S(1)}, u32[]{:S(2)}, u32[]{:S(2)}) collective-permute-start(bf16[1024,128]{1,0:T(8,128)(2,1)S(1)} %bitcast.22), channel_id=1, source_target_pairs={{0,8},{8,0},{16,24},{24,16},{1,9},{9,1},{17,25},{25,17},{2,10},{10... | collective-permute-start | bytes 786440 | tf_op jit(solution)/shard_map/ppermute | solution.py:352
  100.2 1.5 %collective-permute-start.8 = (bf16[1024,128]{1,0:T(8,128)(2,1)S(1)}, bf16[1024,128]{1,0:T(8,128)(2,1)S(1)}, u32[]{:S(2)}, u32[]{:S(2)}) collective-permute-start(bf16[1024,128]{1,0:T(8,128)(2,1)S(1)} %collective-permute-done.7.refs_2_), channel_id=1, source_target_pairs={{0,8},{8,0},{16,24},{24,16},{1,9},{9,1},{17,25},{25,17},{2,10},{10... | collective-permute-start | bytes 786440 | tf_op jit(solution)/shard_map/ppermute | solution.py:352

commit v3 on v2

--- a/solution.py
+++ b/solution.py
@@ -11,6 +11,8 @@
 BF16 = jnp.bfloat16
 NT = (((1,), (1,)), ((), ()))
 CHUNK = 256
+SUB = 256
+SUB2 = 256
 LANES = 128
 VMEM = pl.BlockSpec(memory_space=pltpu.VMEM)
 SMEM = pl.BlockSpec(memory_space=pltpu.SMEM)
@@ -78,12 +80,12 @@
     out[...] = picked[...].astype(BF16)
 
 
-def windows_after(step, base, high):
+def windows_after(step, base, high, rows):
     def run(k, _):
-        step(base + LANES * k)
+        step(base + rows * k)
         return 0
 
-    lax.fori_loop(1, (high - base) // LANES + 1, run, 0)
+    lax.fori_loop(1, (high - base) // rows + 1, run, 0)
 
 
 def chunk_list(rows):
@@ -91,113 +93,118 @@
 
 
 def fine_first_kernel(
-    count, bounds, edges, senders, receivers, local, w_edge, pre, turned, marks, rec, tab, w_self
+    count, bounds, edges, senders, receivers, local, w_edge, pre, agg, marks, rec, *, span
 ):
-    step = pl.program_id(0)
-    tile = edges.shape[0]
     nodes, width = local.shape
+    tile = pre.shape[2]
     blocks = steps(CHUNK)
     small = steps(LANES)
-
-    @pl.when(step == 0)
-    def _():
-        w = w_edge[...]
-        w_send = turn(w[2 * width :])
-        w_self[...] = turn(w[:width])
-        mine = local[...]
-        rec[...] = mm(mine, w[width : 2 * width]).astype(BF16)
-        for c in range(tab.shape[0]):
-            tab[c] = mm_nt(w_send, mine[c * CHUNK : (c + 1) * CHUNK]).astype(BF16)
-
+    w = w_edge[0]
+    w_send = turn(w[2 * width :])
+    mine = local[...]
+    rec[...] = mm(mine, w[width : 2 * width]).astype(BF16)
+    tabs = [
+        mm_nt(w_send, mine[c : c + CHUNK]).astype(BF16) for c in range(0, nodes, CHUNK)
+    ]
+    fixed = jnp.concatenate([turn(w[:width])] + tabs, 1)
+    agg[...] = jnp.zeros_like(agg)
     live = count[0, 0]
-    at = step * tile
-
-    @pl.when(at < live)
-    def _():
-        low = bounds[0, 0]
-        high = bounds[0, jnp.minimum(tile, live - at) - 1]
-        base = pl.multiple_of(jnp.minimum((low >> 4) << 4, nodes - LANES), 16)
-        marks[0, step] = base
-        marks[1, step] = high
-        flat = edges[...].T
-        turned[...] = flat
-        slots = at + lax.broadcasted_iota(jnp.int32, (1, tile), 1)
-        to = jnp.where(slots < live, receivers[...], -1)
-        row = senders[...]
-        first = mm(
-            jnp.concatenate([w_self[...], rec[pl.ds(base, LANES), :].T], 1),
-            jnp.concatenate([flat, hot(to, base, small)], 0),
-        )
-        for c in range(tab.shape[0]):
-            first += mm(tab[c], hot(row, c * CHUNK, blocks))
-        pre[...] = first
-
-        def more(start):
-            begin = pl.multiple_of(jnp.minimum(start, nodes - LANES), 16)
-            far_to = jnp.where(to >= start, to, -1)
-            pre[...] += mm(rec[pl.ds(begin, LANES), :].T, hot(far_to, begin, small))
-
-        windows_after(more, base, high)
+
+    def one(t, _):
+        later = []
+        for p in range(0, tile, span):
+            at = pl.multiple_of(t * tile + p, span)
+            low = bounds[0, at]
+            high = bounds[0, jnp.minimum(at + span, live) - 1]
+            base = pl.multiple_of(jnp.minimum((low >> 4) << 4, nodes - LANES), 16)
+            marks[0, t * (tile // span) + p // span] = base
+            marks[1, t * (tile // span) + p // span] = high
+            slots = at + lax.broadcasted_iota(jnp.int32, (1, span), 1)
+            to = jnp.where(slots < live, receivers[:, pl.ds(at, span)], -1)
+            left = jnp.concatenate([fixed, rec[pl.ds(base, LANES), :].T], 1)
+            hots = []
+            for n in range(0, span, SUB):
+                row = senders[:, pl.ds(at + n, SUB)]
+                hot_to = hot(to[:, n : n + SUB], base, small)
+                right = [edges[pl.ds(at + n, SUB), :].T]
+                right += [hot(row, c, blocks) for c in range(0, nodes, CHUNK)]
+                full = mm(left, jnp.concatenate(right + [hot_to], 0))
+                pre[t, :, p + n : p + n + SUB] = full.astype(BF16)
+                hots.append(hot_to)
+            agg[pl.ds(base, LANES), :] += mm(jnp.concatenate(hots, 1), edges[pl.ds(at, span), :])
+
+            def more(start, at=at, to=to, p=p):
+                begin = pl.multiple_of(jnp.minimum(start, nodes - LANES), 16)
+                hot_far = hot(jnp.where(to >= start, to, -1), begin, small)
+                extra = mm(rec[pl.ds(begin, LANES), :].T, hot_far)
+                here = pre[t, :, p : p + span].astype(F32)
+                pre[t, :, p : p + span] = (here + extra).astype(BF16)
+                agg[pl.ds(begin, LANES), :] += mm(hot_far, edges[pl.ds(at, span), :])
+
+            later.append((more, base, high, LANES))
+        for item in later:
+            windows_after(*item)
+        return 0
+
+    lax.fori_loop(0, (live + tile - 1) // tile, one, 0)
 
 
 def fine_second_kernel(
-    count, marks, pre, turned, senders, receivers, local, ghosts, parents, w_edge, w_node, w_out,
-    out, agg, tabs, second,
+    count, marks, pre, some, senders, receivers, local, ghosts, parents, w_edge, w_node, w_out,
+    out, agg, *, span,
 ):
-    step = pl.program_id(0)
-    width, tile = pre.shape
-    nodes = local.shape[0]
-    small = steps(LANES)
+    tile = pre.shape[2]
+    nodes, width = local.shape
+    wide = 2 * span if tile % (2 * span) == 0 else span
     blocks = steps(CHUNK)
     pieces = chunk_list(ghosts.shape[0])
-
-    @pl.when(step == 0)
-    def _():
-        w_send = turn(w_edge[0][2 * width :])
-        for j, (c, n) in enumerate(pieces):
-            tabs[j, :, :n] = mm_nt(w_send, ghosts[pl.ds(c, n), :]).astype(BF16)
-        second[...] = turn(w_out[0])
-        agg[...] = jnp.zeros_like(agg)
-
+    w_send = turn(w_edge[0][2 * width :])
+    tabs = [mm_nt(w_send, ghosts[pl.ds(c, n), :]).astype(BF16) for c, n in pieces]
+    second = turn(w_out[0])
+    agg[...] = some[...]
     live = count[0, 0]
-    at = step * tile
-
-    @pl.when(at < live)
-    def _():
-        base = pl.multiple_of(marks[0, step], 16)
-        high = marks[1, step]
-        slots = at + lax.broadcasted_iota(jnp.int32, (1, tile), 1)
-        to = jnp.where(slots < live, receivers[...], -1)
-        row = senders[...]
-        first = pre[...]
-        for j, (c, n) in enumerate(pieces):
-            first += mm(tabs[j, :, :n], hot(row, nodes + c, blocks[: n // 16]))
-        y = mm(second[...], silu(first))
-        new = (turned[...].astype(F32) + norm(y, 0)).astype(BF16)
-        agg[pl.ds(base, LANES), :] += mm_nt(hot(to, base, small), new)
-
-        def more(start):
-            begin = pl.multiple_of(jnp.minimum(start, nodes - LANES), 16)
-            far_to = jnp.where(to >= start, to, -1)
-            agg[pl.ds(begin, LANES), :] += mm_nt(hot(far_to, begin, small), new)
-
-        windows_after(more, base, high)
-
-    @pl.when(step == pl.num_programs(0) - 1)
-    def _():
-        mine = local[...]
-        w = w_node[0]
-        first = mm(mine, w[:width]) + mm(agg[...].astype(BF16), w[width:])
-        out[pl.ds(0, nodes), :] = (mine.astype(F32) + mlp_rows(first, w_out[1])).astype(BF16)
-        ids = parents[...]
-        lines = nodes // LANES
-        pads = out.shape[0] - nodes - 2 * lines
-        parts = [ids[:, j * LANES : (j + 1) * LANES] for j in range(lines)]
-        digits = [p >> 6 for p in parts] + [p & 63 for p in parts]
-        digits = digits + [jnp.zeros((1, LANES), jnp.int32)] * pads
-        out[pl.ds(nodes, 2 * lines + pads), :] = (
-            jnp.concatenate(digits, 0).astype(F32).astype(BF16)
-        )
+
+    def one(t, _):
+        later = []
+        for p in range(0, tile, wide):
+            at = pl.multiple_of(t * tile + p, wide)
+            mark = t * (tile // span) + p // span
+            base = pl.multiple_of(jnp.minimum(marks[0, mark], nodes - CHUNK), 16)
+            high = marks[1, mark + wide // span - 1]
+            slots = at + lax.broadcasted_iota(jnp.int32, (1, wide), 1)
+            to = jnp.where(slots < live, receivers[:, pl.ds(at, wide)], -1)
+            news = []
+            for n in range(0, wide, SUB2):
+                row = senders[:, pl.ds(at + n, SUB2)]
+                first = pre[t, :, p + n : p + n + SUB2].astype(F32)
+                for (c, k), tab in zip(pieces, tabs):
+                    first += mm(tab, hot(row, nodes + c, blocks[: k // 16]))
+                news.append(norm(mm(second, silu(first)), 0).astype(BF16))
+            new = jnp.concatenate(news, 1)
+            agg[pl.ds(base, CHUNK), :] += mm_nt(hot(to, base, blocks), new)
+
+            def more(start, to=to, new=new):
+                begin = pl.multiple_of(jnp.minimum(start, nodes - CHUNK), 16)
+                far_to = jnp.where(to >= start, to, -1)
+                agg[pl.ds(begin, CHUNK), :] += mm_nt(hot(far_to, begin, blocks), new)
+
+            later.append((more, base, high, CHUNK))
+        for item in later:
+            windows_after(*item)
+        return 0
+
+    lax.fori_loop(0, (live + tile - 1) // tile, one, 0)
+    mine = local[...]
+    w = w_node[0]
+    first = mm(mine, w[:width]) + mm(agg[...].astype(BF16), w[width:])
+    out[pl.ds(0, nodes), :] = (mine.astype(F32) + mlp_rows(first, w_out[1])).astype(BF16)
+    ids = parents[...]
+    lines = nodes // LANES
+    pads = out.shape[0] - nodes - 2 * lines
+    parts = [ids[:, j * LANES : (j + 1) * LANES] for j in range(lines)]
+    digits = [p >> 6 for p in parts] + [p & 63 for p in parts]
+    digits = digits + [jnp.zeros((1, LANES), jnp.int32)] * pads
+    out[pl.ds(nodes, 2 * lines + pads), :] = jnp.concatenate(digits, 0).astype(F32).astype(BF16)
 
 
 def place(ids, owner_rows, piece, domains, group):
@@ -266,6 +273,14 @@
     for k, part in enumerate(parts):
         for c in range(per):
             tab[k * per + c] = mm_nt(w, part[pl.ds(c * CHUNK, CHUNK), :]).astype(BF16)
+
+
+def look(tab, row, blocks):
+    total = 0.0
+    for c in range(0, tab.shape[0], 4):
+        left = jnp.concatenate([tab[c + j] for j in range(4)], 1)
+        total += mm(left, jnp.concatenate([hot(row, (c + j) * CHUNK, blocks) for j in range(4)], 0))
+    return total
 
 
 def coarse_kernel(
@@ -304,9 +319,7 @@
         slots = at + lax.broadcasted_iota(jnp.int32, (1, tile), 1)
         to = jnp.where(slots >= wanted, receivers[:, here] - low, -1)
         hot_to = hot(to, 0, small)
-        first = mm(mix, jnp.concatenate([flat, hot_to], 0))
-        for c in range(tab.shape[0]):
-            first += mm(tab[c], hot(row, c * CHUNK, blocks))
+        first = mm(mix, jnp.concatenate([flat, hot_to], 0)) + look(tab, row, blocks)
         y = mm(second, silu(first))
         new = (flat.astype(F32) + norm(y, 0)).astype(BF16)
         agg[...] += mm_nt(hot_to, new)
@@ -334,9 +347,9 @@
         to = pl.multiple_of((group ^ side) * piece, piece)
         coarse[pl.ds(to, piece), :] = parts[side][pl.ds(start, piece), :]
     fill_table(parts, turn(w[width:]), tab)
-    mine = packed[pl.ds(0, nodes), :]
     side, spot = place(parents[...], owner_rows, piece, domains, group)
     row = side * (domains * piece) + spot
+    mine = packed[pl.ds(0, nodes), :]
     first = mm_nt(turn(w[:width]), mine)
     for c in range(tab.shape[0]):
         first += mm(tab[c], hot(row, c * CHUNK, blocks))
@@ -397,7 +410,8 @@
     sizes = dict(owner_rows=owner_rows, piece=piece, domains=domains)
     assert nodes % CHUNK == 0 and CHUNK % piece == 0 and piece <= LANES
     assert owner_rows * domains <= 1 << 14
-    tile = max(t for t in (128, 256, 512, 768, 1536) if slots % t == 0)
+    span = max(t for t in (256, 512, 768) if slots % t == 0)
+    tile = max(span * k for k in (1, 2, 4) if slots % (span * k) == 0)
     ctile = max(t for t in (128, 256) if coarse_slots % t == 0)
 
     params = pltpu.CompilerParams(vmem_limit_bytes=24 << 20)
@@ -418,35 +432,16 @@
     incoming = near(swap(outgoing))
 
     tiles = slots // tile
-    row_tile = pl.BlockSpec((1, tile), lambda i: (0, i))
-    square = pl.BlockSpec((None, width, tile), lambda i: (i, 0, 0))
-
-    def whole(shape):
-        return pl.BlockSpec(shape, lambda i: (0,) * len(shape))
-
-    pre, turned, marks = pl.pallas_call(
-        fine_first_kernel,
-        grid=(tiles,),
+    pre, some, marks = pl.pallas_call(
+        functools.partial(fine_first_kernel, span=span),
         out_shape=(
-            pltpu.HBM((tiles, width, tile), F32),
-            pltpu.HBM((tiles, width, tile), BF16),
-            jax.ShapeDtypeStruct((2, tiles), jnp.int32),
+            pltpu.VMEM((tiles, width, tile), BF16),
+            pltpu.VMEM((nodes, width), F32),
+            pltpu.HBM((2, slots // span), jnp.int32),
         ),
-        in_specs=[
-            SMEM,
-            pl.BlockSpec((1, tile), lambda i: (0, i), memory_space=pltpu.SMEM),
-            pl.BlockSpec((tile, width), lambda i: (i, 0)),
-            row_tile,
-            row_tile,
-            whole((nodes, width)),
-            pl.BlockSpec((None, 3 * width, width), lambda i: (0, 0, 0)),
-        ],
-        out_specs=(square, square, SMEM),
-        scratch_shapes=[
-            pltpu.VMEM((nodes, width), BF16),
-            pltpu.VMEM((nodes // CHUNK, width, CHUNK), BF16),
-            pltpu.VMEM((width, width), BF16),
-        ],
+        in_specs=[SMEM, SMEM] + [VMEM] * 5,
+        out_specs=(VMEM, VMEM, SMEM),
+        scratch_shapes=[pltpu.VMEM((nodes, width), BF16)],
         compiler_params=params,
         cost_estimate=pl.CostEstimate(
             flops=2 * slots * width * (nodes + 2 * width), transcendentals=0, bytes_accessed=0
@@ -459,21 +454,16 @@
 
     pack_rows = nodes + -(-2 * (nodes // LANES) // 16) * 16
     packed = pl.pallas_call(
-        fine_second_kernel,
-        grid=(tiles,),
+        functools.partial(fine_second_kernel, span=span),
         out_shape=pltpu.VMEM((pack_rows, width), BF16),
-        in_specs=[SMEM, SMEM, square, square, row_tile, row_tile] + [VMEM] * 6,
+        in_specs=[SMEM, SMEM] + [VMEM] * 10,
         out_specs=VMEM,
-        scratch_shapes=[
-            pltpu.VMEM((nodes, width), F32),
-            pltpu.VMEM((len(chunk_list(ghosts)), width, CHUNK), BF16),
-            pltpu.VMEM((width, width), BF16),
-        ],
+        scratch_shapes=[pltpu.VMEM((nodes, width), F32)],
         compiler_params=params,
         name="fine_second",
     )(
-        edge_count, marks, far(pre), far(turned), far(fine_senders), far(fine_receivers),
-        near(local), incoming, parents, w_edge, w_node, w_out,
+        edge_count, far(marks), near(pre), near(some), far(fine_senders), far(fine_receivers),
+        near(local), incoming, far(fine_parent), w_edge, w_node, w_out,
     )
     packed = near(packed)
 

time: 105 us -> 100 us (0.952); the launches traced: 104 us -> 101 us
  Pallas kernels: 29.8 us -> 25.1 us
  starting transfers between devices: 7.97 us -> 11.9 us
  waiting for transfers between devices: 22.6 us -> 20.9 us
    pallas_call x2, Pallas kernels: 18 us -> 13.3 us  [the longest x1 6.67 us: per_device(): pl.pallas_call(functools.partial(fine_first_kernel, span=span), out_shape...]
    ppermute x9, starting transfers between devices: 0.68 us -> 4.62 us  [spread(): lax.ppermute(held[k], 'grp', [(i, i ^ bit) for i in range(groups)])]
    ppermute x9, waiting for transfers between devices: 22.6 us -> 20.9 us  [spread(): lax.ppermute(held[k], 'grp', [(i, i ^ bit) for i in range(groups)])]
  transfers between devices with their start and end apart: 10 -> 10, of which waited for: 6 -> 6; matrix products, arithmetic and copies ran while one was open for 0% -> 0% of each run, Pallas kernels for 9% -> 7%
where the time goes in v3:
time: 100 us; the launch traced here: 101 us
  blocking collectives  41.5 us (42%)
  Pallas kernels  25.1 us (25%)
  waiting for transfers between devices  20.9 us (21%)
  starting transfers between devices  11.9 us (12%)
  between operations  1.43 us (1%)
    all_to_all x3, blocking collectives, swap(): return lax.all_to_all(x, 'dom', split_axis=0, concat_axis=0, tiled=True)  41.5 us
    ppermute x9, waiting for transfers between devices, spread(): lax.ppermute(held[k], 'grp', [(i, i ^ bit) for i in range(groups)])  20.9 us
    all_to_all x1, starting transfers between devices, swap(): return lax.all_to_all(x, 'dom', split_axis=0, concat_axis=0, tiled=True)  7.28 us
    pallas_call x1, Pallas kernels, per_device(): pl.pallas_call(functools.partial(fine_first_kernel, span=span), out_shape...  6.67 us
    pallas_call x1, Pallas kernels, per_device(): pl.pallas_call(functools.partial(fine_second_kernel, span=span), out_shap...  6.63 us
    pallas_call x1, Pallas kernels, per_device(): pl.pallas_call(functools.partial(coarse_kernel, groups=groups, tile=ctile...  5.55 us
    ppermute x9, starting transfers between devices, spread(): lax.ppermute(held[k], 'grp', [(i, i ^ bit) for i in range(groups)])  4.62 us
    pallas_call x1, Pallas kernels, per_device(): pl.pallas_call(functools.partial(return_kernel, groups=groups, nodes=node...  2.52 us
  transfers between devices with their start and end apart: 10, of which 6 were waited for; matrix products, arithmetic and copies ran while one was open for 0% of the time, Pallas kernels for 7%

profile of v3, /device:TPU:0, one launch (start us, length us, event | category | flops | bytes accessed | tf_op | source)
XLA Modules:
  0.0 100.9 jit_solution(9917202940362915342)
XLA Ops:
  0.6 1.8 %ghosts.1 = bf16[192,128]{1,0:T(8,128)(2,1)} custom-call(s32[8,24]{1,0:T(8,128)} %bitcast.30, bf16[768,128]{1,0:T(8,128)(2,1)} %bitcast.24), custom_call_target="tpu_custom_call" | custom-call | tf_op jit(solution)/shard_map/ghosts/pallas_call | solution.py:423
  2.4 7.3 %all-to-all-start = ((bf16[8,24,128]{2,1,0:T(8,128)(2,1)}), bf16[8,24,128]{2,1,0:T(8,128)(2,1)S(1)}, u32[]{:S(2)}, u32[]{:S(2)}) async-start(bf16[8,24,128]{2,1,0:T(8,128)(2,1)} %bitcast.3), calls=%async_computation | async-start | bytes 98304 | tf_op jit(solution)/shard_map/all_to_all | solution.py:381
  10.3 0.0 copy-start
  10.4 0.0 copy-start.1
  10.4 0.0 copy-start.3
  10.4 0.0 copy-start.4
  10.4 6.7 %fine_first.1 = (bf16[3,128,3072]{2,1,0:T(8,128)(2,1)S(1)}, f32[768,128]{1,0:T(8,128)S(1)}, s32[2,12]{1,0:T(2,128)}) custom-call(s32[1,1]{1,0:T(1,128)S(6)} %copy.16.count, s32[1,9216]{1,0:T(1,128)} %receivers.3, bf16[9216,128]{1,0:T(8,128)(2,1)} %bitcast.31, s32[1,9216]{1,0:T(1,128)} %senders.3, s32[1,9216]{1,0:T(1,128)} %receivers.3, ...), custom_call_target="tpu_custom_call" | custom-call | flops 2415919104 | tf_op jit(solution)/shard_map/fine_first/pallas_call | solution.py:435
  17.1 0.0 all-to-all-done
  17.1 0.0 copy-done
  17.1 0.0 copy-done.1
  17.1 0.0 copy-done.3
  17.1 0.0 copy-done.4
  17.1 0.0 copy-start.5
  17.1 6.6 %fine_second.1.refs_0_.refs_4_ = bf16[784,128]{1,0:T(8,128)(2,1)S(1)} custom-call(s32[1,1]{1,0:T(1,128)S(6)} %copy.16.count, s32[2,12]{1,0:T(2,128)} %get-tuple-element.7.marks, bf16[3,128,3072]{2,1,0:T(8,128)(2,1)S(1)} %get-tuple-element.8.pre, f32[768,128]{1,0:T(8,128)S(1)} %get-tuple-element.9.some, s32[1,9216]{1,0:T(1,128)} %senders.3, ...), custom_call_target="tpu_custom_call" | custom-call | tf_op jit(solution)/shard_map/fine_second/pallas_call | solution.py:456
  23.8 0.0 copy-start.2
  23.8 0.0 copy-start.6
  23.8 0.0 copy-start.7
  23.8 1.6 %collective-permute-start.1 = (bf16[784,128]{1,0:T(8,128)(2,1)S(1)}, bf16[784,128]{1,0:T(8,128)(2,1)S(1)}, u32[]{:S(2)}, u32[]{:S(2)}) collective-permute-start(bf16[784,128]{1,0:T(8,128)(2,1)S(1)} %fine_second.1.refs_0_.refs_4_), channel_id=1, source_target_pairs={{0,16},{8,24},{16,0},{24,8},{1,17},{9,25},{17,1},{25,9},{2,18},{10... | collective-permute-start | bytes 602120 | tf_op jit(solution)/shard_map/ppermute | solution.py:365
  25.4 0.0 collective-permute-start
  25.4 4.9 %collective-permute-done.1.refs_2_ = bf16[784,128]{1,0:T(8,128)(2,1)S(1)} collective-permute-done((bf16[784,128]{1,0:T(8,128)(2,1)S(1)}, bf16[784,128]{1,0:T(8,128)(2,1)S(1)}, u32[]{:S(2)}, u32[]{:S(2)}) %collective-permute-start.1) | collective-permute-done | bytes 200736 | tf_op jit(solution)/shard_map/ppermute | solution.py:365
  30.3 0.0 collective-permute-start.2
  30.3 0.0 collective-permute-done.refs_1_
  30.3 1.4 %collective-permute-done.2.refs_3_ = bf16[784,128]{1,0:T(8,128)(2,1)S(1)} collective-permute-done((bf16[784,128]{1,0:T(8,128)(2,1)S(1)}, bf16[784,128]{1,0:T(8,128)(2,1)S(1)}, u32[]{:S(2)}, u32[]{:S(2)}) %collective-permute-start.2) | collective-permute-done | bytes 200736 | tf_op jit(solution)/shard_map/ppermute | solution.py:365
  31.8 1.8 %pool.1 = bf16[1152,128]{1,0:T(8,128)(2,1)S(1)} custom-call(bf16[784,128]{1,0:T(8,128)(2,1)S(1)} %fine_second.1.refs_0_.refs_4_, bf16[784,128]{1,0:T(8,128)(2,1)S(1)} %collective-permute-done.refs_1_, bf16[784,128]{1,0:T(8,128)(2,1)S(1)} %collective-permute-done.1.refs_2_, bf16[784,128]{1,0:T(8,128)(2,1)S(1)} %collective-permute-done.2.refs_3_), custom_call_target="tpu_custom_call" | custom-call | tf_op jit(solution)/shard_map/pool/pallas_call | solution.py:471
  33.6 16.2 %all_to_all.44 = bf16[8,144,128]{2,1,0:T(8,128)(2,1)S(1)} all-to-all(bf16[8,144,128]{2,1,0:T(8,128)(2,1)S(1)} %bitcast.14), channel_id=1, replica_groups=mesh['grp'=4,'dom'=8] {'dom'}, dimensions={0} | all-to-all | bytes 589824 | tf_op jit(solution)/shard_map/all_to_all | solution.py:381
  49.7 0.0 copy-start.8
  49.7 0.0 copy-done.5
  49.7 0.1 coarse_mid.1
  49.9 11.5 %all_to_all.45 = bf16[8,128,128]{2,1,0:T(8,128)(2,1)S(1)} all-to-all(bf16[8,128,128]{2,1,0:T(8,128)(2,1)S(1)} %bitcast.20), channel_id=1, replica_groups=mesh['grp'=4,'dom'=8] {'dom'}, dimensions={0} | all-to-all | bytes 524288 | tf_op jit(solution)/shard_map/all_to_all | solution.py:381
  61.4 1.5 %collective-permute-start.4 = (bf16[1024,128]{1,0:T(8,128)(2,1)S(1)}, bf16[1024,128]{1,0:T(8,128)(2,1)S(1)}, u32[]{:S(2)}, u32[]{:S(2)}) collective-permute-start(bf16[1024,128]{1,0:T(8,128)(2,1)S(1)} %bitcast.16), channel_id=1, source_target_pairs={{0,16},{8,24},{16,0},{24,8},{1,17},{9,25},{17,1},{25,9},{2,18},{10... | collective-permute-start | bytes 786440 | tf_op jit(solution)/shard_map/ppermute | solution.py:365
  62.9 0.0 collective-permute-start.3
  62.9 4.8 %collective-permute-done.4.refs_2_ = bf16[1024,128]{1,0:T(8,128)(2,1)S(1)} collective-permute-done((bf16[1024,128]{1,0:T(8,128)(2,1)S(1)}, bf16[1024,128]{1,0:T(8,128)(2,1)S(1)}, u32[]{:S(2)}, u32[]{:S(2)}) %collective-permute-start.4) | collective-permute-done | bytes 262176 | tf_op jit(solution)/shard_map/ppermute | solution.py:365
  67.7 0.0 collective-permute-start.5
  67.7 0.0 collective-permute-done.3.refs_1_
  67.7 1.5 %collective-permute-done.5.refs_3_ = bf16[1024,128]{1,0:T(8,128)(2,1)S(1)} collective-permute-done((bf16[1024,128]{1,0:T(8,128)(2,1)S(1)}, bf16[1024,128]{1,0:T(8,128)(2,1)S(1)}, u32[]{:S(2)}, u32[]{:S(2)}) %collective-permute-start.5) | collective-permute-done | bytes 262176 | tf_op jit(solution)/shard_map/ppermute | solution.py:365
  69.3 0.0 copy-done.2
  69.3 0.0 copy-done.6
  69.3 0.0 copy-done.7
  69.3 5.5 %coarse.1 = bf16[1024,128]{1,0:T(8,128)(2,1)S(1)} custom-call(bf16[1024,128]{1,0:T(8,128)(2,1)S(1)} %bitcast.18, bf16[1024,128]{1,0:T(8,128)(2,1)S(1)} %collective-permute-done.3.refs_1_, bf16[1024,128]{1,0:T(8,128)(2,1)S(1)} %collective-permute-done.4.refs_2_, bf16[1024,128]{1,0:T(8,128)(2,1)S(1)} %collective-permute-done.5.refs_3_, ...), custom_call_target="tpu_custom_call" | custom-call | tf_op jit(solution)/shard_map/coarse/pallas_call | solution.py:490
  74.8 13.9 %all_to_all.46 = bf16[8,128,128]{2,1,0:T(8,128)(2,1)S(1)} all-to-all(bf16[8,128,128]{2,1,0:T(8,128)(2,1)S(1)} %bitcast.19), channel_id=1, replica_groups=mesh['grp'=4,'dom'=8] {'dom'}, dimensions={0} | all-to-all | bytes 524288 | tf_op jit(solution)/shard_map/all_to_all | solution.py:381
  88.7 1.5 %collective-permute-start.7 = (bf16[1024,128]{1,0:T(8,128)(2,1)S(1)}, bf16[1024,128]{1,0:T(8,128)(2,1)S(1)}, u32[]{:S(2)}, u32[]{:S(2)}) collective-permute-start(bf16[1024,128]{1,0:T(8,128)(2,1)S(1)} %bitcast.21), channel_id=1, source_target_pairs={{0,16},{8,24},{16,0},{24,8},{1,17},{9,25},{17,1},{25,9},{2,18},{10... | collective-permute-start | bytes 786440 | tf_op jit(solution)/shard_map/ppermute | solution.py:365
  90.2 0.0 collective-permute-start.6
  90.2 6.6 %collective-permute-done.7.refs_2_ = bf16[1024,128]{1,0:T(8,128)(2,1)S(1)} collective-permute-done((bf16[1024,128]{1,0:T(8,128)(2,1)S(1)}, bf16[1024,128]{1,0:T(8,128)(2,1)S(1)}, u32[]{:S(2)}, u32[]{:S(2)}) %collective-permute-start.7) | collective-permute-done | bytes 262176 | tf_op jit(solution)/shard_map/ppermute | solution.py:365
  96.8 0.0 collective-permute-start.8
  96.8 0.0 collective-permute-done.6.refs_1_
  96.8 1.5 %collective-permute-done.8.refs_3_ = bf16[1024,128]{1,0:T(8,128)(2,1)S(1)} collective-permute-done((bf16[1024,128]{1,0:T(8,128)(2,1)S(1)}, bf16[1024,128]{1,0:T(8,128)(2,1)S(1)}, u32[]{:S(2)}, u32[]{:S(2)}) %collective-permute-start.8) | collective-permute-done | bytes 262176 | tf_op jit(solution)/shard_map/ppermute | solution.py:365
  98.4 0.0 copy-done.8
  98.4 2.5 %back.1 = (bf16[768,128]{1,0:T(8,128)(2,1)}, bf16[512,128]{1,0:T(8,128)(2,1)}) custom-call(bf16[1024,128]{1,0:T(8,128)(2,1)S(1)} %bitcast.23, bf16[1024,128]{1,0:T(8,128)(2,1)S(1)} %collective-permute-done.6.refs_1_, bf16[1024,128]{1,0:T(8,128)(2,1)S(1)} %collective-permute-done.7.refs_2_, bf16[1024,128]{1,0:T(8,128)(2,1)S(1)} %collective-permute-done.8.refs_3_, ...), custom_call_target="tpu_custom_call" | custom-call | tf_op jit(solution)/shard_map/back/pallas_call | solution.py:502
Async XLA Ops:
  2.4 14.7 %all-to-all-start = ((bf16[8,24,128]{2,1,0:T(8,128)(2,1)}), bf16[8,24,128]{2,1,0:T(8,128)(2,1)S(1)}, u32[]{:S(2)}, u32[]{:S(2)}) async-start(bf16[8,24,128]{2,1,0:T(8,128)(2,1)} %bitcast.3), calls=%async_computation | async-start | bytes 98304 | tf_op jit(solution)/shard_map/all_to_all | solution.py:381
  10.3 6.7 %copy-start = (bf16[3,256,128]{2,1,0:T(8,128)(2,1)S(1)}, bf16[3,256,128]{2,1,0:T(8,128)(2,1)}, u32[]{:S(2)}) copy-start(bf16[3,256,128]{2,1,0:T(8,128)(2,1)} %refs_6_.1) | copy-start | bytes 589828
  10.4 6.7 %copy-start.1 = (bf16[5,128,128]{2,1,0:T(8,128)(2,1)S(1)}, bf16[5,128,128]{2,1,0:T(8,128)(2,1)}, u32[]{:S(2)}) copy-start(bf16[5,128,128]{2,1,0:T(8,128)(2,1)} %refs_7_.3) | copy-start | bytes 491524
  10.4 6.7 %copy-start.3 = (bf16[2,384,128]{2,1,0:T(8,128)(2,1)S(1)}, bf16[2,384,128]{2,1,0:T(8,128)(2,1)}, u32[]{:S(2)}) copy-start(bf16[2,384,128]{2,1,0:T(8,128)(2,1)} %refs_7_.2) | copy-start | bytes 589828
  10.4 6.7 %copy-start.4 = (bf16[1,768,128]{2,1,0:T(8,128)(2,1)S(1)}, bf16[1,768,128]{2,1,0:T(8,128)(2,1)}, u32[]{:S(2)}) copy-start(bf16[1,768,128]{2,1,0:T(8,128)(2,1)} %param.14) | copy-start | bytes 589828
  17.1 32.6 %copy-start.5 = (bf16[512,128]{1,0:T(8,128)(2,1)S(1)}, bf16[512,128]{1,0:T(8,128)(2,1)}, u32[]{:S(2)}) copy-start(bf16[512,128]{1,0:T(8,128)(2,1)} %nodes.1) | copy-start | bytes 393220
  23.8 45.5 %copy-start.2 = (bf16[4096,128]{1,0:T(8,128)(2,1)S(1)}, bf16[4096,128]{1,0:T(8,128)(2,1)}, u32[]{:S(2)}) copy-start(bf16[4096,128]{1,0:T(8,128)(2,1)} %refs_4_.1) | copy-start | bytes 3145732
  23.8 45.5 %copy-start.6 = (s32[4096]{0:T(1024)S(1)}, s32[4096]{0:T(1024)}, u32[]{:S(2)}) copy-start(s32[4096]{0:T(1024)} %param.23) | copy-start | bytes 49156
  23.8 45.5 %copy-start.7 = (s32[4096]{0:T(1024)S(1)}, s32[4096]{0:T(1024)}, u32[]{:S(2)}) copy-start(s32[4096]{0:T(1024)} %param.24) | copy-start | bytes 49156
  23.8 6.5 %collective-permute-start.1 = (bf16[784,128]{1,0:T(8,128)(2,1)S(1)}, bf16[784,128]{1,0:T(8,128)(2,1)S(1)}, u32[]{:S(2)}, u32[]{:S(2)}) collective-permute-start(bf16[784,128]{1,0:T(8,128)(2,1)S(1)} %fine_second.1.refs_0_.refs_4_), channel_id=1, source_target_pairs={{0,16},{8,24},{16,0},{24,8},{1,17},{9,25},{17,1},{25,9},{2,18},{10... | collective-permute-start | bytes 602120 | tf_op jit(solution)/shard_map/ppermute | solution.py:365
  25.4 4.9 %collective-permute-start = (bf16[784,128]{1,0:T(8,128)(2,1)S(1)}, bf16[784,128]{1,0:T(8,128)(2,1)S(1)}, u32[]{:S(2)}, u32[]{:S(2)}) collective-permute-start(bf16[784,128]{1,0:T(8,128)(2,1)S(1)} %fine_second.1.refs_0_.refs_4_), channel_id=1, source_target_pairs={{0,8},{8,0},{16,24},{24,16},{1,9},{9,1},{17,25},{25,17},{2,10},{10... | collective-permute-start | bytes 602120 | tf_op jit(solution)/shard_map/ppermute | solution.py:365
  30.3 1.4 %collective-permute-start.2 = (bf16[784,128]{1,0:T(8,128)(2,1)S(1)}, bf16[784,128]{1,0:T(8,128)(2,1)S(1)}, u32[]{:S(2)}, u32[]{:S(2)}) collective-permute-start(bf16[784,128]{1,0:T(8,128)(2,1)S(1)} %collective-permute-done.1.refs_2_), channel_id=1, source_target_pairs={{0,8},{8,0},{16,24},{24,16},{1,9},{9,1},{17,25},{25,17},{2,10},{10... | collective-permute-start | bytes 602120 | tf_op jit(solution)/shard_map/ppermute | solution.py:365
  49.7 48.7 %copy-start.8 = (s32[1,768]{1,0:T(1,128)S(1)}, s32[1,768]{1,0:T(1,128)}, u32[]{:S(2)}) copy-start(s32[1,768]{1,0:T(1,128)} %refs_5_.1) | copy-start | bytes 9220
  61.4 6.4 %collective-permute-start.4 = (bf16[1024,128]{1,0:T(8,128)(2,1)S(1)}, bf16[1024,128]{1,0:T(8,128)(2,1)S(1)}, u32[]{:S(2)}, u32[]{:S(2)}) collective-permute-start(bf16[1024,128]{1,0:T(8,128)(2,1)S(1)} %bitcast.16), channel_id=1, source_target_pairs={{0,16},{8,24},{16,0},{24,8},{1,17},{9,25},{17,1},{25,9},{2,18},{10... | collective-permute-start | bytes 786440 | tf_op jit(solution)/shard_map/ppermute | solution.py:365
  62.9 4.9 %collective-permute-start.3 = (bf16[1024,128]{1,0:T(8,128)(2,1)S(1)}, bf16[1024,128]{1,0:T(8,128)(2,1)S(1)}, u32[]{:S(2)}, u32[]{:S(2)}) collective-permute-start(bf16[1024,128]{1,0:T(8,128)(2,1)S(1)} %bitcast.17), channel_id=1, source_target_pairs={{0,8},{8,0},{16,24},{24,16},{1,9},{9,1},{17,25},{25,17},{2,10},{10... | collective-permute-start | bytes 786440 | tf_op jit(solution)/shard_map/ppermute | solution.py:365
  67.7 1.5 %collective-permute-start.5 = (bf16[1024,128]{1,0:T(8,128)(2,1)S(1)}, bf16[1024,128]{1,0:T(8,128)(2,1)S(1)}, u32[]{:S(2)}, u32[]{:S(2)}) collective-permute-start(bf16[1024,128]{1,0:T(8,128)(2,1)S(1)} %collective-permute-done.4.refs_2_), channel_id=1, source_target_pairs={{0,8},{8,0},{16,24},{24,16},{1,9},{9,1},{17,25},{25,17},{2,10},{10... | collective-permute-start | bytes 786440 | tf_op jit(solution)/shard_map/ppermute | solution.py:365
  88.7 8.1 %collective-permute-start.7 = (bf16[1024,128]{1,0:T(8,128)(2,1)S(1)}, bf16[1024,128]{1,0:T(8,128)(2,1)S(1)}, u32[]{:S(2)}, u32[]{:S(2)}) collective-permute-start(bf16[1024,128]{1,0:T(8,128)(2,1)S(1)} %bitcast.21), channel_id=1, source_target_pairs={{0,16},{8,24},{16,0},{24,8},{1,17},{9,25},{17,1},{25,9},{2,18},{10... | collective-permute-start | bytes 786440 | tf_op jit(solution)/shard_map/ppermute | solution.py:365
  90.2 6.6 %collective-permute-start.6 = (bf16[1024,128]{1,0:T(8,128)(2,1)S(1)}, bf16[1024,128]{1,0:T(8,128)(2,1)S(1)}, u32[]{:S(2)}, u32[]{:S(2)}) collective-permute-start(bf16[1024,128]{1,0:T(8,128)(2,1)S(1)} %bitcast.22), channel_id=1, source_target_pairs={{0,8},{8,0},{16,24},{24,16},{1,9},{9,1},{17,25},{25,17},{2,10},{10... | collective-permute-start | bytes 786440 | tf_op jit(solution)/shard_map/ppermute | solution.py:365
  96.8 1.5 %collective-permute-start.8 = (bf16[1024,128]{1,0:T(8,128)(2,1)S(1)}, bf16[1024,128]{1,0:T(8,128)(2,1)S(1)}, u32[]{:S(2)}, u32[]{:S(2)}) collective-permute-start(bf16[1024,128]{1,0:T(8,128)(2,1)S(1)} %collective-permute-done.7.refs_2_), channel_id=1, source_target_pairs={{0,8},{8,0},{16,24},{24,16},{1,9},{9,1},{17,25},{25,17},{2,10},{10... | collective-permute-start | bytes 786440 | tf_op jit(solution)/shard_map/ppermute | solution.py:365

commit v4 on v3

--- a/solution.py
+++ b/solution.py
@@ -275,57 +275,100 @@
             tab[k * per + c] = mm_nt(w, part[pl.ds(c * CHUNK, CHUNK), :]).astype(BF16)
 
 
-def look(tab, row, blocks):
+def look(tab, row, blocks, base):
     total = 0.0
     for c in range(0, tab.shape[0], 4):
         left = jnp.concatenate([tab[c + j] for j in range(4)], 1)
-        total += mm(left, jnp.concatenate([hot(row, (c + j) * CHUNK, blocks) for j in range(4)], 0))
+        right = [hot(row, base + (c + j) * CHUNK, blocks) for j in range(4)]
+        total += mm(left, jnp.concatenate(right, 0))
     return total
 
 
-def coarse_kernel(
-    *refs, groups, owner_rows, piece, domains, tile
-):
-    parts = refs[:groups]
-    edges, senders, receivers, w_edge, w_node, w_out = refs[groups : groups + 6]
-    out, tab, agg = refs[groups + 6 :]
+def edge_range(receivers, low, piece):
+    every = receivers[...]
+    start = jnp.sum((every < low).astype(jnp.int32))
+    end = jnp.sum((every < low + piece).astype(jnp.int32))
+    return (start >> log2(LANES)) << log2(LANES), end
+
+
+def edge_tile(t, begin, tile, senders, receivers, low, owner_rows, piece, domains, group):
+    wanted = begin + t * tile
+    at = pl.multiple_of(jnp.minimum(wanted, senders.shape[1] - tile), LANES)
+    here = pl.ds(at, tile)
+    side, spot = place(senders[:, here], owner_rows, piece, domains, group)
+    slots = at + lax.broadcasted_iota(jnp.int32, (1, tile), 1)
+    to = jnp.where(slots >= wanted, receivers[:, here] - low, -1)
+    return at, side * (domains * piece) + spot, to
+
+
+def coarse_first_kernel(*refs, near_parts, owner_rows, piece, domains):
+    parts = refs[:near_parts]
+    edges, senders, receivers, w_edge = refs[near_parts : near_parts + 4]
+    pre, agg, tab = refs[near_parts + 4 :]
     group = lax.axis_index("grp")
     domain = lax.axis_index("dom")
     width = edges.shape[1]
+    tile = pre.shape[2]
     blocks = steps(CHUNK)
     small = steps(piece)
     w = w_edge[1]
     fill_table(parts, turn(w[2 * width :]), tab)
-    start = pl.multiple_of(domain * piece, piece)
-    mine = parts[0][pl.ds(start, piece), :]
+    mine = parts[0][pl.ds(pl.multiple_of(domain * piece, piece), piece), :]
     rec = mm_nt(turn(w[width : 2 * width]), mine).astype(BF16)
     mix = jnp.concatenate([turn(w[:width]), rec], 1)
+    agg[...] = jnp.zeros_like(agg)
+    low = group * piece
+    begin, end = edge_range(receivers, low, piece)
+
+    def one(t, _):
+        at, row, to = edge_tile(
+            t, begin, tile, senders, receivers, low, owner_rows, piece, domains, group
+        )
+        hots = []
+        for n in range(0, tile, SUB):
+            hot_to = hot(to[:, n : n + SUB], 0, small)
+            flat = edges[pl.ds(at + n, SUB), :].T
+            first = mm(mix, jnp.concatenate([flat, hot_to], 0))
+            first += look(tab, row[:, n : n + SUB], blocks, 0)
+            pre[t, :, n : n + SUB] = first.astype(BF16)
+            hots.append(hot_to)
+        agg[...] += mm(jnp.concatenate(hots, 1), edges[pl.ds(at, tile), :])
+        return 0
+
+    lax.fori_loop(0, (end - begin + tile - 1) // tile, one, 0)
+
+
+def coarse_second_kernel(*refs, far_parts, owner_rows, piece, domains):
+    own, *parts = refs[: far_parts + 1]
+    pre, some, senders, receivers, w_edge, w_node, w_out = refs[far_parts + 1 : far_parts + 8]
+    out, tab, agg = refs[far_parts + 8 :]
+    group = lax.axis_index("grp")
+    domain = lax.axis_index("dom")
+    width = own.shape[1]
+    tile = pre.shape[2]
+    blocks = steps(CHUNK)
+    small = steps(piece)
+    fill_table(parts, turn(w_edge[1][2 * width :]), tab)
+    mine = own[pl.ds(pl.multiple_of(domain * piece, piece), piece), :]
     second = turn(w_out[2])
-    agg[...] = jnp.zeros_like(agg)
-    every = receivers[...]
+    agg[...] = some[...]
     low = group * piece
-    first_edge = jnp.sum((every < low).astype(jnp.int32))
-    last_edge = jnp.sum((every < low + piece).astype(jnp.int32))
-
-    begin = (first_edge >> log2(LANES)) << log2(LANES)
+    begin, end = edge_range(receivers, low, piece)
+    base = far_parts * domains * piece
 
     def one(t, _):
-        wanted = begin + t * tile
-        at = pl.multiple_of(jnp.minimum(wanted, edges.shape[0] - tile), LANES)
-        here = pl.ds(at, tile)
-        side, spot = place(senders[:, here], owner_rows, piece, domains, group)
-        row = side * (domains * piece) + spot
-        flat = edges[here, :].T
-        slots = at + lax.broadcasted_iota(jnp.int32, (1, tile), 1)
-        to = jnp.where(slots >= wanted, receivers[:, here] - low, -1)
-        hot_to = hot(to, 0, small)
-        first = mm(mix, jnp.concatenate([flat, hot_to], 0)) + look(tab, row, blocks)
-        y = mm(second, silu(first))
-        new = (flat.astype(F32) + norm(y, 0)).astype(BF16)
-        agg[...] += mm_nt(hot_to, new)
+        _, row, to = edge_tile(
+            t, begin, tile, senders, receivers, low, owner_rows, piece, domains, group
+        )
+        news = []
+        for n in range(0, tile, SUB):
+            first = pre[t, :, n : n + SUB].astype(F32)
+            first += look(tab, row[:, n : n + SUB], blocks, base)
+            news.append(norm(mm(second, silu(first)), 0).astype(BF16))
+        agg[...] += mm_nt(hot(to, 0, small), jnp.concatenate(news, 1))
         return 0
 
-    lax.fori_loop(0, (last_edge - begin + tile - 1) // tile, one, 0)
+    lax.fori_loop(0, (end - begin + tile - 1) // tile, one, 0)
     wn = w_node[1]
     first = mm(mine, wn[:width]) + mm(agg[...].astype(BF16), wn[width:])
     new = (mine.astype(F32) + mlp_rows(first, w_out[3])).astype(BF16)
@@ -333,40 +376,62 @@
         out[pl.ds(s * piece, piece), :] = new
 
 
-def return_kernel(*refs, groups, owner_rows, piece, domains, nodes):
+def return_first_kernel(*refs, near_parts, owner_rows, piece, domains, nodes):
+    parts = refs[:near_parts]
+    packed, parents, w_node = refs[near_parts : near_parts + 3]
+    pre, tab = refs[near_parts + 3 :]
+    width = packed.shape[1]
+    w = w_node[2]
+    fill_table(parts, turn(w[width:]), tab)
+    side, spot = place(parents[...], owner_rows, piece, domains, lax.axis_index("grp"))
+    row = side * (domains * piece) + spot
+    first = mm_nt(turn(w[:width]), packed[pl.ds(0, nodes), :])
+    blocks = steps(CHUNK)
+    for c in range(tab.shape[0]):
+        first += mm(tab[c], hot(row, c * CHUNK, blocks))
+    pre[...] = first
+
+
+def return_second_kernel(*refs, groups, owner_rows, piece, domains, nodes):
     parts = refs[:groups]
-    packed, parents, w_node, w_out = refs[groups : groups + 4]
-    out, coarse, tab = refs[groups + 4 :]
+    pre, packed, parents, w_node, w_out = refs[groups : groups + 5]
+    out, coarse, tab = refs[groups + 5 :]
     group = lax.axis_index("grp")
     domain = lax.axis_index("dom")
     width = out.shape[1]
     blocks = steps(CHUNK)
-    w = w_node[2]
     start = pl.multiple_of(domain * piece, piece)
     for side in range(groups):
         to = pl.multiple_of((group ^ side) * piece, piece)
         coarse[pl.ds(to, piece), :] = parts[side][pl.ds(start, piece), :]
-    fill_table(parts, turn(w[width:]), tab)
+    fill_table(parts[groups // 2 :], turn(w_node[2][width:]), tab)
     side, spot = place(parents[...], owner_rows, piece, domains, group)
     row = side * (domains * piece) + spot
-    mine = packed[pl.ds(0, nodes), :]
-    first = mm_nt(turn(w[:width]), mine)
+    first = pre[...]
     for c in range(tab.shape[0]):
-        first += mm(tab[c], hot(row, c * CHUNK, blocks))
+        first += mm(tab[c], hot(row, (c + tab.shape[0]) * CHUNK, blocks))
     y = norm(mm(turn(w_out[4]), silu(first)), 0)
-    out[...] = (mine.astype(F32) + y.T).astype(BF16)
-
-
-def spread(x, groups):
+    out[...] = (packed[pl.ds(0, nodes), :].astype(F32) + y.T).astype(BF16)
+
+
+def spread(x, groups, bit):
     held = {0: x}
-    bit = groups >> 1
     while bit:
         for k in sorted(held):
             held[k | bit] = lax.ppermute(
                 held[k], "grp", [(i, i ^ bit) for i in range(groups)]
             )
         bit >>= 1
-    return [held[k] for k in range(groups)]
+    return [near(held[k]) for k in sorted(held)]
+
+
+def spread_over(x, groups, work):
+    bit = groups >> 1
+    other = lax.ppermute(x, "grp", [(i, i ^ bit) for i in range(groups)])
+    parts = spread(x, groups, bit >> 1)
+    done = work(parts)
+    other, done = lax.optimization_barrier((other, done))
+    return parts, spread(other, groups, bit >> 1), done
 
 
 def near(x):
@@ -412,7 +477,8 @@
     assert owner_rows * domains <= 1 << 14
     span = max(t for t in (256, 512, 768) if slots % t == 0)
     tile = max(span * k for k in (1, 2, 4) if slots % (span * k) == 0)
-    ctile = max(t for t in (128, 256) if coarse_slots % t == 0)
+    ctile = max(t for t in (256, 512, 1280) if coarse_slots >= t)
+    assert coarse_slots % LANES == 0 and groups % 2 == 0
 
     params = pltpu.CompilerParams(vmem_limit_bytes=24 << 20)
     w_edge = near(edge_in)
@@ -467,7 +533,7 @@
     )
     packed = near(packed)
 
-    packs = [near(p) for p in spread(packed, groups)]
+    packs = spread(packed, groups, groups >> 1)
     pooled = pl.pallas_call(
         functools.partial(pool_kernel, nodes=nodes, **sizes),
         out_shape=pltpu.VMEM((domains * (piece + 16), width), BF16),
@@ -486,31 +552,63 @@
         compiler_params=params,
         name="coarse_mid",
     )(got, near(coarse_nodes))
-    table = pltpu.VMEM((owner_rows * domains // CHUNK, width, CHUNK), BF16)
+    half = groups // 2
+    table = pltpu.VMEM((owner_rows * domains // CHUNK // 2, width, CHUNK), BF16)
+    ctiles = -(-(coarse_slots + LANES) // ctile)
+    csenders = near(coarse_senders[None])
+    creceivers = near(coarse_receivers[None])
+    cost = pl.CostEstimate(flops=1 << 31, transcendentals=0, bytes_accessed=0)
+
+    def coarse_first(parts):
+        return pl.pallas_call(
+            functools.partial(coarse_first_kernel, near_parts=half, **sizes),
+            out_shape=(pltpu.VMEM((ctiles, width, ctile), BF16), pltpu.VMEM((piece, width), F32)),
+            in_specs=[VMEM] * (half + 4),
+            out_specs=(VMEM, VMEM),
+            scratch_shapes=[table],
+            compiler_params=params,
+            cost_estimate=cost,
+            name="coarse_first",
+        )(*parts, far(coarse_edges), csenders, creceivers, w_edge)
+
+    closer, others, (cpre, csome) = spread_over(swap(mid), groups, coarse_first)
     coarse = pl.pallas_call(
-        functools.partial(coarse_kernel, groups=groups, tile=ctile, **sizes),
+        functools.partial(coarse_second_kernel, far_parts=half, **sizes),
         out_shape=copies,
-        in_specs=[VMEM] * (groups + 6),
+        in_specs=[VMEM] * (half + 8),
         out_specs=VMEM,
         scratch_shapes=[table, pltpu.VMEM((piece, width), F32)],
         compiler_params=params,
-        name="coarse",
+        name="coarse_second",
     )(
-        *[near(p) for p in spread(swap(mid), groups)], near(coarse_edges),
-        near(coarse_senders[None]), near(coarse_receivers[None]), w_edge, w_node, w_out,
-    )
+        closer[0], *others, near(cpre), near(csome), csenders, creceivers, w_edge, w_node, w_out,
+    )
+
+    def return_first(parts):
+        return pl.pallas_call(
+            functools.partial(return_first_kernel, near_parts=half, nodes=nodes, **sizes),
+            out_shape=pltpu.VMEM((width, nodes), F32),
+            in_specs=[VMEM] * (half + 3),
+            out_specs=VMEM,
+            scratch_shapes=[table],
+            compiler_params=params,
+            cost_estimate=cost,
+            name="back_first",
+        )(*parts, packed, parents, w_node)
+
+    closer, others, pre_out = spread_over(swap(coarse), groups, return_first)
     fine_out, coarse_out = pl.pallas_call(
-        functools.partial(return_kernel, groups=groups, nodes=nodes, **sizes),
+        functools.partial(return_second_kernel, groups=groups, nodes=nodes, **sizes),
         out_shape=(
             jax.ShapeDtypeStruct((nodes, width), BF16),
             jax.ShapeDtypeStruct((owner_rows, width), BF16),
         ),
-        in_specs=[VMEM] * (groups + 4),
+        in_specs=[VMEM] * (groups + 5),
         out_specs=(VMEM, VMEM),
         scratch_shapes=[table],
         compiler_params=params,
-        name="back",
-    )(*[near(p) for p in spread(swap(coarse), groups)], packed, parents, w_node, w_out)
+        name="back_second",
+    )(*closer, *others, near(pre_out), packed, parents, w_node, w_out)
     return (fine_out[None], coarse_out)
 
 

time: 100 us -> 100 us (level); the launches traced: 101 us -> 98.7 us
  blocking collectives: 41.5 us -> 39.4 us
  starting transfers between devices: 11.9 us -> 13.4 us
    ppermute x9 -> x7, waiting for transfers between devices: 20.9 us -> 9.47 us  [spread(): lax.ppermute(held[k], 'grp', [(i, i ^ bit) for i in range(groups)])]
    ppermute x0 -> x2, waiting for transfers between devices: none -> 10.8 us  [spread_over(): other = lax.ppermute(x, 'grp', [(i, i ^ bit) for i in range(groups)])]
    ppermute x0 -> x2, starting transfers between devices: none -> 3.04 us  [spread_over(): other = lax.ppermute(x, 'grp', [(i, i ^ bit) for i in range(groups)])]
    all_to_all x3, blocking collectives: 41.5 us -> 39.4 us  [swap(): return lax.all_to_all(x, 'dom', split_axis=0, concat_axis=0, tiled=True)]
    ppermute x9 -> x7, starting transfers between devices: 4.62 us -> 3.05 us  [spread(): lax.ppermute(held[k], 'grp', [(i, i ^ bit) for i in range(groups)])]
    pallas_call x1, Pallas kernels: 6.63 us -> 5.34 us  [per_device(): pl.pallas_call(functools.partial(fine_second_kernel, span=span), out_shap...]
    pallas_call x2 -> x4, Pallas kernels: 8.07 us -> 8.64 us  [the longest x1 3.2 us: per_device(): pl.pallas_call(functools.partial(coarse_second_kernel, far_parts=half, **...]
  transfers between devices with their start and end apart: 10 -> 10, of which waited for: 6 -> 6; matrix products, arithmetic and copies ran while one was open for 0% -> 0% of each run, Pallas kernels for 7% -> 10%
where the time goes in v4:
time: 100 us; the launch traced here: 98.7 us
  blocking collectives  39.4 us (39%)
  Pallas kernels  24.2 us (24%)
  waiting for transfers between devices  20.3 us (20%)
  starting transfers between devices  13.4 us (13%)
  between operations  1.44 us (1%)
    all_to_all x3, blocking collectives, swap(): return lax.all_to_all(x, 'dom', split_axis=0, concat_axis=0, tiled=True)  39.4 us
    ppermute x2, waiting for transfers between devices, spread_over(): other = lax.ppermute(x, 'grp', [(i, i ^ bit) for i in range(groups)])  10.8 us
    ppermute x7, waiting for transfers between devices, spread(): lax.ppermute(held[k], 'grp', [(i, i ^ bit) for i in range(groups)])  9.47 us
    all_to_all x1, starting transfers between devices, swap(): return lax.all_to_all(x, 'dom', split_axis=0, concat_axis=0, tiled=True)  7.28 us
    pallas_call x1, Pallas kernels, per_device(): pl.pallas_call(functools.partial(fine_first_kernel, span=span), out_shape...  6.51 us
    pallas_call x1, Pallas kernels, per_device(): pl.pallas_call(functools.partial(fine_second_kernel, span=span), out_shap...  5.34 us
    pallas_call x1, Pallas kernels, per_device(): pl.pallas_call(functools.partial(coarse_second_kernel, far_parts=half, **...  3.2 us
    ppermute x7, starting transfers between devices, spread(): lax.ppermute(held[k], 'grp', [(i, i ^ bit) for i in range(groups)])  3.05 us
  transfers between devices with their start and end apart: 10, of which 6 were waited for; matrix products, arithmetic and copies ran while one was open for 0% of the time, Pallas kernels for 10%

profile of v4, /device:TPU:0, one launch (start us, length us, event | category | flops | bytes accessed | tf_op | source)
XLA Modules:
  0.0 98.7 jit_solution(6106704286539665297)
XLA Ops:
  0.6 1.8 %ghosts.1 = bf16[192,128]{1,0:T(8,128)(2,1)} custom-call(s32[8,24]{1,0:T(8,128)} %bitcast.34, bf16[768,128]{1,0:T(8,128)(2,1)} %bitcast.26), custom_call_target="tpu_custom_call" | custom-call | tf_op jit(solution)/shard_map/ghosts/pallas_call | solution.py:489
  2.4 7.3 %all-to-all-start = ((bf16[8,24,128]{2,1,0:T(8,128)(2,1)}), bf16[8,24,128]{2,1,0:T(8,128)(2,1)S(1)}, u32[]{:S(2)}, u32[]{:S(2)}) async-start(bf16[8,24,128]{2,1,0:T(8,128)(2,1)} %bitcast.3), calls=%async_computation | async-start | bytes 98304 | tf_op jit(solution)/shard_map/all_to_all | solution.py:446
  10.3 0.0 copy-start
  10.4 0.0 copy-start.1
  10.4 0.0 copy-start.2
  10.4 0.0 copy-start.3
  10.4 6.5 %fine_first.1 = (bf16[3,128,3072]{2,1,0:T(8,128)(2,1)S(1)}, f32[768,128]{1,0:T(8,128)S(1)}, s32[2,12]{1,0:T(2,128)}) custom-call(s32[1,1]{1,0:T(1,128)S(6)} %copy.16.count, s32[1,9216]{1,0:T(1,128)} %receivers.3, bf16[9216,128]{1,0:T(8,128)(2,1)} %bitcast.35, s32[1,9216]{1,0:T(1,128)} %senders.3, s32[1,9216]{1,0:T(1,128)} %receivers.3, ...), custom_call_target="tpu_custom_call" | custom-call | flops 2415919104 | tf_op jit(solution)/shard_map/fine_first/pallas_call | solution.py:501
  16.9 0.0 all-to-all-done
  16.9 0.0 copy-done
  16.9 0.0 copy-done.1
  16.9 0.0 copy-done.2
  17.0 0.0 copy-done.3
  17.0 0.0 copy-start.4
  17.0 5.3 %fine_second.1.refs_0_.refs_2_.refs_5_ = bf16[784,128]{1,0:T(8,128)(2,1)S(1)} custom-call(s32[1,1]{1,0:T(1,128)S(6)} %copy.16.count, s32[2,12]{1,0:T(2,128)} %get-tuple-element.14.marks, bf16[3,128,3072]{2,1,0:T(8,128)(2,1)S(1)} %get-tuple-element.15.pre, f32[768,128]{1,0:T(8,128)S(1)} %get-tuple-element.16.some, s32[1,9216]{1,0:T(1,128)} %senders.3, ...), custom_call_target="tpu_custom_call" | custom-call | tf_op jit(solution)/shard_map/fine_second/pallas_call | solution.py:522
  22.3 0.0 copy-start.5
  22.3 0.0 copy-start.6
  22.4 3.0 %collective-permute-start.1 = (bf16[784,128]{1,0:T(8,128)(2,1)S(1)}, bf16[784,128]{1,0:T(8,128)(2,1)S(1)}, u32[]{:S(2)}, u32[]{:S(2)}) collective-permute-start(bf16[784,128]{1,0:T(8,128)(2,1)S(1)} %fine_second.1.refs_0_.refs_2_.refs_5_), channel_id=1, source_target_pairs={{0,16},{8,24},{16,0},{24,8},{1,17},{9,25},{17,1},{25,9},{2,18},{10... | collective-permute-start | bytes 602120 | tf_op jit(solution)/shard_map/ppermute | solution.py:421
  25.4 0.0 collective-permute-start
  25.4 4.9 %collective-permute-done.1.refs_2_ = bf16[784,128]{1,0:T(8,128)(2,1)S(1)} collective-permute-done((bf16[784,128]{1,0:T(8,128)(2,1)S(1)}, bf16[784,128]{1,0:T(8,128)(2,1)S(1)}, u32[]{:S(2)}, u32[]{:S(2)}) %collective-permute-start.1) | collective-permute-done | bytes 200736 | tf_op jit(solution)/shard_map/ppermute | solution.py:421
  30.3 0.0 collective-permute-start.2
  30.3 0.0 collective-permute-done.refs_1_
  30.3 1.4 %collective-permute-done.2.refs_3_ = bf16[784,128]{1,0:T(8,128)(2,1)S(1)} collective-permute-done((bf16[784,128]{1,0:T(8,128)(2,1)S(1)}, bf16[784,128]{1,0:T(8,128)(2,1)S(1)}, u32[]{:S(2)}, u32[]{:S(2)}) %collective-permute-start.2) | collective-permute-done | bytes 200736 | tf_op jit(solution)/shard_map/ppermute | solution.py:421
  31.8 1.8 %pool.1 = bf16[1152,128]{1,0:T(8,128)(2,1)S(1)} custom-call(bf16[784,128]{1,0:T(8,128)(2,1)S(1)} %fine_second.1.refs_0_.refs_2_.refs_5_, bf16[784,128]{1,0:T(8,128)(2,1)S(1)} %collective-permute-done.refs_1_, bf16[784,128]{1,0:T(8,128)(2,1)S(1)} %collective-permute-done.1.refs_2_, bf16[784,128]{1,0:T(8,128)(2,1)S(1)} %collective-permute-done.2.refs_3_), custom_call_target="tpu_custom_call" | custom-call | tf_op jit(solution)/shard_map/pool/pallas_call | solution.py:537
  33.6 15.3 %all_to_all.44 = bf16[8,144,128]{2,1,0:T(8,128)(2,1)S(1)} all-to-all(bf16[8,144,128]{2,1,0:T(8,128)(2,1)S(1)} %bitcast.14), channel_id=1, replica_groups=mesh['grp'=4,'dom'=8] {'dom'}, dimensions={0} | all-to-all | bytes 589824 | tf_op jit(solution)/shard_map/all_to_all | solution.py:446
  48.8 0.0 copy-done.4
  48.8 0.1 coarse_mid.1
  48.9 11.5 %all_to_all.45 = bf16[8,128,128]{2,1,0:T(8,128)(2,1)S(1)} all-to-all(bf16[8,128,128]{2,1,0:T(8,128)(2,1)S(1)} %bitcast.25), channel_id=1, replica_groups=mesh['grp'=4,'dom'=8] {'dom'}, dimensions={0} | all-to-all | bytes 524288 | tf_op jit(solution)/shard_map/all_to_all | solution.py:446
  60.5 0.0 collective-permute-start.4
  60.5 1.5 %collective-permute-start.3 = (bf16[1024,128]{1,0:T(8,128)(2,1)S(1)}, bf16[1024,128]{1,0:T(8,128)(2,1)S(1)}, u32[]{:S(2)}, u32[]{:S(2)}) collective-permute-start(bf16[1024,128]{1,0:T(8,128)(2,1)S(1)} %bitcast.17), channel_id=1, source_target_pairs={{0,16},{8,24},{16,0},{24,8},{1,17},{9,25},{17,1},{25,9},{2,18},{10... | collective-permute-start | bytes 786440 | tf_op jit(solution)/shard_map/ppermute | solution.py:430
  62.0 0.0 collective-permute-done.4.refs_1_
  62.0 0.0 copy-done.5
  62.0 0.0 copy-done.6
  62.0 2.6 %coarse_first.1 = (bf16[4,128,1280]{2,1,0:T(8,128)(2,1)S(1)}, f32[128,128]{1,0:T(8,128)S(1)}) custom-call(bf16[1024,128]{1,0:T(8,128)(2,1)S(1)} %bitcast.18, bf16[1024,128]{1,0:T(8,128)(2,1)S(1)} %collective-permute-done.4.refs_1_, bf16[4096,128]{1,0:T(8,128)(2,1)} %refs_2_.1, s32[1,4096]{1,0:T(1,128)S(1)} %bitcast.30, s32[1,4096]{1,0:T(1,128)S(1)} %bitcast.32, ...), custom_call_target="tpu_custom_call" | custom-call | flops 2147483648 | tf_op jit(solution)/shard_map/coarse_first/pallas_call | solution.py:563
  64.6 0.0 copy-start.7
  64.6 4.5 %collective-permute-done.3.refs_1_ = bf16[1024,128]{1,0:T(8,128)(2,1)S(1)} collective-permute-done((bf16[1024,128]{1,0:T(8,128)(2,1)S(1)}, bf16[1024,128]{1,0:T(8,128)(2,1)S(1)}, u32[]{:S(2)}, u32[]{:S(2)}) %collective-permute-start.3) | collective-permute-done | bytes 262176 | tf_op jit(solution)/shard_map/ppermute | solution.py:430
  69.2 0.0 collective-permute-start.5
  69.2 1.5 %collective-permute-done.5.refs_2_ = bf16[1024,128]{1,0:T(8,128)(2,1)S(1)} collective-permute-done((bf16[1024,128]{1,0:T(8,128)(2,1)S(1)}, bf16[1024,128]{1,0:T(8,128)(2,1)S(1)}, u32[]{:S(2)}, u32[]{:S(2)}) %collective-permute-start.5) | collective-permute-done | bytes 262176 | tf_op jit(solution)/shard_map/ppermute | solution.py:421
  70.7 3.2 %coarse_second.1 = bf16[1024,128]{1,0:T(8,128)(2,1)S(1)} custom-call(bf16[1024,128]{1,0:T(8,128)(2,1)S(1)} %bitcast.19, bf16[1024,128]{1,0:T(8,128)(2,1)S(1)} %collective-permute-done.3.refs_1_, bf16[1024,128]{1,0:T(8,128)(2,1)S(1)} %collective-permute-done.5.refs_2_, bf16[4,128,1280]{2,1,0:T(8,128)(2,1)S(1)} %get-tuple-element.20.refs_3_, ...), custom_call_target="tpu_custom_call" | custom-call | tf_op jit(solution)/shard_map/coarse_second/pallas_call | solution.py:575
  73.9 12.6 %all_to_all.46 = bf16[8,128,128]{2,1,0:T(8,128)(2,1)S(1)} all-to-all(bf16[8,128,128]{2,1,0:T(8,128)(2,1)S(1)} %bitcast.24), channel_id=1, replica_groups=mesh['grp'=4,'dom'=8] {'dom'}, dimensions={0} | all-to-all | bytes 524288 | tf_op jit(solution)/shard_map/all_to_all | solution.py:446
  86.5 0.0 collective-permute-start.6
  86.5 1.5 %collective-permute-start.7 = (bf16[1024,128]{1,0:T(8,128)(2,1)S(1)}, bf16[1024,128]{1,0:T(8,128)(2,1)S(1)}, u32[]{:S(2)}, u32[]{:S(2)}) collective-permute-start(bf16[1024,128]{1,0:T(8,128)(2,1)S(1)} %bitcast.21), channel_id=1, source_target_pairs={{0,16},{8,24},{16,0},{24,8},{1,17},{9,25},{17,1},{25,9},{2,18},{10... | collective-permute-start | bytes 786440 | tf_op jit(solution)/shard_map/ppermute | solution.py:430
  88.0 0.0 collective-permute-done.6.refs_1_
  88.1 0.0 copy-done.7
  88.1 0.9 back_first.1.refs_4_
  89.0 6.3 %collective-permute-done.7.refs_2_ = bf16[1024,128]{1,0:T(8,128)(2,1)S(1)} collective-permute-done((bf16[1024,128]{1,0:T(8,128)(2,1)S(1)}, bf16[1024,128]{1,0:T(8,128)(2,1)S(1)}, u32[]{:S(2)}, u32[]{:S(2)}) %collective-permute-start.7) | collective-permute-done | bytes 262176 | tf_op jit(solution)/shard_map/ppermute | solution.py:430
  95.2 0.0 collective-permute-start.8
  95.2 1.5 %collective-permute-done.8.refs_3_ = bf16[1024,128]{1,0:T(8,128)(2,1)S(1)} collective-permute-done((bf16[1024,128]{1,0:T(8,128)(2,1)S(1)}, bf16[1024,128]{1,0:T(8,128)(2,1)S(1)}, u32[]{:S(2)}, u32[]{:S(2)}) %collective-permute-start.8) | collective-permute-done | bytes 262176 | tf_op jit(solution)/shard_map/ppermute | solution.py:421
  96.8 1.9 %back_second.1 = (bf16[768,128]{1,0:T(8,128)(2,1)}, bf16[512,128]{1,0:T(8,128)(2,1)}) custom-call(bf16[1024,128]{1,0:T(8,128)(2,1)S(1)} %bitcast.23, bf16[1024,128]{1,0:T(8,128)(2,1)S(1)} %collective-permute-done.6.refs_1_, bf16[1024,128]{1,0:T(8,128)(2,1)S(1)} %collective-permute-done.7.refs_2_, bf16[1024,128]{1,0:T(8,128)(2,1)S(1)} %collective-permute-done.8.refs_3_, ...), custom_call_target="tpu_custom_call" | custom-call | tf_op jit(solution)/shard_map/back_second/pallas_call | solution.py:600
Async XLA Ops:
  2.4 14.5 %all-to-all-start = ((bf16[8,24,128]{2,1,0:T(8,128)(2,1)}), bf16[8,24,128]{2,1,0:T(8,128)(2,1)S(1)}, u32[]{:S(2)}, u32[]{:S(2)}) async-start(bf16[8,24,128]{2,1,0:T(8,128)(2,1)} %bitcast.3), calls=%async_computation | async-start | bytes 98304 | tf_op jit(solution)/shard_map/all_to_all | solution.py:446
  10.3 6.6 %copy-start = (bf16[3,256,128]{2,1,0:T(8,128)(2,1)S(1)}, bf16[3,256,128]{2,1,0:T(8,128)(2,1)}, u32[]{:S(2)}) copy-start(bf16[3,256,128]{2,1,0:T(8,128)(2,1)} %refs_7_.3) | copy-start | bytes 589828
  10.4 6.6 %copy-start.1 = (bf16[5,128,128]{2,1,0:T(8,128)(2,1)S(1)}, bf16[5,128,128]{2,1,0:T(8,128)(2,1)}, u32[]{:S(2)}) copy-start(bf16[5,128,128]{2,1,0:T(8,128)(2,1)} %refs_8_.3) | copy-start | bytes 491524
  10.4 6.6 %copy-start.2 = (bf16[2,384,128]{2,1,0:T(8,128)(2,1)S(1)}, bf16[2,384,128]{2,1,0:T(8,128)(2,1)}, u32[]{:S(2)}) copy-start(bf16[2,384,128]{2,1,0:T(8,128)(2,1)} %refs_7_.2) | copy-start | bytes 589828
  10.4 6.6 %copy-start.3 = (bf16[1,768,128]{2,1,0:T(8,128)(2,1)S(1)}, bf16[1,768,128]{2,1,0:T(8,128)(2,1)}, u32[]{:S(2)}) copy-start(bf16[1,768,128]{2,1,0:T(8,128)(2,1)} %param.14) | copy-start | bytes 589828
  17.0 31.9 %copy-start.4 = (bf16[512,128]{1,0:T(8,128)(2,1)S(1)}, bf16[512,128]{1,0:T(8,128)(2,1)}, u32[]{:S(2)}) copy-start(bf16[512,128]{1,0:T(8,128)(2,1)} %nodes.1) | copy-start | bytes 393220
  22.3 39.7 %copy-start.5 = (s32[4096]{0:T(1024)S(1)}, s32[4096]{0:T(1024)}, u32[]{:S(2)}) copy-start(s32[4096]{0:T(1024)} %param.23) | copy-start | bytes 49156
  22.3 39.7 %copy-start.6 = (s32[4096]{0:T(1024)S(1)}, s32[4096]{0:T(1024)}, u32[]{:S(2)}) copy-start(s32[4096]{0:T(1024)} %param.24) | copy-start | bytes 49156
  22.4 8.0 %collective-permute-start.1 = (bf16[784,128]{1,0:T(8,128)(2,1)S(1)}, bf16[784,128]{1,0:T(8,128)(2,1)S(1)}, u32[]{:S(2)}, u32[]{:S(2)}) collective-permute-start(bf16[784,128]{1,0:T(8,128)(2,1)S(1)} %fine_second.1.refs_0_.refs_2_.refs_5_), channel_id=1, source_target_pairs={{0,16},{8,24},{16,0},{24,8},{1,17},{9,25},{17,1},{25,9},{2,18},{10... | collective-permute-start | bytes 602120 | tf_op jit(solution)/shard_map/ppermute | solution.py:421
  25.4 4.9 %collective-permute-start = (bf16[784,128]{1,0:T(8,128)(2,1)S(1)}, bf16[784,128]{1,0:T(8,128)(2,1)S(1)}, u32[]{:S(2)}, u32[]{:S(2)}) collective-permute-start(bf16[784,128]{1,0:T(8,128)(2,1)S(1)} %fine_second.1.refs_0_.refs_2_.refs_5_), channel_id=1, source_target_pairs={{0,8},{8,0},{16,24},{24,16},{1,9},{9,1},{17,25},{25,17},{2,10},{10... | collective-permute-start | bytes 602120 | tf_op jit(solution)/shard_map/ppermute | solution.py:421
  30.3 1.4 %collective-permute-start.2 = (bf16[784,128]{1,0:T(8,128)(2,1)S(1)}, bf16[784,128]{1,0:T(8,128)(2,1)S(1)}, u32[]{:S(2)}, u32[]{:S(2)}) collective-permute-start(bf16[784,128]{1,0:T(8,128)(2,1)S(1)} %collective-permute-done.1.refs_2_), channel_id=1, source_target_pairs={{0,8},{8,0},{16,24},{24,16},{1,9},{9,1},{17,25},{25,17},{2,10},{10... | collective-permute-start | bytes 602120 | tf_op jit(solution)/shard_map/ppermute | solution.py:421
  60.5 1.5 %collective-permute-start.4 = (bf16[1024,128]{1,0:T(8,128)(2,1)S(1)}, bf16[1024,128]{1,0:T(8,128)(2,1)S(1)}, u32[]{:S(2)}, u32[]{:S(2)}) collective-permute-start(bf16[1024,128]{1,0:T(8,128)(2,1)S(1)} %bitcast.16), channel_id=1, source_target_pairs={{0,8},{8,0},{16,24},{24,16},{1,9},{9,1},{17,25},{25,17},{2,10},{10... | collective-permute-start | bytes 786440 | tf_op jit(solution)/shard_map/ppermute | solution.py:421
  60.5 8.7 %collective-permute-start.3 = (bf16[1024,128]{1,0:T(8,128)(2,1)S(1)}, bf16[1024,128]{1,0:T(8,128)(2,1)S(1)}, u32[]{:S(2)}, u32[]{:S(2)}) collective-permute-start(bf16[1024,128]{1,0:T(8,128)(2,1)S(1)} %bitcast.17), channel_id=1, source_target_pairs={{0,16},{8,24},{16,0},{24,8},{1,17},{9,25},{17,1},{25,9},{2,18},{10... | collective-permute-start | bytes 786440 | tf_op jit(solution)/shard_map/ppermute | solution.py:430
  64.6 23.4 %copy-start.7 = (s32[1,768]{1,0:T(1,128)S(1)}, s32[1,768]{1,0:T(1,128)}, u32[]{:S(2)}) copy-start(s32[1,768]{1,0:T(1,128)} %refs_6_.1) | copy-start | bytes 9220
  69.2 1.5 %collective-permute-start.5 = (bf16[1024,128]{1,0:T(8,128)(2,1)S(1)}, bf16[1024,128]{1,0:T(8,128)(2,1)S(1)}, u32[]{:S(2)}, u32[]{:S(2)}) collective-permute-start(bf16[1024,128]{1,0:T(8,128)(2,1)S(1)} %collective-permute-done.3.refs_1_), channel_id=1, source_target_pairs={{0,8},{8,0},{16,24},{24,16},{1,9},{9,1},{17,25},{25,17},{2,10},{10... | collective-permute-start | bytes 786440 | tf_op jit(solution)/shard_map/ppermute | solution.py:421
  86.5 1.5 %collective-permute-start.6 = (bf16[1024,128]{1,0:T(8,128)(2,1)S(1)}, bf16[1024,128]{1,0:T(8,128)(2,1)S(1)}, u32[]{:S(2)}, u32[]{:S(2)}) collective-permute-start(bf16[1024,128]{1,0:T(8,128)(2,1)S(1)} %bitcast.20), channel_id=1, source_target_pairs={{0,8},{8,0},{16,24},{24,16},{1,9},{9,1},{17,25},{25,17},{2,10},{10... | collective-permute-start | bytes 786440 | tf_op jit(solution)/shard_map/ppermute | solution.py:421
  86.5 8.7 %collective-permute-start.7 = (bf16[1024,128]{1,0:T(8,128)(2,1)S(1)}, bf16[1024,128]{1,0:T(8,128)(2,1)S(1)}, u32[]{:S(2)}, u32[]{:S(2)}) collective-permute-start(bf16[1024,128]{1,0:T(8,128)(2,1)S(1)} %bitcast.21), channel_id=1, source_target_pairs={{0,16},{8,24},{16,0},{24,8},{1,17},{9,25},{17,1},{25,9},{2,18},{10... | collective-permute-start | bytes 786440 | tf_op jit(solution)/shard_map/ppermute | solution.py:430
  95.2 1.5 %collective-permute-start.8 = (bf16[1024,128]{1,0:T(8,128)(2,1)S(1)}, bf16[1024,128]{1,0:T(8,128)(2,1)S(1)}, u32[]{:S(2)}, u32[]{:S(2)}) collective-permute-start(bf16[1024,128]{1,0:T(8,128)(2,1)S(1)} %collective-permute-done.7.refs_2_), channel_id=1, source_target_pairs={{0,8},{8,0},{16,24},{24,16},{1,9},{9,1},{17,25},{25,17},{2,10},{10... | collective-permute-start | bytes 786440 | tf_op jit(solution)/shard_map/ppermute | solution.py:421

commit v5 on v4

--- a/solution.py
+++ b/solution.py
@@ -6,6 +6,7 @@
 from jax.experimental import pallas as pl
 from jax.experimental.pallas import tpu as pltpu
 from jax.sharding import PartitionSpec as P
+
 
 F32 = jnp.float32
 BF16 = jnp.bfloat16
@@ -207,7 +208,7 @@
     out[pl.ds(nodes, 2 * lines + pads), :] = jnp.concatenate(digits, 0).astype(F32).astype(BF16)
 
 
-def place(ids, owner_rows, piece, domains, group):
+def place(ids, owner_rows, piece, group):
     owner = ids >> log2(owner_rows)
     within = ids & (owner_rows - 1)
     return (within >> log2(piece)) ^ group, owner * piece + (within & (piece - 1))
@@ -227,7 +228,7 @@
         ids = jnp.concatenate(
             [(tail[j : j + 1] << 6) + tail[lines + j : lines + j + 1] for j in range(lines)], 1
         )
-        side, spot = place(ids, owner_rows, piece, domains, group)
+        side, spot = place(ids, owner_rows, piece, group)
         spots.append(jnp.where(side == 0, spot, -1))
         fulls.append(
             jnp.concatenate([pack[pl.ds(0, nodes), :], jnp.ones((nodes, LANES), BF16)], 1)
@@ -295,7 +296,7 @@
     wanted = begin + t * tile
     at = pl.multiple_of(jnp.minimum(wanted, senders.shape[1] - tile), LANES)
     here = pl.ds(at, tile)
-    side, spot = place(senders[:, here], owner_rows, piece, domains, group)
+    side, spot = place(senders[:, here], owner_rows, piece, group)
     slots = at + lax.broadcasted_iota(jnp.int32, (1, tile), 1)
     to = jnp.where(slots >= wanted, receivers[:, here] - low, -1)
     return at, side * (domains * piece) + spot, to
@@ -383,7 +384,7 @@
     width = packed.shape[1]
     w = w_node[2]
     fill_table(parts, turn(w[width:]), tab)
-    side, spot = place(parents[...], owner_rows, piece, domains, lax.axis_index("grp"))
+    side, spot = place(parents[...], owner_rows, piece, lax.axis_index("grp"))
     row = side * (domains * piece) + spot
     first = mm_nt(turn(w[:width]), packed[pl.ds(0, nodes), :])
     blocks = steps(CHUNK)
@@ -405,7 +406,7 @@
         to = pl.multiple_of((group ^ side) * piece, piece)
         coarse[pl.ds(to, piece), :] = parts[side][pl.ds(start, piece), :]
     fill_table(parts[groups // 2 :], turn(w_node[2][width:]), tab)
-    side, spot = place(parents[...], owner_rows, piece, domains, group)
+    side, spot = place(parents[...], owner_rows, piece, group)
     row = side * (domains * piece) + spot
     first = pre[...]
     for c in range(tab.shape[0]):

time: 100 us -> 99.8 us (level)
  Pallas kernels: 24.2 us -> 25.6 us
  starting transfers between devices: 13.4 us -> 12.4 us
    ppermute x7, starting transfers between devices: 3.05 us -> 1.6 us  [spread(): lax.ppermute(held[k], 'grp', [(i, i ^ bit) for i in range(groups)])]
    pallas_call x1, Pallas kernels: 5.34 us -> 6.63 us  [per_device(): pl.pallas_call(functools.partial(fine_second_kernel, span=span), out_shap...]
where the time goes in v5:
time: 99.8 us; the launch traced here: 99.4 us
  blocking collectives  40.3 us (40%)
  Pallas kernels  25.6 us (26%)
  waiting for transfers between devices  19.6 us (20%)
  starting transfers between devices  12.4 us (12%)
  between operations  1.44 us (1%)
    all_to_all x3, blocking collectives, swap(): return lax.all_to_all(x, 'dom', split_axis=0, concat_axis=0, tiled=True)  40.3 us
    ppermute x2, waiting for transfers between devices, spread_over(): other = lax.ppermute(x, 'grp', [(i, i ^ bit) for i in range(groups)])  10.4 us
    ppermute x7, waiting for transfers between devices, spread(): lax.ppermute(held[k], 'grp', [(i, i ^ bit) for i in range(groups)])  9.22 us
    all_to_all x1, starting transfers between devices, swap(): return lax.all_to_all(x, 'dom', split_axis=0, concat_axis=0, tiled=True)  7.28 us
    pallas_call x1, Pallas kernels, per_device(): pl.pallas_call(functools.partial(fine_first_kernel, span=span), out_shape...  6.67 us
    pallas_call x1, Pallas kernels, per_device(): pl.pallas_call(functools.partial(fine_second_kernel, span=span), out_shap...  6.63 us
    ppermute x2, starting transfers between devices, spread_over(): other = lax.ppermute(x, 'grp', [(i, i ^ bit) for i in range(groups)])  3.48 us
    pallas_call x1, Pallas kernels, per_device(): pl.pallas_call(functools.partial(coarse_second_kernel, far_parts=half, **...  3.2 us
  transfers between devices with their start and end apart: 10, of which 6 were waited for; matrix products, arithmetic and copies ran while one was open for 0% of the time, Pallas kernels for 10%

profile of v5, /device:TPU:0, one launch (start us, length us, event | category | flops | bytes accessed | tf_op | source)
XLA Modules:
  0.0 99.4 jit_solution(6106704286539665297)
XLA Ops:
  0.6 1.8 %ghosts.1 = bf16[192,128]{1,0:T(8,128)(2,1)} custom-call(s32[8,24]{1,0:T(8,128)} %bitcast.34, bf16[768,128]{1,0:T(8,128)(2,1)} %bitcast.26), custom_call_target="tpu_custom_call" | custom-call | tf_op jit(solution)/shard_map/ghosts/pallas_call | solution.py:490
  2.4 7.3 %all-to-all-start = ((bf16[8,24,128]{2,1,0:T(8,128)(2,1)}), bf16[8,24,128]{2,1,0:T(8,128)(2,1)S(1)}, u32[]{:S(2)}, u32[]{:S(2)}) async-start(bf16[8,24,128]{2,1,0:T(8,128)(2,1)} %bitcast.3), calls=%async_computation | async-start | bytes 98304 | tf_op jit(solution)/shard_map/all_to_all | solution.py:447
  10.3 0.0 copy-start
  10.4 0.0 copy-start.1
  10.4 0.0 copy-start.2
  10.4 0.0 copy-start.3
  10.4 6.7 %fine_first.1 = (bf16[3,128,3072]{2,1,0:T(8,128)(2,1)S(1)}, f32[768,128]{1,0:T(8,128)S(1)}, s32[2,12]{1,0:T(2,128)}) custom-call(s32[1,1]{1,0:T(1,128)S(6)} %copy.16.count, s32[1,9216]{1,0:T(1,128)} %receivers.3, bf16[9216,128]{1,0:T(8,128)(2,1)} %bitcast.35, s32[1,9216]{1,0:T(1,128)} %senders.3, s32[1,9216]{1,0:T(1,128)} %receivers.3, ...), custom_call_target="tpu_custom_call" | custom-call | flops 2415919104 | tf_op jit(solution)/shard_map/fine_first/pallas_call | solution.py:502
  17.1 0.0 all-to-all-done
  17.1 0.0 copy-done
  17.1 0.0 copy-done.1
  17.1 0.0 copy-done.2
  17.1 0.0 copy-done.3
  17.1 0.0 copy-start.4
  17.1 6.6 %fine_second.1.refs_0_.refs_2_.refs_5_ = bf16[784,128]{1,0:T(8,128)(2,1)S(1)} custom-call(s32[1,1]{1,0:T(1,128)S(6)} %copy.16.count, s32[2,12]{1,0:T(2,128)} %get-tuple-element.14.marks, bf16[3,128,3072]{2,1,0:T(8,128)(2,1)S(1)} %get-tuple-element.15.pre, f32[768,128]{1,0:T(8,128)S(1)} %get-tuple-element.16.some, s32[1,9216]{1,0:T(1,128)} %senders.3, ...), custom_call_target="tpu_custom_call" | custom-call | tf_op jit(solution)/shard_map/fine_second/pallas_call | solution.py:523
  23.8 0.0 copy-start.5
  23.8 0.0 copy-start.6
  23.8 1.6 %collective-permute-start.1 = (bf16[784,128]{1,0:T(8,128)(2,1)S(1)}, bf16[784,128]{1,0:T(8,128)(2,1)S(1)}, u32[]{:S(2)}, u32[]{:S(2)}) collective-permute-start(bf16[784,128]{1,0:T(8,128)(2,1)S(1)} %fine_second.1.refs_0_.refs_2_.refs_5_), channel_id=1, source_target_pairs={{0,16},{8,24},{16,0},{24,8},{1,17},{9,25},{17,1},{25,9},{2,18},{10... | collective-permute-start | bytes 602120 | tf_op jit(solution)/shard_map/ppermute | solution.py:422
  25.4 0.0 collective-permute-start
  25.4 4.7 %collective-permute-done.1.refs_2_ = bf16[784,128]{1,0:T(8,128)(2,1)S(1)} collective-permute-done((bf16[784,128]{1,0:T(8,128)(2,1)S(1)}, bf16[784,128]{1,0:T(8,128)(2,1)S(1)}, u32[]{:S(2)}, u32[]{:S(2)}) %collective-permute-start.1) | collective-permute-done | bytes 200736 | tf_op jit(solution)/shard_map/ppermute | solution.py:422
  30.1 0.0 collective-permute-start.2
  30.1 0.0 collective-permute-done.refs_1_
  30.1 1.4 %collective-permute-done.2.refs_3_ = bf16[784,128]{1,0:T(8,128)(2,1)S(1)} collective-permute-done((bf16[784,128]{1,0:T(8,128)(2,1)S(1)}, bf16[784,128]{1,0:T(8,128)(2,1)S(1)}, u32[]{:S(2)}, u32[]{:S(2)}) %collective-permute-start.2) | collective-permute-done | bytes 200736 | tf_op jit(solution)/shard_map/ppermute | solution.py:422
  31.5 1.8 %pool.1 = bf16[1152,128]{1,0:T(8,128)(2,1)S(1)} custom-call(bf16[784,128]{1,0:T(8,128)(2,1)S(1)} %fine_second.1.refs_0_.refs_2_.refs_5_, bf16[784,128]{1,0:T(8,128)(2,1)S(1)} %collective-permute-done.refs_1_, bf16[784,128]{1,0:T(8,128)(2,1)S(1)} %collective-permute-done.1.refs_2_, bf16[784,128]{1,0:T(8,128)(2,1)S(1)} %collective-permute-done.2.refs_3_), custom_call_target="tpu_custom_call" | custom-call | tf_op jit(solution)/shard_map/pool/pallas_call | solution.py:538
  33.3 16.2 %all_to_all.44 = bf16[8,144,128]{2,1,0:T(8,128)(2,1)S(1)} all-to-all(bf16[8,144,128]{2,1,0:T(8,128)(2,1)S(1)} %bitcast.14), channel_id=1, replica_groups=mesh['grp'=4,'dom'=8] {'dom'}, dimensions={0} | all-to-all | bytes 589824 | tf_op jit(solution)/shard_map/all_to_all | solution.py:447
  49.5 0.0 copy-done.4
  49.5 0.1 coarse_mid.1
  49.6 11.5 %all_to_all.45 = bf16[8,128,128]{2,1,0:T(8,128)(2,1)S(1)} all-to-all(bf16[8,128,128]{2,1,0:T(8,128)(2,1)S(1)} %bitcast.25), channel_id=1, replica_groups=mesh['grp'=4,'dom'=8] {'dom'}, dimensions={0} | all-to-all | bytes 524288 | tf_op jit(solution)/shard_map/all_to_all | solution.py:447
  61.1 0.0 collective-permute-start.4
  61.1 1.7 %collective-permute-start.3 = (bf16[1024,128]{1,0:T(8,128)(2,1)S(1)}, bf16[1024,128]{1,0:T(8,128)(2,1)S(1)}, u32[]{:S(2)}, u32[]{:S(2)}) collective-permute-start(bf16[1024,128]{1,0:T(8,128)(2,1)S(1)} %bitcast.17), channel_id=1, source_target_pairs={{0,16},{8,24},{16,0},{24,8},{1,17},{9,25},{17,1},{25,9},{2,18},{10... | collective-permute-start | bytes 786440 | tf_op jit(solution)/shard_map/ppermute | solution.py:431
  62.9 0.0 collective-permute-done.4.refs_1_
  62.9 0.0 copy-done.5
  62.9 0.0 copy-done.6
  62.9 2.6 %coarse_first.1 = (bf16[4,128,1280]{2,1,0:T(8,128)(2,1)S(1)}, f32[128,128]{1,0:T(8,128)S(1)}) custom-call(bf16[1024,128]{1,0:T(8,128)(2,1)S(1)} %bitcast.18, bf16[1024,128]{1,0:T(8,128)(2,1)S(1)} %collective-permute-done.4.refs_1_, bf16[4096,128]{1,0:T(8,128)(2,1)} %refs_2_.1, s32[1,4096]{1,0:T(1,128)S(1)} %bitcast.30, s32[1,4096]{1,0:T(1,128)S(1)} %bitcast.32, ...), custom_call_target="tpu_custom_call" | custom-call | flops 2147483648 | tf_op jit(solution)/shard_map/coarse_first/pallas_call | solution.py:564
  65.5 0.0 copy-start.7
  65.5 4.3 %collective-permute-done.3.refs_1_ = bf16[1024,128]{1,0:T(8,128)(2,1)S(1)} collective-permute-done((bf16[1024,128]{1,0:T(8,128)(2,1)S(1)}, bf16[1024,128]{1,0:T(8,128)(2,1)S(1)}, u32[]{:S(2)}, u32[]{:S(2)}) %collective-permute-start.3) | collective-permute-done | bytes 262176 | tf_op jit(solution)/shard_map/ppermute | solution.py:431
  69.9 0.0 collective-permute-start.5
  69.9 1.5 %collective-permute-done.5.refs_2_ = bf16[1024,128]{1,0:T(8,128)(2,1)S(1)} collective-permute-done((bf16[1024,128]{1,0:T(8,128)(2,1)S(1)}, bf16[1024,128]{1,0:T(8,128)(2,1)S(1)}, u32[]{:S(2)}, u32[]{:S(2)}) %collective-permute-start.5) | collective-permute-done | bytes 262176 | tf_op jit(solution)/shard_map/ppermute | solution.py:422
  71.4 3.2 %coarse_second.1 = bf16[1024,128]{1,0:T(8,128)(2,1)S(1)} custom-call(bf16[1024,128]{1,0:T(8,128)(2,1)S(1)} %bitcast.19, bf16[1024,128]{1,0:T(8,128)(2,1)S(1)} %collective-permute-done.3.refs_1_, bf16[1024,128]{1,0:T(8,128)(2,1)S(1)} %collective-permute-done.5.refs_2_, bf16[4,128,1280]{2,1,0:T(8,128)(2,1)S(1)} %get-tuple-element.20.refs_3_, ...), custom_call_target="tpu_custom_call" | custom-call | tf_op jit(solution)/shard_map/coarse_second/pallas_call | solution.py:576
  74.6 12.6 %all_to_all.46 = bf16[8,128,128]{2,1,0:T(8,128)(2,1)S(1)} all-to-all(bf16[8,128,128]{2,1,0:T(8,128)(2,1)S(1)} %bitcast.24), channel_id=1, replica_groups=mesh['grp'=4,'dom'=8] {'dom'}, dimensions={0} | all-to-all | bytes 524288 | tf_op jit(solution)/shard_map/all_to_all | solution.py:447
  87.2 0.0 collective-permute-start.6
  87.2 1.7 %collective-permute-start.7 = (bf16[1024,128]{1,0:T(8,128)(2,1)S(1)}, bf16[1024,128]{1,0:T(8,128)(2,1)S(1)}, u32[]{:S(2)}, u32[]{:S(2)}) collective-permute-start(bf16[1024,128]{1,0:T(8,128)(2,1)S(1)} %bitcast.21), channel_id=1, source_target_pairs={{0,16},{8,24},{16,0},{24,8},{1,17},{9,25},{17,1},{25,9},{2,18},{10... | collective-permute-start | bytes 786440 | tf_op jit(solution)/shard_map/ppermute | solution.py:431
  88.9 0.0 collective-permute-done.6.refs_1_
  88.9 0.0 copy-done.7
  89.0 0.9 back_first.1.refs_4_
  89.9 6.1 %collective-permute-done.7.refs_2_ = bf16[1024,128]{1,0:T(8,128)(2,1)S(1)} collective-permute-done((bf16[1024,128]{1,0:T(8,128)(2,1)S(1)}, bf16[1024,128]{1,0:T(8,128)(2,1)S(1)}, u32[]{:S(2)}, u32[]{:S(2)}) %collective-permute-start.7) | collective-permute-done | bytes 262176 | tf_op jit(solution)/shard_map/ppermute | solution.py:431
  95.9 0.0 collective-permute-start.8
  95.9 1.5 %collective-permute-done.8.refs_3_ = bf16[1024,128]{1,0:T(8,128)(2,1)S(1)} collective-permute-done((bf16[1024,128]{1,0:T(8,128)(2,1)S(1)}, bf16[1024,128]{1,0:T(8,128)(2,1)S(1)}, u32[]{:S(2)}, u32[]{:S(2)}) %collective-permute-start.8) | collective-permute-done | bytes 262176 | tf_op jit(solution)/shard_map/ppermute | solution.py:422
  97.5 1.9 %back_second.1 = (bf16[768,128]{1,0:T(8,128)(2,1)}, bf16[512,128]{1,0:T(8,128)(2,1)}) custom-call(bf16[1024,128]{1,0:T(8,128)(2,1)S(1)} %bitcast.23, bf16[1024,128]{1,0:T(8,128)(2,1)S(1)} %collective-permute-done.6.refs_1_, bf16[1024,128]{1,0:T(8,128)(2,1)S(1)} %collective-permute-done.7.refs_2_, bf16[1024,128]{1,0:T(8,128)(2,1)S(1)} %collective-permute-done.8.refs_3_, ...), custom_call_target="tpu_custom_call" | custom-call | tf_op jit(solution)/shard_map/back_second/pallas_call | solution.py:601
Async XLA Ops:
  2.4 14.7 %all-to-all-start = ((bf16[8,24,128]{2,1,0:T(8,128)(2,1)}), bf16[8,24,128]{2,1,0:T(8,128)(2,1)S(1)}, u32[]{:S(2)}, u32[]{:S(2)}) async-start(bf16[8,24,128]{2,1,0:T(8,128)(2,1)} %bitcast.3), calls=%async_computation | async-start | bytes 98304 | tf_op jit(solution)/shard_map/all_to_all | solution.py:447
  10.3 6.7 %copy-start = (bf16[3,256,128]{2,1,0:T(8,128)(2,1)S(1)}, bf16[3,256,128]{2,1,0:T(8,128)(2,1)}, u32[]{:S(2)}) copy-start(bf16[3,256,128]{2,1,0:T(8,128)(2,1)} %refs_7_.3) | copy-start | bytes 589828
  10.4 6.7 %copy-start.1 = (bf16[5,128,128]{2,1,0:T(8,128)(2,1)S(1)}, bf16[5,128,128]{2,1,0:T(8,128)(2,1)}, u32[]{:S(2)}) copy-start(bf16[5,128,128]{2,1,0:T(8,128)(2,1)} %refs_8_.3) | copy-start | bytes 491524
  10.4 6.7 %copy-start.2 = (bf16[2,384,128]{2,1,0:T(8,128)(2,1)S(1)}, bf16[2,384,128]{2,1,0:T(8,128)(2,1)}, u32[]{:S(2)}) copy-start(bf16[2,384,128]{2,1,0:T(8,128)(2,1)} %refs_7_.2) | copy-start | bytes 589828
  10.4 6.7 %copy-start.3 = (bf16[1,768,128]{2,1,0:T(8,128)(2,1)S(1)}, bf16[1,768,128]{2,1,0:T(8,128)(2,1)}, u32[]{:S(2)}) copy-start(bf16[1,768,128]{2,1,0:T(8,128)(2,1)} %param.14) | copy-start | bytes 589828
  17.1 32.4 %copy-start.4 = (bf16[512,128]{1,0:T(8,128)(2,1)S(1)}, bf16[512,128]{1,0:T(8,128)(2,1)}, u32[]{:S(2)}) copy-start(bf16[512,128]{1,0:T(8,128)(2,1)} %nodes.1) | copy-start | bytes 393220
  23.8 39.1 %copy-start.5 = (s32[4096]{0:T(1024)S(1)}, s32[4096]{0:T(1024)}, u32[]{:S(2)}) copy-start(s32[4096]{0:T(1024)} %param.23) | copy-start | bytes 49156
  23.8 39.1 %copy-start.6 = (s32[4096]{0:T(1024)S(1)}, s32[4096]{0:T(1024)}, u32[]{:S(2)}) copy-start(s32[4096]{0:T(1024)} %param.24) | copy-start | bytes 49156
  23.8 6.3 %collective-permute-start.1 = (bf16[784,128]{1,0:T(8,128)(2,1)S(1)}, bf16[784,128]{1,0:T(8,128)(2,1)S(1)}, u32[]{:S(2)}, u32[]{:S(2)}) collective-permute-start(bf16[784,128]{1,0:T(8,128)(2,1)S(1)} %fine_second.1.refs_0_.refs_2_.refs_5_), channel_id=1, source_target_pairs={{0,16},{8,24},{16,0},{24,8},{1,17},{9,25},{17,1},{25,9},{2,18},{10... | collective-permute-start | bytes 602120 | tf_op jit(solution)/shard_map/ppermute | solution.py:422
  25.4 4.7 %collective-permute-start = (bf16[784,128]{1,0:T(8,128)(2,1)S(1)}, bf16[784,128]{1,0:T(8,128)(2,1)S(1)}, u32[]{:S(2)}, u32[]{:S(2)}) collective-permute-start(bf16[784,128]{1,0:T(8,128)(2,1)S(1)} %fine_second.1.refs_0_.refs_2_.refs_5_), channel_id=1, source_target_pairs={{0,8},{8,0},{16,24},{24,16},{1,9},{9,1},{17,25},{25,17},{2,10},{10... | collective-permute-start | bytes 602120 | tf_op jit(solution)/shard_map/ppermute | solution.py:422
  30.1 1.4 %collective-permute-start.2 = (bf16[784,128]{1,0:T(8,128)(2,1)S(1)}, bf16[784,128]{1,0:T(8,128)(2,1)S(1)}, u32[]{:S(2)}, u32[]{:S(2)}) collective-permute-start(bf16[784,128]{1,0:T(8,128)(2,1)S(1)} %collective-permute-done.1.refs_2_), channel_id=1, source_target_pairs={{0,8},{8,0},{16,24},{24,16},{1,9},{9,1},{17,25},{25,17},{2,10},{10... | collective-permute-start | bytes 602120 | tf_op jit(solution)/shard_map/ppermute | solution.py:422
  61.1 1.7 %collective-permute-start.4 = (bf16[1024,128]{1,0:T(8,128)(2,1)S(1)}, bf16[1024,128]{1,0:T(8,128)(2,1)S(1)}, u32[]{:S(2)}, u32[]{:S(2)}) collective-permute-start(bf16[1024,128]{1,0:T(8,128)(2,1)S(1)} %bitcast.16), channel_id=1, source_target_pairs={{0,8},{8,0},{16,24},{24,16},{1,9},{9,1},{17,25},{25,17},{2,10},{10... | collective-permute-start | bytes 786440 | tf_op jit(solution)/shard_map/ppermute | solution.py:422
  61.1 8.7 %collective-permute-start.3 = (bf16[1024,128]{1,0:T(8,128)(2,1)S(1)}, bf16[1024,128]{1,0:T(8,128)(2,1)S(1)}, u32[]{:S(2)}, u32[]{:S(2)}) collective-permute-start(bf16[1024,128]{1,0:T(8,128)(2,1)S(1)} %bitcast.17), channel_id=1, source_target_pairs={{0,16},{8,24},{16,0},{24,8},{1,17},{9,25},{17,1},{25,9},{2,18},{10... | collective-permute-start | bytes 786440 | tf_op jit(solution)/shard_map/ppermute | solution.py:431
  65.5 23.4 %copy-start.7 = (s32[1,768]{1,0:T(1,128)S(1)}, s32[1,768]{1,0:T(1,128)}, u32[]{:S(2)}) copy-start(s32[1,768]{1,0:T(1,128)} %refs_6_.1) | copy-start | bytes 9220
  69.9 1.5 %collective-permute-start.5 = (bf16[1024,128]{1,0:T(8,128)(2,1)S(1)}, bf16[1024,128]{1,0:T(8,128)(2,1)S(1)}, u32[]{:S(2)}, u32[]{:S(2)}) collective-permute-start(bf16[1024,128]{1,0:T(8,128)(2,1)S(1)} %collective-permute-done.3.refs_1_), channel_id=1, source_target_pairs={{0,8},{8,0},{16,24},{24,16},{1,9},{9,1},{17,25},{25,17},{2,10},{10... | collective-permute-start | bytes 786440 | tf_op jit(solution)/shard_map/ppermute | solution.py:422
  87.2 1.7 %collective-permute-start.6 = (bf16[1024,128]{1,0:T(8,128)(2,1)S(1)}, bf16[1024,128]{1,0:T(8,128)(2,1)S(1)}, u32[]{:S(2)}, u32[]{:S(2)}) collective-permute-start(bf16[1024,128]{1,0:T(8,128)(2,1)S(1)} %bitcast.20), channel_id=1, source_target_pairs={{0,8},{8,0},{16,24},{24,16},{1,9},{9,1},{17,25},{25,17},{2,10},{10... | collective-permute-start | bytes 786440 | tf_op jit(solution)/shard_map/ppermute | solution.py:422
  87.2 8.7 %collective-permute-start.7 = (bf16[1024,128]{1,0:T(8,128)(2,1)S(1)}, bf16[1024,128]{1,0:T(8,128)(2,1)S(1)}, u32[]{:S(2)}, u32[]{:S(2)}) collective-permute-start(bf16[1024,128]{1,0:T(8,128)(2,1)S(1)} %bitcast.21), channel_id=1, source_target_pairs={{0,16},{8,24},{16,0},{24,8},{1,17},{9,25},{17,1},{25,9},{2,18},{10... | collective-permute-start | bytes 786440 | tf_op jit(solution)/shard_map/ppermute | solution.py:431
  95.9 1.5 %collective-permute-start.8 = (bf16[1024,128]{1,0:T(8,128)(2,1)S(1)}, bf16[1024,128]{1,0:T(8,128)(2,1)S(1)}, u32[]{:S(2)}, u32[]{:S(2)}) collective-permute-start(bf16[1024,128]{1,0:T(8,128)(2,1)S(1)} %collective-permute-done.7.refs_2_), channel_id=1, source_target_pairs={{0,8},{8,0},{16,24},{24,16},{1,9},{9,1},{17,25},{25,17},{2,10},{10... | collective-permute-start | bytes 786440 | tf_op jit(solution)/shard_map/ppermute | solution.py:422
